TPU v7x, 256 devices: a whole 4x4x8 slice. The times are simulated.
256 devices in a mesh: gx: 8 (over z), gy: 4 (over y), gz: 8 (over x, core).
Axes of the slice: x: 4, y: 4, z: 8, core: 2. Of those that a mesh axis runs over, the one named last changes fastest.
Arguments:
- right_side: float32 [4, 192, 96, 192], P(None, 'gx', 'gy', 'gz'), may hold values from -6 to 6
- iterate: float32 [4, 192, 96, 192], P(None, 'gx', 'gy', 'gz'), may hold values from -6 to 6
- coefficient: float32 [192, 96, 192], P('gx', 'gy', 'gz'), may hold values from 0.1 to 2
- ordering: int32 [8, 4, 8, 216], P('gx', 'gy', 'gz'), may hold values from 0 to 215, as said below
- leaf_inverse: float32 [8, 4, 8, 125, 125], P('gx', 'gy', 'gz'), may hold values from -2 to 3
- leaf_first: float32 [8, 4, 8, 125, 50], P('gx', 'gy', 'gz'), may hold values from -0.5 to 0.5
- leaf_second: float32 [8, 4, 8, 125, 60], P('gx', 'gy', 'gz'), may hold values from -0.5 to 0.5
- leaf_top: float32 [8, 4, 8, 125, 72], P('gx', 'gy', 'gz'), may hold values from -0.5 to 0.5
- first_inverse: float32 [8, 4, 200, 200], P('gx', 'gy', 'gz'), may hold values from -2 to 3
- first_second: float32 [8, 4, 8, 25, 60], P('gx', 'gy', 'gz'), may hold values from -1.25 to 1.25
- first_top: float32 [8, 4, 8, 25, 72], P('gx', 'gy', 'gz'), may hold values from -1.25 to 1.25
- second_inverse: float32 [8, 960, 960], P('gx', ('gy', 'gz')), may hold values from -2 to 3
- second_top: float32 [8, 4, 8, 30, 72], P('gx', 'gy', 'gz'), may hold values from -1 to 1
- top_inverse: float32 [9216, 9216], P(('gx', 'gy', 'gz')), may hold values from -2 to 3
Outputs:
- correction: float32 [4, 192, 96, 192], P(None, 'gx', 'gy', 'gz')
Inputs may be any that keep to these rules, and one draw needn't show every extreme that they name: `ordering`: each device's row names each of its 216 coarse cells once (cell x 6^2 + y * 6 + z): first the 125 cells with x, y and z all below 5, then the 25 cells with z = 5 and x, y below it, then the 30 cells with y = 5 and x below it, then the 36 cells with x = 5, each group in any order.
All inputs are finite; a program needn't handle non-finite values.
Results may differ from a plain program's by a relative error of at most 0.0003.
Values sent between devices are 32-bit elements; how exact they have to be, the bound alone decides.
No kernel may reach another device: no remote copies, remote signals or barrier semaphores. Data moves between devices by JAX's collectives and lax.ppermute only.
A program may use at most 64 MiB of HBM per device.

v0:
```python
import jax
import jax.numpy as jnp
from jax import lax
from jax.sharding import Mesh
from jax.sharding import PartitionSpec as P

GZ = ("gz_0", "gz_1")
GX_GY_GZ = ("gx", "gy", "gz_0", "gz_1")
GY_GZ = ("gy", "gz_0", "gz_1")


precise = lax.Precision.HIGHEST


def shifted(shard, axis, by):
    peers = lax.axis_size(axis)
    pairs = [(i, i + by) for i in range(peers) if 0 <= i + by < peers]
    return lax.ppermute(shard, axis, pairs)


def padded_2(shard, sides, width):
    edges = {}
    for axis, dim in sides:
        peers, length = (lax.axis_size(axis), shard.shape[dim])
        up = [(i, (i + 1) % peers) for i in range(peers - 1)]
        last = lax.slice_in_dim(shard, length - width, length, axis=dim)
        leading = lax.slice_in_dim(shard, 0, width, axis=dim)
        edges[dim] = (
            lax.ppermute(last, axis, up),
            lax.ppermute(leading, axis, [(b, a) for a, b in up]),
        )
    done = []
    for _, dim in sides:
        low, high = edges[dim]
        around = [(width, width) if d in done else (0, 0) for d in range(shard.ndim)]
        shard = jnp.concatenate([jnp.pad(low, around), shard, jnp.pad(high, around)], axis=dim)
        done.append(dim)
    return shard


def cut_along(shard, dim, peers):
    before, after = (shard.shape[:dim], shard.shape[dim + 1 :])
    return jnp.moveaxis(shard.reshape(*before, peers, -1, *after), dim, 0)


def summed_on_arrival(shard, axis, dim):
    peers = lax.axis_size(axis)
    pieces = lax.all_to_all(cut_along(shard, dim, peers), axis, 0, 0, tiled=True)
    return jnp.sum(pieces, axis=0)


def sum_by_axis(shard, axes, dim):
    far, near = axes
    own = summed_on_arrival(cut_along(shard, dim, lax.axis_size(far)), near, dim + 1)
    return jnp.sum(lax.all_to_all(own, far, 0, 0, tiled=True), axis=0)


def sent_to_all(shard, axis):
    copies = jnp.broadcast_to(shard, (lax.axis_size(axis), *shard.shape))
    return lax.all_to_all(copies, axis, split_axis=0, concat_axis=0, tiled=True)


def laid_out(pieces, dim):
    pieces = jnp.moveaxis(pieces, 0, dim)
    shape = pieces.shape
    return pieces.reshape(*shape[:dim], shape[dim] * shape[dim + 1], *shape[dim + 2 :])


def gathered_by_axis(shard, axes, dim):
    far, near = axes
    pieces = sent_to_all(sent_to_all(shard, far), near)
    return laid_out(pieces.swapaxes(0, 1).reshape(-1, *shard.shape), dim)


def gather_directly(shard, axis, dim):
    pieces = sent_to_all(shard, axis)
    return laid_out(pieces, dim)


def product(operand, matrix):
    return jnp.dot(operand, matrix, precision=precise, preferred_element_type=jnp.float32)


def product_back(operand, matrix):
    return lax.dot_general(
        operand,
        matrix,
        (((1,), (1,)), ((), ())),
        precision=precise,
        preferred_element_type=jnp.float32,
    )


def weigh(extended, dimension):
    length = extended.shape[dimension] - 1
    previous = lax.slice_in_dim(extended, 0, length, 2, dimension)
    centre = lax.slice_in_dim(extended, 1, length + 1, 2, dimension)
    following = lax.slice_in_dim(extended, 2, length + 1, 2, dimension)
    return 0.25 * previous + 0.5 * centre + 0.25 * following


def spread(extended, dimension):
    length = extended.shape[dimension] - 1
    current = lax.slice_in_dim(extended, 0, length, 1, dimension)
    following = lax.slice_in_dim(extended, 1, length + 1, 1, dimension)
    paired = jnp.stack([current, 0.5 * (current + following)], axis=dimension + 1)
    new_shape = list(current.shape)
    new_shape[dimension] = 2 * length
    return paired.reshape(new_shape)


def lower_rims(values):
    boundary = shifted(values[:, -1:], "gx", 1)
    values = jnp.concatenate([boundary, values], axis=1)
    boundary = shifted(values[:, :, -1:], "gy", 1)
    values = jnp.concatenate([boundary, values], axis=2)
    boundary = shifted(values[:, :, :, -1:], GZ, 1)
    return jnp.concatenate([boundary, values], axis=3)


def upper_rims(values):
    boundary = shifted(values[:, :1], "gx", -1)
    values = jnp.concatenate([values, boundary], axis=1)
    boundary = shifted(values[:, :, :1], "gy", -1)
    values = jnp.concatenate([values, boundary], axis=2)
    boundary = shifted(values[:, :, :, :1], GZ, -1)
    return jnp.concatenate([values, boundary], axis=3)


def restrict(values):
    extended = lower_rims(values)
    for dimension in (1, 2, 3):
        extended = weigh(extended, dimension)
    return extended


def prolong(values):
    extended = upper_rims(values)
    for dimension in (1, 2, 3):
        extended = spread(extended, dimension)
    return extended


def residual_of(right_side, iterate, coefficient):
    padded = padded_2(iterate, (("gx", 1), ("gy", 2), (GZ, 3)), 1)
    beside = padded[:, 2:, 1:-1, 1:-1] + padded[:, :-2, 1:-1, 1:-1]
    beside = beside + padded[:, 1:-1, 2:, 1:-1] + padded[:, 1:-1, :-2, 1:-1]
    beside = beside + padded[:, 1:-1, 1:-1, 2:] + padded[:, 1:-1, 1:-1, :-2]
    return right_side - ((6.0 + coefficient) * iterate - beside)


def per_device(
    right_side,
    iterate,
    coefficient,
    ordering,
    leaf_inverse,
    leaf_first,
    leaf_second,
    leaf_top,
    first_inverse,
    first_second,
    first_top,
    second_inverse,
    second_top,
    top_inverse,
):
    rhs_count = right_side.shape[0]
    leaf_size = leaf_inverse.shape[-1]
    first_size = first_second.shape[3]
    second_size = second_top.shape[3]
    top_size = top_inverse.shape[0]
    first_rows = first_inverse[0, 0]
    second_rows = second_inverse[0]
    coarse = restrict(restrict(residual_of(right_side, iterate, coefficient)))
    coarse_side = coarse.shape[1]
    flattened = coarse.reshape(rhs_count, coarse_side**3)
    order_row = ordering.reshape(-1)
    chosen = jnp.take(flattened, order_row, axis=1)
    first_end = leaf_size + first_size
    second_end = first_end + second_size
    leaf_rhs = chosen[:, :leaf_size]
    first_rhs = chosen[:, leaf_size:first_end]
    second_rhs = chosen[:, first_end:second_end]
    top_rhs = chosen[:, second_end:]
    leaf_block = leaf_inverse[0, 0, 0]
    to_first = leaf_first[0, 0, 0]
    to_second = leaf_second[0, 0, 0]
    to_top = leaf_top[0, 0, 0]
    first_to_second = first_second[0, 0, 0]
    first_to_top = first_top[0, 0, 0]
    second_to_top = second_top[0, 0, 0]
    leaf_solved = product(leaf_rhs, leaf_block)
    toward = product(leaf_solved, to_first)
    arrived = shifted(toward[:, first_size:], GZ, -1)
    first_target = first_rhs - toward[:, :first_size] - arrived
    first_own = summed_on_arrival(product(first_target, first_rows), GZ, 1)
    toward = product(leaf_solved, to_second) + product(first_own, first_to_second)
    arrived = shifted(toward[:, second_size:], "gy", -1)
    second_target = second_rhs - toward[:, :second_size] - arrived
    second_own = summed_on_arrival(product(second_target, second_rows), GY_GZ, 1)
    toward = (
        product(leaf_solved, to_top)
        + product(first_own, first_to_top)
        + product(second_own, second_to_top)
    )
    arrived = shifted(toward[:, top_size:], "gx", -1)
    top_target = top_rhs - toward[:, :top_size] - arrived
    top_own = sum_by_axis(product(top_target, top_inverse), (("gx", "gy"), ("gz_0", "gz_1")), 1)
    top_whole = gathered_by_axis(top_own, (("gx", "gy"), ("gz_0", "gz_1")), 1)
    top_back = product_back(top_whole, top_inverse)
    top_lower = shifted(top_back, "gx", 1)
    top_pair = jnp.concatenate([top_back, top_lower], axis=1)
    second_gap = second_own - product_back(top_pair, second_to_top)
    second_whole = gather_directly(second_gap, GY_GZ, 1)
    second_back = product_back(second_whole, second_rows)
    second_lower = shifted(second_back, "gy", 1)
    second_pair = jnp.concatenate([second_back, second_lower], axis=1)
    first_gap = (
        first_own
        - product_back(second_pair, first_to_second)
        - product_back(top_pair, first_to_top)
    )
    first_whole = gather_directly(first_gap, GZ, 1)
    first_back = product_back(first_whole, first_rows)
    first_lower = shifted(first_back, GZ, 1)
    first_pair = jnp.concatenate([first_back, first_lower], axis=1)
    leaf_gap = (
        leaf_solved - product_back(first_pair, to_first) - product_back(second_pair, to_second)
    )
    leaf_gap = leaf_gap - product_back(top_pair, to_top)
    leaf_back = product_back(leaf_gap, leaf_block)
    ordered = jnp.concatenate([leaf_back, first_back, second_back, top_back], axis=1)
    coarse_cells = jnp.zeros_like(ordered).at[:, order_row].set(ordered)
    coarse_grid = coarse_cells.reshape(rhs_count, coarse_side, coarse_side, coarse_side)
    return prolong(prolong(coarse_grid))


def solution(mesh):
    finer = Mesh(
        mesh.devices.reshape(mesh.shape["gx"], mesh.shape["gy"], 4, 2), ("gx", "gy", "gz_0", "gz_1")
    )
    return jax.shard_map(
        per_device,
        mesh=finer,
        in_specs=(
            P(None, "gx", "gy", GZ),
            P(None, "gx", "gy", GZ),
            P("gx", "gy", GZ),
            P("gx", "gy", GZ, None),
            P("gx", "gy", GZ, None, None),
            P("gx", "gy", GZ, None, None),
            P("gx", "gy", GZ, None, None),
            P("gx", "gy", GZ, None, None),
            P("gx", "gy", GZ, None),
            P("gx", "gy", GZ, None, None),
            P("gx", "gy", GZ, None, None),
            P("gx", GY_GZ, None),
            P("gx", "gy", GZ, None, None),
            P(GX_GY_GZ, None),
        ),
        out_specs=P(None, "gx", "gy", GZ),
        check_vma=False,
    )
```

profile of v0, /device:TPU:1, one launch (start us, length us, event | category | flops | bytes accessed | tf_op | source)
XLA Modules:
  0.0 278.1 jit_solution(7628728062553296326)
XLA Ops:
  0.0 1.6 fusion.84
  1.6 4.3 %collective-permute-start.1 = (f32[4,1,24,24]{3,2,1,0:T(8,128)}, f32[4,1,24,24]{3,2,1,0:T(8,128)S(1)}, u32[]{:S(2)}, u32[]{:S(2)}) collective-permute-start(f32[4,1,24,24]{3,2,1,0:T(8,128)} %get-tuple-element.10), channel_id=1, source_target_pairs={{0,32},{32,64},{64,96},{96,128},{128,160},{160,192},{192,224},{1,3... | collective-permute-start | bytes 27656 | tf_op jit(solution)/shard_map/ppermute | solution.py:29
  5.9 1.3 collective-permute-start
  7.2 3.5 %fusion.82 = (f32[4,24,24,1]{3,2,1,0:T(8,128)}, f32[4,24,24,1]{3,2,1,0:T(8,128)}) fusion(f32[4,24,24,24]{3,2,1,0:T(8,128)} %param.15), kind=kLoop, calls=%fused_computation.161 | loop fusion | bytes 36864 | tf_op jit(solution)/shard_map/slice | solution.py:27
  10.7 2.0 copy.258
  12.7 2.9 %collective-permute-start.4 = (f32[4,24,24,1]{2,1,3,0:T(8,128)S(1)}, f32[4,24,24,1]{2,1,3,0:T(8,128)S(1)}, u32[]{:S(2)}, u32[]{:S(2)}) collective-permute-start(f32[4,24,24,1]{2,1,3,0:T(8,128)S(1)} %copy.258), channel_id=1, source_target_pairs={{1,0},{2,1},{3,2},{4,3},{5,4},{6,5},{7,6},{9,8},{10,9},{11,10},{12... | collective-permute-start | bytes 27656 | tf_op jit(solution)/shard_map/ppermute | solution.py:30
  15.6 1.9 copy.259
  17.5 3.0 %collective-permute-start.5 = (f32[4,24,24,1]{2,1,3,0:T(8,128)S(1)}, f32[4,24,24,1]{2,1,3,0:T(8,128)S(1)}, u32[]{:S(2)}, u32[]{:S(2)}) collective-permute-start(f32[4,24,24,1]{2,1,3,0:T(8,128)S(1)} %copy.259), channel_id=1, source_target_pairs={{0,1},{1,2},{2,3},{3,4},{4,5},{5,6},{6,7},{8,9},{9,10},{10,11},{11... | collective-permute-start | bytes 27656 | tf_op jit(solution)/shard_map/ppermute | solution.py:29
  20.6 1.3 collective-permute-start.2
  21.9 4.0 %collective-permute-start.3 = (f32[4,24,1,24]{3,1,2,0:T(8,128)S(1)}, f32[4,24,1,24]{3,1,2,0:T(8,128)S(1)}, u32[]{:S(2)}, u32[]{:S(2)}) collective-permute-start(f32[4,24,1,24]{3,1,2,0:T(8,128)S(1)} %bitcast.159), channel_id=1, source_target_pairs={{0,8},{8,16},{16,24},{1,9},{9,17},{17,25},{2,10},{10,18},{18,26},{... | collective-permute-start | bytes 27656 | tf_op jit(solution)/shard_map/ppermute | solution.py:29
  27.8 1.7 copy.262
  29.5 1.6 copy.263
  31.7 5.2 %fusion.3 = f32[4,24,24,24]{3,2,1,0:T(8,128)S(1)} fusion(f32[4,24,24,24]{3,2,1,0:T(8,128)} %param.14, f32[4,24,24,1]{3,2,1,0:T(8,128)} %copy.263, f32[4,26,1,24]{3,2,1,0:T(1,128)S(1)} %pad.14.clone, f32[4,26,24,24]{3,2,1,0:T(8,128)} %constant_dynamic-update-slice_fusion, f32[4,26,1,24]{3,2,1,0:T(1,128)S(1)} %pad.15.clone, f32[4,24,24,1]{3,2,1,0:T(8,128)} %copy.262, ...), kind=kLoop, calls=%fused_computation.9 | loop fusion | flops 1327104 | bytes 1015296 | tf_op jit(solution)/shard_map/sub | solution.py:149
  37.0 4.3 %collective-permute-start.6 = (f32[4,1,24,24]{3,2,1,0:T(8,128)S(1)}, f32[4,1,24,24]{3,2,1,0:T(8,128)S(1)}, u32[]{:S(2)}, u32[]{:S(2)}) collective-permute-start(f32[4,1,24,24]{3,2,1,0:T(8,128)S(1)} %slice.264), channel_id=1, source_target_pairs={{0,32},{32,64},{64,96},{96,128},{128,160},{160,192},{192,224},{1,3... | collective-permute-start | bytes 27656 | tf_op jit(solution)/shard_map/ppermute | solution.py:18
  41.3 1.2 collective-permute-done.6
  42.6 3.7 %collective-permute-start.7 = (f32[4,25,1,24]{1,3,2,0:T(8,128)S(1)}, f32[4,25,1,24]{1,3,2,0:T(8,128)S(1)}, u32[]{:S(2)}, u32[]{:S(2)}) collective-permute-start(f32[4,25,1,24]{1,3,2,0:T(8,128)S(1)} %copy.207), channel_id=1, source_target_pairs={{0,8},{8,16},{16,24},{1,9},{9,17},{17,25},{2,10},{10,18},{18,26},{... | collective-permute-start | bytes 28808 | tf_op jit(solution)/shard_map/ppermute | solution.py:18
  46.3 1.2 collective-permute-done.7
  47.5 1.9 pad_maximum_fusion
  50.3 5.4 %collective-permute-start.8 = (f32[4,25,25,1]{2,1,3,0:T(8,128)S(1)}, f32[4,25,25,1]{2,1,3,0:T(8,128)S(1)}, u32[]{:S(2)}, u32[]{:S(2)}) collective-permute-start(f32[4,25,25,1]{2,1,3,0:T(8,128)S(1)} %copy.209), channel_id=1, source_target_pairs={{0,1},{1,2},{2,3},{3,4},{4,5},{5,6},{6,7},{8,9},{9,10},{10,11},{11... | collective-permute-start | bytes 30008 | tf_op jit(solution)/shard_map/ppermute | solution.py:18
  55.6 1.3 collective-permute-done.8
  57.0 2.0 copy.210
  58.9 2.0 maximum_maximum_fusion
  61.9 1.2 slice.219
  63.1 1.3 slice.220
  64.4 1.3 slice.221
  65.8 4.0 %collective-permute-start.9 = (f32[4,1,12,12]{3,2,1,0:T(8,128)S(1)}, f32[4,1,12,12]{3,2,1,0:T(8,128)S(1)}, u32[]{:S(2)}, u32[]{:S(2)}) collective-permute-start(f32[4,1,12,12]{3,2,1,0:T(8,128)S(1)} %slice.265), channel_id=1, source_target_pairs={{0,32},{32,64},{64,96},{96,128},{128,160},{160,192},{192,224},{1,3... | collective-permute-start | bytes 6920 | tf_op jit(solution)/shard_map/ppermute | solution.py:18
  70.9 4.0 %collective-permute-start.10 = (f32[4,13,1,12]{3,2,1,0:T(1,128)S(1)}, f32[4,13,1,12]{3,2,1,0:T(1,128)S(1)}, u32[]{:S(2)}, u32[]{:S(2)}) collective-permute-start(f32[4,13,1,12]{3,2,1,0:T(1,128)S(1)} %pad_maximum_fusion.25), channel_id=1, source_target_pairs={{0,8},{8,16},{16,24},{1,9},{9,17},{17,25},{2,10},{10,18},{18,26},{... | collective-permute-start | bytes 7496 | tf_op jit(solution)/shard_map/ppermute | solution.py:18
  76.0 6.0 %collective-permute-start.11 = (f32[4,13,13,1]{3,2,1,0:T(8,128)S(1)}, f32[4,13,13,1]{3,2,1,0:T(8,128)S(1)}, u32[]{:S(2)}, u32[]{:S(2)}) collective-permute-start(f32[4,13,13,1]{3,2,1,0:T(8,128)S(1)} %pad_maximum_fusion.13), channel_id=1, source_target_pairs={{0,1},{1,2},{2,3},{3,4},{4,5},{5,6},{6,7},{8,9},{9,10},{10,11},{11... | collective-permute-start | bytes 8120 | tf_op jit(solution)/shard_map/ppermute | solution.py:18
  82.0 5.0 %collective-permute-done.11 = f32[4,13,13,1]{3,2,1,0:T(8,128)S(1)} collective-permute-done((f32[4,13,13,1]{3,2,1,0:T(8,128)S(1)}, f32[4,13,13,1]{3,2,1,0:T(8,128)S(1)}, u32[]{:S(2)}, u32[]{:S(2)}) %collective-permute-start.11) | collective-permute-done | bytes 2736 | tf_op jit(solution)/shard_map/ppermute | solution.py:18
  90.8 1.9 collective-permute-start.12
  94.1 2.3 collective-permute-done.12
  97.3 3.7 %all-to-all-start = ((f32[8,4,25]{2,1,0:T(4,128)}), f32[8,4,25]{2,1,0:T(4,128)S(1)}, u32[]{:S(2)}, u32[]{:S(2)}) async-start(f32[8,4,25]{2,1,0:T(4,128)} %convolution_bitcast_fusion.1), calls=%async_computation | async-start | bytes 32768 | tf_op jit(solution)/shard_map/all_to_all | solution.py:48
  101.2 4.5 %all-to-all-done = f32[8,4,25]{2,1,0:T(4,128)S(1)} async-done(((f32[8,4,25]{2,1,0:T(4,128)}), f32[8,4,25]{2,1,0:T(4,128)S(1)}, u32[]{:S(2)}, u32[]{:S(2)}) %all-to-all-start) | async-done | bytes 3232 | tf_op jit(solution)/shard_map/all_to_all | solution.py:48
  105.9 1.3 collective-permute-start.13
  107.4 3.4 %collective-permute-done.13 = f32[4,30]{1,0:T(4,128)S(1)} collective-permute-done((f32[4,30]{1,0:T(4,128)S(1)}, f32[4,30]{1,0:T(4,128)S(1)}, u32[]{:S(2)}, u32[]{:S(2)}) %collective-permute-start.13) | collective-permute-done | bytes 512 | tf_op jit(solution)/shard_map/ppermute | solution.py:18
  110.8 2.0 convolution_bitcast_fusion
  113.6 7.2 %all-to-all-start.1 = ((f32[32,4,30]{2,1,0:T(4,128)}), f32[32,4,30]{2,1,0:T(4,128)S(1)}, u32[]{:S(2)}, u32[]{:S(2)}) async-start(f32[32,4,30]{2,1,0:T(4,128)} %copy.215), calls=%async_computation.1 | async-start | bytes 131072 | tf_op jit(solution)/shard_map/all_to_all | solution.py:48
  121.0 7.2 %all-to-all-done.1 = f32[32,4,30]{2,1,0:T(4,128)S(1)} async-done(((f32[32,4,30]{2,1,0:T(4,128)}), f32[32,4,30]{2,1,0:T(4,128)S(1)}, u32[]{:S(2)}, u32[]{:S(2)}) %all-to-all-start.1) | async-done | bytes 15392 | tf_op jit(solution)/shard_map/all_to_all | solution.py:48
  128.4 1.5 collective-permute-start.14
  129.9 3.7 %collective-permute-done.14 = f32[4,36]{1,0:T(4,128)S(1)} collective-permute-done((f32[4,36]{1,0:T(4,128)S(1)}, f32[4,36]{1,0:T(4,128)S(1)}, u32[]{:S(2)}, u32[]{:S(2)}) %collective-permute-start.14) | collective-permute-done | bytes 608 | tf_op jit(solution)/shard_map/ppermute | solution.py:18
  135.6 9.0 %all_to_all.40 = f32[8,1,4608]{2,1,0:T(1,128)S(1)} all-to-all(f32[8,1,4608]{2,1,0:T(1,128)S(1)} %reshape.122), channel_id=1, replica_groups=mesh['gx'=8,'gy'=4,'gz_0'=4,'gz_1'=2] {'gz_0','gz_1'}, dimensions={0} | all-to-all | bytes 294912 | tf_op jit(solution)/shard_map/all_to_all | solution.py:48
  147.0 21.2 %all_to_all.41 = f32[32,1,144]{2,1,0:T(1,128)S(1)} all-to-all(f32[32,1,144]{2,1,0:T(1,128)S(1)} %reshape.124), channel_id=1, replica_groups=mesh['gx'=8,'gy'=4,'gz_0'=4,'gz_1'=2] {'gx','gy'}, dimensions={0} | all-to-all | bytes 36864 | tf_op jit(solution)/shard_map/all_to_all | solution.py:55
  169.2 11.6 %all_to_all.42 = f32[32,1,144]{2,1,0:T(1,128)S(1)} all-to-all(f32[32,1,144]{2,1,0:T(1,128)S(1)} %reshape.126), channel_id=1, replica_groups=mesh['gx'=8,'gy'=4,'gz_0'=4,'gz_1'=2] {'gx','gy'}, dimensions={0} | all-to-all | bytes 36864 | tf_op jit(solution)/shard_map/all_to_all | solution.py:60
  182.3 11.2 %all_to_all.43 = f32[8,1,4608]{2,1,0:T(1,128)S(1)} all-to-all(f32[8,1,4608]{2,1,0:T(1,128)S(1)} %reshape.128), channel_id=1, replica_groups=mesh['gx'=8,'gy'=4,'gz_0'=4,'gz_1'=2] {'gz_0','gz_1'}, dimensions={0} | all-to-all | bytes 294912 | tf_op jit(solution)/shard_map/all_to_all | solution.py:60
  195.9 1.2 fusion.85
  197.2 2.3 collective-permute-start.15
  200.4 12.1 %all_to_all.44 = f32[32,4,30]{2,1,0:T(4,128)S(1)} all-to-all(f32[32,4,30]{2,1,0:T(4,128)S(1)} %broadcast_in_dim.32), channel_id=1, replica_groups=mesh['gx'=8,'gy'=4,'gz_0'=4,'gz_1'=2] {'gy','gz_0','gz_1'}, dimensions={0} | all-to-all | bytes 30720 | tf_op jit(solution)/shard_map/all_to_all | solution.py:60
  212.9 2.3 collective-permute-start.16
  216.1 8.3 %all_to_all.45 = f32[8,4,25]{2,1,0:T(4,128)S(1)} all-to-all(f32[8,4,25]{2,1,0:T(4,128)S(1)} %broadcast_in_dim.33), channel_id=1, replica_groups=mesh['gx'=8,'gy'=4,'gz_0'=4,'gz_1'=2] {'gz_0','gz_1'}, dimensions={0} | all-to-all | bytes 6400 | tf_op jit(solution)/shard_map/all_to_all | solution.py:60
  224.5 2.8 %collective-permute-start.17 = (f32[4,25]{1,0:T(4,128)S(1)}, f32[4,25]{1,0:T(4,128)S(1)}, u32[]{:S(2)}, u32[]{:S(2)}) collective-permute-start(f32[4,25]{1,0:T(4,128)S(1)} %fusion.39), channel_id=1, source_target_pairs={{0,1},{1,2},{2,3},{3,4},{4,5},{5,6},{6,7},{8,9},{9,10},{10,11},{11... | collective-permute-start | bytes 1208 | tf_op jit(solution)/shard_map/ppermute | solution.py:18
  230.2 1.3 collective-permute-start.18
  231.5 4.0 %collective-permute-done.18 = f32[4,1,6,6]{3,2,1,0:T(8,128)S(1)} collective-permute-done((f32[4,1,6,6]{3,2,1,0:T(8,128)S(1)}, f32[4,1,6,6]{3,2,1,0:T(8,128)S(1)}, u32[]{:S(2)}, u32[]{:S(2)}) %collective-permute-start.18) | collective-permute-done | bytes 608 | tf_op jit(solution)/shard_map/ppermute | solution.py:18
  235.5 1.3 collective-permute-start.19
  236.8 3.7 %collective-permute-done.19 = f32[4,7,1,6]{3,2,1,0:T(1,128)S(1)} collective-permute-done((f32[4,7,1,6]{3,2,1,0:T(1,128)S(1)}, f32[4,7,1,6]{3,2,1,0:T(1,128)S(1)}, u32[]{:S(2)}, u32[]{:S(2)}) %collective-permute-start.19) | collective-permute-done | bytes 704 | tf_op jit(solution)/shard_map/ppermute | solution.py:18
  240.6 3.2 %collective-permute-start.20 = (f32[4,7,7,1]{3,2,1,0:T(8,128)S(1)}, f32[4,7,7,1]{3,2,1,0:T(8,128)S(1)}, u32[]{:S(2)}, u32[]{:S(2)}) collective-permute-start(f32[4,7,7,1]{3,2,1,0:T(8,128)S(1)} %pad_maximum_fusion.20), channel_id=1, source_target_pairs={{1,0},{2,1},{3,2},{4,3},{5,4},{6,5},{7,6},{9,8},{10,9},{11,10},{12... | collective-permute-start | bytes 2360 | tf_op jit(solution)/shard_map/ppermute | solution.py:18
  243.7 5.0 %collective-permute-done.20 = f32[4,7,7,1]{3,2,1,0:T(8,128)S(1)} collective-permute-done((f32[4,7,7,1]{3,2,1,0:T(8,128)S(1)}, f32[4,7,7,1]{3,2,1,0:T(8,128)S(1)}, u32[]{:S(2)}, u32[]{:S(2)}) %collective-permute-start.20) | collective-permute-done | bytes 816 | tf_op jit(solution)/shard_map/ppermute | solution.py:18
  250.1 1.3 collective-permute-start.21
  251.4 3.6 %collective-permute-done.21 = f32[4,1,12,12]{2,0,3,1:T(4,128)S(1)} collective-permute-done((f32[4,1,12,12]{2,0,3,1:T(4,128)S(1)}, f32[4,1,12,12]{2,0,3,1:T(4,128)S(1)}, u32[]{:S(2)}, u32[]{:S(2)}) %collective-permute-start.21) | collective-permute-done | bytes 2336 | tf_op jit(solution)/shard_map/ppermute | solution.py:18
  255.0 1.3 collective-permute-start.22
  256.3 7.5 %collective-permute-done.22 = f32[4,13,1,12]{2,0,3,1:T(4,128)S(1)} collective-permute-done((f32[4,13,1,12]{2,0,3,1:T(4,128)S(1)}, f32[4,13,1,12]{2,0,3,1:T(4,128)S(1)}, u32[]{:S(2)}, u32[]{:S(2)}) %collective-permute-start.22) | collective-permute-done | bytes 2528 | tf_op jit(solution)/shard_map/ppermute | solution.py:18
  263.9 1.9 collective-permute-start.23
  265.9 5.4 %collective-permute-done.23 = f32[4,13,13,1]{2,0,3,1:T(4,128)S(1)} collective-permute-done((f32[4,13,13,1]{2,0,3,1:T(4,128)S(1)}, f32[4,13,13,1]{2,0,3,1:T(4,128)S(1)}, u32[]{:S(2)}, u32[]{:S(2)}) %collective-permute-start.23) | collective-permute-done | bytes 2736 | tf_op jit(solution)/shard_map/ppermute | solution.py:18
  274.0 1.4 copy.240
  275.4 2.7 copy.241
  (172 shorter events, 32.7 us)
Async XLA Ops:
  0.0 133.6 %copy-start = (f32[36,9216]{1,0:T(8,128)S(1)}, f32[36,9216]{1,0:T(8,128)}, u32[]{:S(2)}) copy-start(f32[36,9216]{1,0:T(8,128)} %param.27) | copy-start | bytes 3981316
  1.6 20.4 %collective-permute-start.1 = (f32[4,1,24,24]{3,2,1,0:T(8,128)}, f32[4,1,24,24]{3,2,1,0:T(8,128)S(1)}, u32[]{:S(2)}, u32[]{:S(2)}) collective-permute-start(f32[4,1,24,24]{3,2,1,0:T(8,128)} %get-tuple-element.10), channel_id=1, source_target_pairs={{0,32},{32,64},{64,96},{96,128},{128,160},{160,192},{192,224},{1,3... | collective-permute-start | bytes 27656 | tf_op jit(solution)/shard_map/ppermute | solution.py:29
  5.9 25.2 %collective-permute-start = (f32[4,1,24,24]{3,2,1,0:T(8,128)}, f32[4,1,24,24]{3,2,1,0:T(8,128)S(1)}, u32[]{:S(2)}, u32[]{:S(2)}) collective-permute-start(f32[4,1,24,24]{3,2,1,0:T(8,128)} %get-tuple-element.9), channel_id=1, source_target_pairs={{32,0},{64,32},{96,64},{128,96},{160,128},{192,160},{224,192},{33,... | collective-permute-start | bytes 27656 | tf_op jit(solution)/shard_map/ppermute | solution.py:30
  10.7 9.8 %copy-start.1 = (f32[4,24,24,24]{3,2,1,0:T(8,128)S(1)}, f32[4,24,24,24]{3,2,1,0:T(8,128)}, u32[]{:S(2)}) copy-start(f32[4,24,24,24]{3,2,1,0:T(8,128)} %param.15) | copy-start | bytes 663556
  10.7 11.2 %copy-start.5 = (f32[24,24,24]{2,1,0:T(8,128)S(1)}, f32[24,24,24]{2,1,0:T(8,128)}, u32[]{:S(2)}) copy-start(f32[24,24,24]{2,1,0:T(8,128)} %param.16) | copy-start | bytes 165892
  12.7 15.1 %collective-permute-start.4 = (f32[4,24,24,1]{2,1,3,0:T(8,128)S(1)}, f32[4,24,24,1]{2,1,3,0:T(8,128)S(1)}, u32[]{:S(2)}, u32[]{:S(2)}) collective-permute-start(f32[4,24,24,1]{2,1,3,0:T(8,128)S(1)} %copy.258), channel_id=1, source_target_pairs={{1,0},{2,1},{3,2},{4,3},{5,4},{6,5},{7,6},{9,8},{10,9},{11,10},{12... | collective-permute-start | bytes 27656 | tf_op jit(solution)/shard_map/ppermute | solution.py:30
  17.5 12.0 %collective-permute-start.5 = (f32[4,24,24,1]{2,1,3,0:T(8,128)S(1)}, f32[4,24,24,1]{2,1,3,0:T(8,128)S(1)}, u32[]{:S(2)}, u32[]{:S(2)}) collective-permute-start(f32[4,24,24,1]{2,1,3,0:T(8,128)S(1)} %copy.259), channel_id=1, source_target_pairs={{0,1},{1,2},{2,3},{3,4},{4,5},{5,6},{6,7},{8,9},{9,10},{10,11},{11... | collective-permute-start | bytes 27656 | tf_op jit(solution)/shard_map/ppermute | solution.py:29
  20.6 7.1 %collective-permute-start.2 = (f32[4,24,1,24]{3,1,2,0:T(8,128)S(1)}, f32[4,24,1,24]{3,1,2,0:T(8,128)S(1)}, u32[]{:S(2)}, u32[]{:S(2)}) collective-permute-start(f32[4,24,1,24]{3,1,2,0:T(8,128)S(1)} %bitcast.160), channel_id=1, source_target_pairs={{8,0},{16,8},{24,16},{9,1},{17,9},{25,17},{10,2},{18,10},{26,18},{... | collective-permute-start | bytes 27656 | tf_op jit(solution)/shard_map/ppermute | solution.py:30
  21.9 5.8 %collective-permute-start.3 = (f32[4,24,1,24]{3,1,2,0:T(8,128)S(1)}, f32[4,24,1,24]{3,1,2,0:T(8,128)S(1)}, u32[]{:S(2)}, u32[]{:S(2)}) collective-permute-start(f32[4,24,1,24]{3,1,2,0:T(8,128)S(1)} %bitcast.159), channel_id=1, source_target_pairs={{0,8},{8,16},{16,24},{1,9},{9,17},{17,25},{2,10},{10,18},{18,26},{... | collective-permute-start | bytes 27656 | tf_op jit(solution)/shard_map/ppermute | solution.py:29
  37.0 5.5 %copy-start.2 = (f32[4,24,24,24]{3,2,1,0:T(8,128)}, f32[4,24,24,24]{3,2,1,0:T(8,128)S(1)}, u32[]{:S(2)}) copy-start(f32[4,24,24,24]{3,2,1,0:T(8,128)S(1)} %fusion.3) | copy-start | bytes 663556
  37.0 5.4 %collective-permute-start.6 = (f32[4,1,24,24]{3,2,1,0:T(8,128)S(1)}, f32[4,1,24,24]{3,2,1,0:T(8,128)S(1)}, u32[]{:S(2)}, u32[]{:S(2)}) collective-permute-start(f32[4,1,24,24]{3,2,1,0:T(8,128)S(1)} %slice.264), channel_id=1, source_target_pairs={{0,32},{32,64},{64,96},{96,128},{128,160},{160,192},{192,224},{1,3... | collective-permute-start | bytes 27656 | tf_op jit(solution)/shard_map/ppermute | solution.py:18
  42.6 4.9 %collective-permute-start.7 = (f32[4,25,1,24]{1,3,2,0:T(8,128)S(1)}, f32[4,25,1,24]{1,3,2,0:T(8,128)S(1)}, u32[]{:S(2)}, u32[]{:S(2)}) collective-permute-start(f32[4,25,1,24]{1,3,2,0:T(8,128)S(1)} %copy.207), channel_id=1, source_target_pairs={{0,8},{8,16},{16,24},{1,9},{9,17},{17,25},{2,10},{10,18},{18,26},{... | collective-permute-start | bytes 28808 | tf_op jit(solution)/shard_map/ppermute | solution.py:18
  50.3 8.7 %copy-start.3 = (f32[4,24,24,24]{3,2,1,0:T(8,128)S(1)}, f32[4,24,24,24]{3,2,1,0:T(8,128)}, u32[]{:S(2)}) copy-start(f32[4,24,24,24]{3,2,1,0:T(8,128)} %copy-done.2) | copy-start | bytes 663556
  50.3 6.7 %collective-permute-start.8 = (f32[4,25,25,1]{2,1,3,0:T(8,128)S(1)}, f32[4,25,25,1]{2,1,3,0:T(8,128)S(1)}, u32[]{:S(2)}, u32[]{:S(2)}) collective-permute-start(f32[4,25,25,1]{2,1,3,0:T(8,128)S(1)} %copy.209), channel_id=1, source_target_pairs={{0,1},{1,2},{2,3},{3,4},{4,5},{5,6},{6,7},{8,9},{9,10},{10,11},{11... | collective-permute-start | bytes 30008 | tf_op jit(solution)/shard_map/ppermute | solution.py:18
  64.4 5.4 %copy-start.14 = (s32[1,1,1,216]{3,2,1,0:T(1,128)S(1)}, s32[1,1,1,216]{3,2,1,0:T(1,128)}, u32[]{:S(2)}) copy-start(s32[1,1,1,216]{3,2,1,0:T(1,128)} %param.17) | copy-start | bytes 2596
  65.8 5.0 %collective-permute-start.9 = (f32[4,1,12,12]{3,2,1,0:T(8,128)S(1)}, f32[4,1,12,12]{3,2,1,0:T(8,128)S(1)}, u32[]{:S(2)}, u32[]{:S(2)}) collective-permute-start(f32[4,1,12,12]{3,2,1,0:T(8,128)S(1)} %slice.265), channel_id=1, source_target_pairs={{0,32},{32,64},{64,96},{96,128},{128,160},{160,192},{192,224},{1,3... | collective-permute-start | bytes 6920 | tf_op jit(solution)/shard_map/ppermute | solution.py:18
  70.9 4.9 %collective-permute-start.10 = (f32[4,13,1,12]{3,2,1,0:T(1,128)S(1)}, f32[4,13,1,12]{3,2,1,0:T(1,128)S(1)}, u32[]{:S(2)}, u32[]{:S(2)}) collective-permute-start(f32[4,13,1,12]{3,2,1,0:T(1,128)S(1)} %pad_maximum_fusion.25), channel_id=1, source_target_pairs={{0,8},{8,16},{16,24},{1,9},{9,17},{17,25},{2,10},{10,18},{18,26},{... | collective-permute-start | bytes 7496 | tf_op jit(solution)/shard_map/ppermute | solution.py:18
  76.0 11.0 %collective-permute-start.11 = (f32[4,13,13,1]{3,2,1,0:T(8,128)S(1)}, f32[4,13,13,1]{3,2,1,0:T(8,128)S(1)}, u32[]{:S(2)}, u32[]{:S(2)}) collective-permute-start(f32[4,13,13,1]{3,2,1,0:T(8,128)S(1)} %pad_maximum_fusion.13), channel_id=1, source_target_pairs={{0,1},{1,2},{2,3},{3,4},{4,5},{5,6},{6,7},{8,9},{9,10},{10,11},{11... | collective-permute-start | bytes 8120 | tf_op jit(solution)/shard_map/ppermute | solution.py:18
  87.3 3.1 %copy-start.6 = (f32[1,1,1,125,125]{4,2,3,1,0:T(1,128)S(1)}, f32[1,1,1,125,125]{4,2,3,1,0:T(1,128)}, u32[]{:S(2)}) copy-start(f32[1,1,1,125,125]{4,2,3,1,0:T(1,128)} %param.18) | copy-start | bytes 187504
  87.3 3.2 %copy-start.10 = (f32[1,1,1,125,50]{3,2,4,1,0:T(1,128)S(1)}, f32[1,1,1,125,50]{3,2,4,1,0:T(1,128)}, u32[]{:S(2)}) copy-start(f32[1,1,1,125,50]{3,2,4,1,0:T(1,128)} %param.19) | copy-start | bytes 75004
  87.3 5.4 %copy-start.9 = (f32[1,1,25,200]{3,1,2,0:T(1,128)S(1)}, f32[1,1,25,200]{3,1,2,0:T(1,128)}, u32[]{:S(2)}) copy-start(f32[1,1,25,200]{3,1,2,0:T(1,128)} %param.22) | copy-start | bytes 60004
  87.5 5.4 %copy-start.4 = (f32[1,30,960]{2,0,1:T(1,128)S(1)}, f32[1,30,960]{2,0,1:T(1,128)}, u32[]{:S(2)}) copy-start(f32[1,30,960]{2,0,1:T(1,128)} %param.25) | copy-start | bytes 345604
  90.4 10.7 %copy-start.8 = (f32[1,1,1,125,60]{3,2,4,1,0:T(1,128)S(1)}, f32[1,1,1,125,60]{3,2,4,1,0:T(1,128)}, u32[]{:S(2)}) copy-start(f32[1,1,1,125,60]{3,2,4,1,0:T(1,128)} %param.20) | copy-start | bytes 90004
  90.5 15.2 %copy-start.12 = (f32[1,1,1,25,60]{4,2,3,1,0:T(1,128)S(1)}, f32[1,1,1,25,60]{4,2,3,1,0:T(1,128)}, u32[]{:S(2)}) copy-start(f32[1,1,1,25,60]{4,2,3,1,0:T(1,128)} %param.23) | copy-start | bytes 18004
  90.5 16.7 %copy-start.7 = (f32[1,1,1,125,72]{3,4,2,1,0:T(8,128)S(1)}, f32[1,1,1,125,72]{3,4,2,1,0:T(8,128)}, u32[]{:S(2)}) copy-start(f32[1,1,1,125,72]{3,4,2,1,0:T(8,128)} %param.21) | copy-start | bytes 108004
  90.8 5.7 %collective-permute-start.12 = (f32[4,25]{1,0:T(4,128)S(1)}, f32[4,25]{1,0:T(4,128)S(1)}, u32[]{:S(2)}, u32[]{:S(2)}) collective-permute-start(f32[4,25]{1,0:T(4,128)S(1)} %slice.237), channel_id=1, source_target_pairs={{1,0},{2,1},{3,2},{4,3},{5,4},{6,5},{7,6},{9,8},{10,9},{11,10},{12... | collective-permute-start | bytes 1208 | tf_op jit(solution)/shard_map/ppermute | solution.py:18
  93.5 27.4 %copy-start.11 = (f32[1,1,1,25,72]{4,2,3,1,0:T(1,128)S(1)}, f32[1,1,1,25,72]{4,2,3,1,0:T(1,128)}, u32[]{:S(2)}) copy-start(f32[1,1,1,25,72]{4,2,3,1,0:T(1,128)} %param.24) | copy-start | bytes 21604
  93.5 34.7 %copy-start.13 = (f32[1,1,1,30,72]{4,2,3,1,0:T(1,128)S(1)}, f32[1,1,1,30,72]{4,2,3,1,0:T(1,128)}, u32[]{:S(2)}) copy-start(f32[1,1,1,30,72]{4,2,3,1,0:T(1,128)} %param.26) | copy-start | bytes 25924
  97.3 8.4 %all-to-all-start = ((f32[8,4,25]{2,1,0:T(4,128)}), f32[8,4,25]{2,1,0:T(4,128)S(1)}, u32[]{:S(2)}, u32[]{:S(2)}) async-start(f32[8,4,25]{2,1,0:T(4,128)} %convolution_bitcast_fusion.1), calls=%async_computation | async-start | bytes 32768 | tf_op jit(solution)/shard_map/all_to_all | solution.py:48
  105.9 4.9 %collective-permute-start.13 = (f32[4,30]{1,0:T(4,128)S(1)}, f32[4,30]{1,0:T(4,128)S(1)}, u32[]{:S(2)}, u32[]{:S(2)}) collective-permute-start(f32[4,30]{1,0:T(4,128)S(1)} %slice.240), channel_id=1, source_target_pairs={{8,0},{16,8},{24,16},{9,1},{17,9},{25,17},{10,2},{18,10},{26,18},{... | collective-permute-start | bytes 1448 | tf_op jit(solution)/shard_map/ppermute | solution.py:18
  113.6 14.6 %all-to-all-start.1 = ((f32[32,4,30]{2,1,0:T(4,128)}), f32[32,4,30]{2,1,0:T(4,128)S(1)}, u32[]{:S(2)}, u32[]{:S(2)}) async-start(f32[32,4,30]{2,1,0:T(4,128)} %copy.215), calls=%async_computation.1 | async-start | bytes 131072 | tf_op jit(solution)/shard_map/all_to_all | solution.py:48
  128.4 5.2 %collective-permute-start.14 = (f32[4,36]{1,0:T(4,128)S(1)}, f32[4,36]{1,0:T(4,128)S(1)}, u32[]{:S(2)}, u32[]{:S(2)}) collective-permute-start(f32[4,36]{1,0:T(4,128)S(1)} %slice.243), channel_id=1, source_target_pairs={{32,0},{64,32},{96,64},{128,96},{160,128},{192,160},{224,192},{33,... | collective-permute-start | bytes 1736 | tf_op jit(solution)/shard_map/ppermute | solution.py:18
  197.2 3.0 %collective-permute-start.15 = (f32[4,36]{1,0:T(4,128)S(1)}, f32[4,36]{1,0:T(4,128)S(1)}, u32[]{:S(2)}, u32[]{:S(2)}) collective-permute-start(f32[4,36]{1,0:T(4,128)S(1)} %fusion.85), channel_id=1, source_target_pairs={{0,32},{32,64},{64,96},{96,128},{128,160},{160,192},{192,224},{1,3... | collective-permute-start | bytes 1736 | tf_op jit(solution)/shard_map/ppermute | solution.py:18
  212.9 3.0 %collective-permute-start.16 = (f32[4,30]{1,0:T(4,128)S(1)}, f32[4,30]{1,0:T(4,128)S(1)}, u32[]{:S(2)}, u32[]{:S(2)}) collective-permute-start(f32[4,30]{1,0:T(4,128)S(1)} %fusion.21), channel_id=1, source_target_pairs={{0,8},{8,16},{16,24},{1,9},{9,17},{17,25},{2,10},{10,18},{18,26},{... | collective-permute-start | bytes 1448 | tf_op jit(solution)/shard_map/ppermute | solution.py:18
  224.5 3.5 %collective-permute-start.17 = (f32[4,25]{1,0:T(4,128)S(1)}, f32[4,25]{1,0:T(4,128)S(1)}, u32[]{:S(2)}, u32[]{:S(2)}) collective-permute-start(f32[4,25]{1,0:T(4,128)S(1)} %fusion.39), channel_id=1, source_target_pairs={{0,1},{1,2},{2,3},{3,4},{4,5},{5,6},{6,7},{8,9},{9,10},{10,11},{11... | collective-permute-start | bytes 1208 | tf_op jit(solution)/shard_map/ppermute | solution.py:18
  230.2 5.3 %collective-permute-start.18 = (f32[4,1,6,6]{3,2,1,0:T(8,128)S(1)}, f32[4,1,6,6]{3,2,1,0:T(8,128)S(1)}, u32[]{:S(2)}, u32[]{:S(2)}) collective-permute-start(f32[4,1,6,6]{3,2,1,0:T(8,128)S(1)} %slice.270), channel_id=1, source_target_pairs={{32,0},{64,32},{96,64},{128,96},{160,128},{192,160},{224,192},{33,... | collective-permute-start | bytes 1736 | tf_op jit(solution)/shard_map/ppermute | solution.py:18
  235.5 5.0 %collective-permute-start.19 = (f32[4,7,1,6]{3,2,1,0:T(1,128)S(1)}, f32[4,7,1,6]{3,2,1,0:T(1,128)S(1)}, u32[]{:S(2)}, u32[]{:S(2)}) collective-permute-start(f32[4,7,1,6]{3,2,1,0:T(1,128)S(1)} %slice.271), channel_id=1, source_target_pairs={{8,0},{16,8},{24,16},{9,1},{17,9},{25,17},{10,2},{18,10},{26,18},{... | collective-permute-start | bytes 2024 | tf_op jit(solution)/shard_map/ppermute | solution.py:18
  240.6 8.1 %collective-permute-start.20 = (f32[4,7,7,1]{3,2,1,0:T(8,128)S(1)}, f32[4,7,7,1]{3,2,1,0:T(8,128)S(1)}, u32[]{:S(2)}, u32[]{:S(2)}) collective-permute-start(f32[4,7,7,1]{3,2,1,0:T(8,128)S(1)} %pad_maximum_fusion.20), channel_id=1, source_target_pairs={{1,0},{2,1},{3,2},{4,3},{5,4},{6,5},{7,6},{9,8},{10,9},{11,10},{12... | collective-permute-start | bytes 2360 | tf_op jit(solution)/shard_map/ppermute | solution.py:18
  250.1 4.9 %collective-permute-start.21 = (f32[4,1,12,12]{2,0,3,1:T(4,128)S(1)}, f32[4,1,12,12]{2,0,3,1:T(4,128)S(1)}, u32[]{:S(2)}, u32[]{:S(2)}) collective-permute-start(f32[4,1,12,12]{2,0,3,1:T(4,128)S(1)} %slice.278), channel_id=1, source_target_pairs={{32,0},{64,32},{96,64},{128,96},{160,128},{192,160},{224,192},{33,... | collective-permute-start | bytes 6920 | tf_op jit(solution)/shard_map/ppermute | solution.py:18
  255.0 8.8 %collective-permute-start.22 = (f32[4,13,1,12]{2,0,3,1:T(4,128)S(1)}, f32[4,13,1,12]{2,0,3,1:T(4,128)S(1)}, u32[]{:S(2)}, u32[]{:S(2)}) collective-permute-start(f32[4,13,1,12]{2,0,3,1:T(4,128)S(1)} %pad_maximum_fusion.16), channel_id=1, source_target_pairs={{8,0},{16,8},{24,16},{9,1},{17,9},{25,17},{10,2},{18,10},{26,18},{... | collective-permute-start | bytes 7496 | tf_op jit(solution)/shard_map/ppermute | solution.py:18
  263.9 7.3 %collective-permute-start.23 = (f32[4,13,13,1]{2,0,3,1:T(4,128)S(1)}, f32[4,13,13,1]{2,0,3,1:T(4,128)S(1)}, u32[]{:S(2)}, u32[]{:S(2)}) collective-permute-start(f32[4,13,13,1]{2,0,3,1:T(4,128)S(1)} %pad_maximum_fusion.23), channel_id=1, source_target_pairs={{1,0},{2,1},{3,2},{4,3},{5,4},{6,5},{7,6},{9,8},{10,9},{11,10},{12... | collective-permute-start | bytes 8120 | tf_op jit(solution)/shard_map/ppermute | solution.py:18
where the time goes:
time: 279 us; the launch traced here: 278 us
  starting transfers between devices  77.4 us (28%)
  blocking collectives  73.5 us (26%)
  waiting for transfers between devices  62.6 us (22%)
  local copies, waits for them, and re-layouts  40.7 us (15%)
  other arithmetic  15.3 us (5%)
  matrix products  7.63 us (3%)
    ppermute x18, waiting for transfers between devices, shifted(): return lax.ppermute(shard, axis, pairs)  50.9 us
    ppermute x18, starting transfers between devices, shifted(): return lax.ppermute(shard, axis, pairs)  49.6 us
    all_to_all x4, blocking collectives, sent_to_all(): return lax.all_to_all(copies, axis, split_axis=0, concat_axis=0, tiled=True)  43.2 us
    all_to_all x1, blocking collectives, sum_by_axis(): return jnp.sum(lax.all_to_all(own, far, 0, 0, tiled=True), axis=0)  21.2 us
    unnamed x48, local copies, waits for them, and re-layouts  11.9 us
    all_to_all x2, waiting for transfers between devices, summed_on_arrival(): lax.all_to_all(cut_along(shard, dim, peers), axis, 0, 0, tiled=True)  11.7 us
    ppermute x3, starting transfers between devices, padded_2(): lax.ppermute(last, axis, up)  11.4 us
    all_to_all x2, starting transfers between devices, summed_on_arrival(): lax.all_to_all(cut_along(shard, dim, peers), axis, 0, 0, tiled=True)  11 us
  transfers between devices with their start and end apart: 26, of which 20 were waited for; matrix products, arithmetic and copies ran while one was open for 5% of the time, Pallas kernels for 0%

commit v1 on v0

v1 whole, which is shorter than its diff:
```python
import numpy as np
import jax
import jax.numpy as jnp
from jax import lax
from jax.experimental import pallas as pl
from jax.experimental.pallas import tpu as pltpu
from jax.sharding import PartitionSpec as P

PLANE = ("gy", "gz")
precise = lax.Precision.HIGHEST


def shifted(shard, axis, by):
    peers = lax.axis_size(axis)
    pairs = [(i, i + by) for i in range(peers) if 0 <= i + by < peers]
    return lax.ppermute(shard, axis, pairs)


def exchanged(pieces, axis):
    return lax.all_to_all(pieces, axis, split_axis=0, concat_axis=0, tiled=True)


def sent_to_all(shard, axis):
    copies = jnp.broadcast_to(shard, (lax.axis_size(axis), *shard.shape))
    return exchanged(copies, axis)


def product(operand, matrix):
    return jnp.dot(operand, matrix, precision=precise, preferred_element_type=jnp.float32)


def product_back(operand, matrix):
    return lax.dot_general(
        operand,
        matrix,
        (((1,), (1,)), ((), ())),
        precision=precise,
        preferred_element_type=jnp.float32,
    )


def two_restrictions(distance):
    return np.maximum(0.0, 4.0 - np.abs(distance)) / 16.0


def restriction_weights(fine):
    cell = 4.0 * (np.arange(fine // 4 + 2) - 1)[:, None]
    at = np.arange(fine)[None, :]
    own = two_restrictions(cell - at)
    through_before = two_restrictions(cell - (at - 1))
    beside = through_before + two_restrictions(cell - (at + 1))
    before = np.where(at == 0, through_before, 0.0)
    return own, beside, before


def prolongation_weights(fine):
    at = np.arange(fine)[:, None] / 4.0
    cell = np.arange(fine // 4 + 1)[None, :]
    return np.maximum(0.0, 1.0 - np.abs(at - cell))


def by_lane(weights, count):
    coarse, fine = weights.shape
    out = np.zeros((count, fine, coarse, count), np.float32)
    for r in range(count):
        out[r, :, :, r] = weights.T
    return out.reshape(count, fine, coarse * count)


def parts_of(values):
    first = values.astype(jnp.bfloat16)
    rest = values - first.astype(jnp.float32)
    second = rest.astype(jnp.bfloat16)
    third = (rest - second.astype(jnp.float32)).astype(jnp.bfloat16)
    return first, second, third


def dot(left, right):
    return jnp.dot(left, right, preferred_element_type=jnp.float32)


def times_weights(values, weights):
    first, second, third = parts_of(values)
    return dot(first, weights) + (dot(second, weights) + dot(third, weights))


def weights_times(weights, values):
    first, second, third = parts_of(values)
    return dot(weights, first) + (dot(weights, second) + dot(weights, third))


def restrict_body(
    own, beside, before, edge, rhs, iterate, coefficient, z_own, z_beside, z_before,
    y_own, y_beside, y_before, out,
):
    count, fine = rhs.shape[:2]
    coarse = own.shape[0]
    at_x, at_y, at_z = edge[0], edge[1], edge[2]
    beside_sum = None
    own_sum = None
    for r in range(count):
        planes = [iterate[r, x] for x in range(fine)]
        gaps = [rhs[r, x] - (6.0 + coefficient[x]) * planes[x] for x in range(fine)]
        values, cells = [], []
        for i in range(coarse):
            value = cell = None
            for x in range(fine):
                if own[i, x]:
                    term = float(own[i, x]) * gaps[x]
                    value = term if value is None else value + term
                    term = float(own[i, x]) * planes[x]
                    cell = term if cell is None else cell + term
                if beside[i, x]:
                    weight = float(beside[i, x])
                    if before[i, x]:
                        weight = weight - at_x * float(before[i, x])
                    term = weight * planes[x]
                    value = term if value is None else value + term
            values.append(value)
            cells.append(jnp.zeros_like(planes[0]) if cell is None else cell)
        value = jnp.concatenate(values, axis=0)
        cell = jnp.concatenate(cells, axis=0)
        z_pair = (z_beside[r] - at_z * z_before[r]).astype(jnp.bfloat16)
        z_cell = z_own[r].astype(jnp.bfloat16)
        term = times_weights(value, z_cell) + times_weights(cell, z_pair)
        beside_sum = term if beside_sum is None else beside_sum + term
        term = times_weights(cell, z_cell)
        own_sum = term if own_sum is None else own_sum + term
    y_pair = (y_beside[...] - at_y * y_before[...]).astype(jnp.bfloat16)
    y_cell = y_own[...].astype(jnp.bfloat16)
    result = weights_times(y_cell, beside_sum) + weights_times(y_pair, own_sum)
    out[...] = result.reshape(out.shape)


def restricted(edge, right_side, iterate, coefficient):
    count, fine = right_side.shape[:2]
    own, beside, before = restriction_weights(fine)
    coarse = own.shape[0]
    lanes = [by_lane(w, count) for w in (own, beside, before)]
    rows = [np.kron(np.eye(coarse), w).astype(np.float32) for w in (own, beside, before)]

    def body(*refs):
        restrict_body(own, beside, before, *refs)

    vmem = pl.BlockSpec(memory_space=pltpu.VMEM)
    return pl.pallas_call(
        body,
        out_shape=jax.ShapeDtypeStruct((coarse, coarse, coarse * count), jnp.float32),
        in_specs=[pl.BlockSpec(memory_space=pltpu.SMEM)] + [vmem] * 9,
        out_specs=vmem,
        name="restrict_twice",
    )(edge, right_side, iterate, coefficient, *lanes, *rows)


def prolong_body(window, y_weights, z_weights, out):
    count, fine = out.shape[:2]
    cells = window.shape[0]
    flat = window[...].reshape(cells * window.shape[1], window.shape[2])
    along_y = weights_times(y_weights[...].astype(jnp.bfloat16), flat)
    for r in range(count):
        along_z = times_weights(along_y, z_weights[r].astype(jnp.bfloat16))
        planes = [along_z[i * fine : (i + 1) * fine] for i in range(cells)]
        for i in range(cells - 1):
            for q in range(4):
                value = planes[i]
                if q:
                    value = (1.0 - q / 4.0) * value + (q / 4.0) * planes[i + 1]
                out[r, 4 * i + q] = value


def prolonged(window, count, fine):
    cells = window.shape[0]
    weights = prolongation_weights(fine)
    along_y = np.zeros((fine, window.shape[1]))
    along_y[:, :cells] = weights
    rows = np.kron(np.eye(cells), along_y).astype(np.float32)
    lanes = np.zeros((count, window.shape[2], fine), np.float32)
    for r in range(count):
        for k in range(cells):
            lanes[r, k * count + r] = weights[:, k]
    vmem = pl.BlockSpec(memory_space=pltpu.VMEM)
    return pl.pallas_call(
        prolong_body,
        out_shape=jax.ShapeDtypeStruct((count, fine, fine, fine), jnp.float32),
        in_specs=[vmem] * 3,
        out_specs=vmem,
        name="prolong_twice",
    )(window, rows, lanes)


def padded(values, dim, before, after):
    widths = [(0, 0)] * values.ndim
    widths[dim] = (before, after)
    return jnp.pad(values, widths)


def with_neighbours(values, axis, dim, width):
    length = values.shape[dim]
    first = lax.slice_in_dim(values, 0, width, axis=dim)
    last = lax.slice_in_dim(values, length - width, length, axis=dim)
    from_below = shifted(last, axis, 1)
    from_above = shifted(first, axis, -1)
    inner = lax.slice_in_dim(values, width, length - width, axis=dim)
    room = length - 3 * width
    return inner + padded(from_below, dim, 0, room) + padded(from_above, dim, room, 0)


def with_next(values, axis, dim, width):
    first = lax.slice_in_dim(values, 0, width, axis=dim)
    return jnp.concatenate([values, shifted(first, axis, -1)], axis=dim)


def per_device(
    right_side,
    iterate,
    coefficient,
    ordering,
    leaf_inverse,
    leaf_first,
    leaf_second,
    leaf_top,
    first_inverse,
    first_second,
    first_top,
    second_inverse,
    second_top,
    top_inverse,
):
    count, fine = right_side.shape[:2]
    leaf_size = leaf_inverse.shape[-1]
    first_size = first_second.shape[3]
    second_size = second_top.shape[3]
    top_total = top_inverse.shape[1]
    top_size = top_inverse.shape[0]
    side = fine // 4
    cells = side**3
    first_rows = first_inverse[0, 0]
    second_rows = second_inverse[0]
    to_first = leaf_first[0, 0, 0]
    to_second = leaf_second[0, 0, 0]
    to_top = leaf_top[0, 0, 0]
    first_to_second = first_second[0, 0, 0]
    first_to_top = first_top[0, 0, 0]
    second_to_top = second_top[0, 0, 0]
    leaf_block = leaf_inverse[0, 0, 0]

    edge = jnp.stack([lax.axis_index(a) == 0 for a in ("gx", "gy", "gz")]).astype(jnp.float32)
    partial = restricted(edge, right_side, iterate, coefficient)
    coarse = with_neighbours(partial, "gx", 0, 1)
    first_below = shifted(first_rows, "gz", 1)
    second_below = shifted(second_rows, "gy", 1)
    top_rows, coarse = lax.optimization_barrier((top_inverse, coarse))
    top_below = shifted(top_rows, "gx", 1)
    coarse = with_neighbours(coarse, "gy", 1, 1)
    coarse = with_neighbours(coarse, "gz", 2, count)
    natural = coarse.reshape(cells, count).T

    chosen_at = ordering.reshape(-1)[:, None] == jnp.arange(cells, dtype=jnp.int32)[None, :]
    pick = chosen_at.astype(jnp.float32)
    chosen = product_back(natural, pick)
    first_end = leaf_size + first_size
    second_end = first_end + second_size
    leaf_rhs = chosen[:, :leaf_size]
    first_rhs = chosen[:, leaf_size:first_end]
    second_rhs = chosen[:, first_end:second_end]
    top_rhs = chosen[:, second_end:]

    leaf_solved = product(leaf_rhs, leaf_block)
    toward = product(leaf_solved, to_first)
    terms = product(first_rhs - toward[:, :first_size], first_rows)
    terms = terms - product(toward[:, first_size:], first_below)
    peers = lax.axis_size("gz")
    pieces = jnp.moveaxis(terms.reshape(count, peers, first_size), 1, 0)
    first_own = jnp.sum(exchanged(pieces, "gz"), axis=0)

    toward = product(leaf_solved, to_second) + product(first_own, first_to_second)
    terms = product(second_rhs - toward[:, :second_size], second_rows)
    terms = terms - product(toward[:, second_size:], second_below)
    plane_peers = lax.axis_size(PLANE)
    pieces = jnp.moveaxis(terms.reshape(count, plane_peers, second_size), 1, 0)
    second_own = jnp.sum(exchanged(pieces, PLANE), axis=0)

    toward = (
        product(leaf_solved, to_top)
        + product(first_own, first_to_top)
        + product(second_own, second_to_top)
    )
    terms = product(top_rhs - toward[:, :top_size], top_inverse)
    terms = terms - product(toward[:, top_size:], top_below)
    width = 128 * -(-top_total // (128 * plane_peers))
    used = top_total // width
    pieces = jnp.moveaxis(terms.reshape(count, used, width), 1, 0)
    pieces = padded(pieces, 0, 0, plane_peers - used)
    chunk = jnp.sum(exchanged(pieces, PLANE), axis=0)
    chunk = jnp.sum(sent_to_all(chunk, "gx"), axis=0)
    top_whole = jnp.moveaxis(sent_to_all(chunk, PLANE)[:used], 0, 1).reshape(count, top_total)

    top_back = product_back(top_whole, top_inverse)
    top_pair = jnp.concatenate([top_back, product_back(top_whole, top_below)], axis=1)
    second_gap = second_own - product_back(top_pair, second_to_top)
    second_whole = jnp.moveaxis(sent_to_all(second_gap, PLANE), 0, 1).reshape(count, -1)
    second_back = product_back(second_whole, second_rows)
    second_pair = jnp.concatenate([second_back, product_back(second_whole, second_below)], axis=1)
    first_gap = (
        first_own
        - product_back(second_pair, first_to_second)
        - product_back(top_pair, first_to_top)
    )
    first_whole = jnp.moveaxis(sent_to_all(first_gap, "gz"), 0, 1).reshape(count, -1)
    first_back = product_back(first_whole, first_rows)
    first_pair = jnp.concatenate([first_back, product_back(first_whole, first_below)], axis=1)
    leaf_gap = (
        leaf_solved - product_back(first_pair, to_first) - product_back(second_pair, to_second)
    )
    leaf_gap = leaf_gap - product_back(top_pair, to_top)
    leaf_back = product_back(leaf_gap, leaf_block)
    ordered = jnp.concatenate([leaf_back, first_back, second_back, top_back], axis=1)
    natural = product(ordered, pick)

    window = natural.T.reshape(side, side, side * count)
    window = with_next(window, "gx", 0, 1)
    window = with_next(window, "gy", 1, 1)
    window = with_next(window, "gz", 2, count)
    window = jnp.pad(window, ((0, 0), (0, 1), (0, count)))
    return prolonged(window, count, fine)


def solution(mesh):
    blocks = P("gx", "gy", "gz")
    return jax.shard_map(
        per_device,
        mesh=mesh,
        in_specs=(
            P(None, "gx", "gy", "gz"),
            P(None, "gx", "gy", "gz"),
            blocks,
            blocks,
            blocks,
            blocks,
            blocks,
            blocks,
            blocks,
            blocks,
            blocks,
            P("gx", PLANE, None),
            blocks,
            P(("gx", "gy", "gz"), None),
        ),
        out_specs=P(None, "gx", "gy", "gz"),
        check_vma=False,
    )
```

time: 279 us -> 163 us (0.58)
  waiting for transfers between devices: 62.6 us -> 27.3 us
  local copies, waits for them, and re-layouts: 40.7 us -> 5.96 us
  starting transfers between devices: 77.4 us -> 44.8 us
  blocking collectives: 73.5 us -> 61.1 us
  other arithmetic: 15.3 us -> 3.51 us
  Pallas kernels: 0 us -> 6.3 us
  matrix products: 7.63 us -> 12.3 us
    ppermute x18 -> x12, waiting for transfers between devices: 50.9 us -> 16.3 us  [shifted(): return lax.ppermute(shard, axis, pairs)]
    ppermute x6 -> x0, starting transfers between devices: 16.8 us -> none  [the longest x3 11.4 us: padded_2(): lax.ppermute(last, axis, up)]
    ppermute x18 -> x12, starting transfers between devices: 49.6 us -> 36.3 us  [shifted(): return lax.ppermute(shard, axis, pairs)]
    all_to_all x6 -> x5, blocking collectives: 73.5 us -> 61.1 us  [exchanged(): return lax.all_to_all(pieces, axis, split_axis=0, concat_axis=0, tiled=True)]
    slice x25 -> x8, local copies, waits for them, and re-layouts: 12.6 us -> 0.99 us  [the longest x3 0.79 us: with_neighbours(): last = lax.slice_in_dim(values, length - width, length, axis=dim)]
    unnamed x48 -> x39, local copies, waits for them, and re-layouts: 11.9 us -> 1.4 us
    pallas_call x0 -> x2, Pallas kernels: none -> 6.3 us  [the longest x1 3.67 us: restricted(): pl.pallas_call(body, out_shape=jax.ShapeDtypeStruct((coarse, coarse, coar...]
    sub x1 -> x0, other arithmetic: 5.19 us -> none  [residual_of(): return right_side - ((6.0 + coefficient) * iterate - beside)]
  transfers between devices with their start and end apart: 26 -> 14, of which waited for: 20 -> 8; matrix products, arithmetic and copies ran while one was open for 5% -> 7% of each run, Pallas kernels for 0% -> 0%
where the time goes in v1:
time: 163 us; the launch traced here: 162 us
  blocking collectives  61.1 us (37%)
  starting transfers between devices  44.8 us (27%)
  waiting for transfers between devices  27.3 us (17%)
  matrix products  12.3 us (8%)
  Pallas kernels  6.3 us (4%)
  local copies, waits for them, and re-layouts  5.96 us (4%)
  other arithmetic  3.51 us (2%)
    all_to_all x5, blocking collectives, exchanged(): return lax.all_to_all(pieces, axis, split_axis=0, concat_axis=0, tiled=True)  61.1 us
    ppermute x12, starting transfers between devices, shifted(): return lax.ppermute(shard, axis, pairs)  36.3 us
    ppermute x12, waiting for transfers between devices, shifted(): return lax.ppermute(shard, axis, pairs)  16.3 us
    all_to_all x2, waiting for transfers between devices, exchanged(): return lax.all_to_all(pieces, axis, split_axis=0, concat_axis=0, tiled=True)  11 us
    all_to_all x2, starting transfers between devices, exchanged(): return lax.all_to_all(pieces, axis, split_axis=0, concat_axis=0, tiled=True)  8.47 us
    dot_general x14, matrix products, product(): jnp.dot(operand, matrix, precision=precise, preferred_element_type=jnp.fl...  6.69 us
    dot_general x14, matrix products, product_back(): lax.dot_general(operand, matrix, (((1,), (1,)), ((), ())), precision=prec...  5.6 us
    pallas_call x1, Pallas kernels, restricted(): pl.pallas_call(body, out_shape=jax.ShapeDtypeStruct((coarse, coarse, coar...  3.67 us
  transfers between devices with their start and end apart: 14, of which 8 were waited for; matrix products, arithmetic and copies ran while one was open for 7% of the time, Pallas kernels for 0%

profile of v1, /device:TPU:1, one launch (start us, length us, event | category | flops | bytes accessed | tf_op | source)
XLA Modules:
  0.0 161.7 jit_solution(15665059218790111211)
XLA Ops:
  0.0 0.7 add_convert_fusion.refs_0_
  0.7 3.7 %restrict_twice.1 = f32[8,8,32]{2,1,0:T(8,128)} custom-call(f32[3]{0:T(128)} %add_convert_fusion.refs_0_, f32[4,24,24,24]{3,2,1,0:T(8,128)} %refs_1_.1, f32[4,24,24,24]{3,2,1,0:T(8,128)} %refs_2_.1, f32[24,24,24]{2,1,0:T(8,128)} %refs_3_.1, f32[4,24,32]{2,1,0:T(8,128)} %constant.33.clone.refs_4_, f32[4,24,32]{2,1,0:T(8,128)} %constant.34.clone.refs_5_, ...), custom_call_target="tpu_custom_call" | custom-call | tf_op jit(solution)/shard_map/restrict_twice/pallas_call | solution.py:146
  4.4 0.7 fusion.63
  5.1 4.3 %collective-permute-start = (f32[1,8,32]{2,1,0:T(8,128)S(1)}, f32[1,8,32]{2,1,0:T(8,128)S(1)}, u32[]{:S(2)}, u32[]{:S(2)}) collective-permute-start(f32[1,8,32]{2,1,0:T(8,128)S(1)} %get-tuple-element.9), channel_id=1, source_target_pairs={{0,32},{32,64},{64,96},{96,128},{128,160},{160,192},{192,224},{1,3... | collective-permute-start | bytes 3080 | tf_op jit(solution)/shard_map/ppermute | solution.py:16
  9.4 1.3 collective-permute-start.1
  10.7 3.2 %collective-permute-done.1 = f32[1,8,32]{2,1,0:T(8,128)S(1)} collective-permute-done((f32[1,8,32]{2,1,0:T(8,128)S(1)}, f32[1,8,32]{2,1,0:T(8,128)S(1)}, u32[]{:S(2)}, u32[]{:S(2)}) %collective-permute-start.1) | collective-permute-done | bytes 1056 | tf_op jit(solution)/shard_map/ppermute | solution.py:16
  14.0 0.7 fusion.24
  14.7 3.2 %collective-permute-start.2 = (f32[6,1,32]{2,1,0:T(1,128)S(1)}, f32[6,1,32]{2,1,0:T(1,128)S(1)}, u32[]{:S(2)}, u32[]{:S(2)}) collective-permute-start(f32[6,1,32]{2,1,0:T(1,128)S(1)} %get-tuple-element.13), channel_id=1, source_target_pairs={{0,8},{8,16},{16,24},{1,9},{9,17},{17,25},{2,10},{10,18},{18,26},{... | collective-permute-start | bytes 2312 | tf_op jit(solution)/shard_map/ppermute | solution.py:16
  17.9 1.3 collective-permute-start.3
  19.2 3.0 %collective-permute-done.3 = f32[6,1,32]{2,1,0:T(1,128)S(1)} collective-permute-done((f32[6,1,32]{2,1,0:T(1,128)S(1)}, f32[6,1,32]{2,1,0:T(1,128)S(1)}, u32[]{:S(2)}, u32[]{:S(2)}) %collective-permute-start.3) | collective-permute-done | bytes 800 | tf_op jit(solution)/shard_map/ppermute | solution.py:16
  22.4 6.3 %collective-permute-start.4 = (f32[6,6,4]{2,1,0:T(8,128)S(1)}, f32[6,6,4]{2,1,0:T(8,128)S(1)}, u32[]{:S(2)}, u32[]{:S(2)}) collective-permute-start(f32[6,6,4]{2,1,0:T(8,128)S(1)} %get-tuple-element.11), channel_id=1, source_target_pairs={{0,1},{1,2},{2,3},{3,4},{4,5},{5,6},{6,7},{8,9},{9,10},{10,11},{11... | collective-permute-start | bytes 1736 | tf_op jit(solution)/shard_map/ppermute | solution.py:16
  28.7 1.9 %collective-permute-start.5 = (f32[6,6,4]{2,1,0:T(8,128)S(1)}, f32[6,6,4]{2,1,0:T(8,128)S(1)}, u32[]{:S(2)}, u32[]{:S(2)}) collective-permute-start(f32[6,6,4]{2,1,0:T(8,128)S(1)} %get-tuple-element.12), channel_id=1, source_target_pairs={{1,0},{2,1},{3,2},{4,3},{5,4},{6,5},{7,6},{9,8},{10,9},{11,10},{12... | collective-permute-start | bytes 1736 | tf_op jit(solution)/shard_map/ppermute | solution.py:16
  30.6 0.6 copy.114
  31.3 3.6 %collective-permute-start.6 = (f32[25,200]{1,0:T(8,128)}, f32[25,200]{1,0:T(8,128)S(1)}, u32[]{:S(2)}, u32[]{:S(2)}) collective-permute-start(f32[25,200]{1,0:T(8,128)} %bitcast.81), channel_id=1, source_target_pairs={{0,1},{1,2},{2,3},{3,4},{4,5},{5,6},{6,7},{8,9},{9,10},{10,11},{11... | collective-permute-start | bytes 60008 | tf_op jit(solution)/shard_map/ppermute | solution.py:16
  34.9 0.7 copy.113
  35.6 3.2 %collective-permute-start.7 = (f32[30,960]{1,0:T(8,128)}, f32[30,960]{1,0:T(8,128)S(1)}, u32[]{:S(2)}, u32[]{:S(2)}) collective-permute-start(f32[30,960]{1,0:T(8,128)} %bitcast.80), channel_id=1, source_target_pairs={{0,8},{8,16},{16,24},{1,9},{9,17},{17,25},{2,10},{10,18},{18,26},{... | collective-permute-start | bytes 345608 | tf_op jit(solution)/shard_map/ppermute | solution.py:16
  38.8 3.6 %collective-permute-start.8 = (f32[36,9216]{1,0:T(8,128)S(1)}, f32[36,9216]{1,0:T(8,128)S(1)}, u32[]{:S(2)}, u32[]{:S(2)}) collective-permute-start(f32[36,9216]{1,0:T(8,128)S(1)} %copy-done.1), channel_id=1, source_target_pairs={{0,32},{32,64},{64,96},{96,128},{128,160},{160,192},{192,224},{1,3... | collective-permute-start | bytes 3981320 | tf_op jit(solution)/shard_map/ppermute | solution.py:16
  42.5 0.7 fusion.23
  43.2 0.8 reshape.26
  44.0 0.9 fusion.1
  45.3 0.2 fusion.11
  45.5 0.2 fusion.45
  45.7 0.2 convolution_subtract_fusion.2
  46.0 0.6 copy.115
  46.6 4.1 %all-to-all-start = ((f32[8,4,25]{2,1,0:T(4,128)}), f32[8,4,25]{2,1,0:T(4,128)S(1)}, u32[]{:S(2)}, u32[]{:S(2)}) async-start(f32[8,4,25]{2,1,0:T(4,128)} %bitcast.82), calls=%async_computation | async-start | bytes 32768 | tf_op jit(solution)/shard_map/all_to_all | solution.py:20
  50.9 4.5 %all-to-all-done = f32[8,4,25]{2,1,0:T(4,128)S(1)} async-done(((f32[8,4,25]{2,1,0:T(4,128)}), f32[8,4,25]{2,1,0:T(4,128)S(1)}, u32[]{:S(2)}, u32[]{:S(2)}) %all-to-all-start) | async-done | bytes 3232 | tf_op jit(solution)/shard_map/all_to_all | solution.py:20
  55.6 0.9 fusion.47
  56.5 0.2 convolution_subtract_fusion.1
  56.8 0.7 copy.42
  57.5 4.4 %all-to-all-start.1 = ((f32[32,4,30]{2,1,0:T(4,128)}), f32[32,4,30]{2,1,0:T(4,128)S(1)}, u32[]{:S(2)}, u32[]{:S(2)}) async-start(f32[32,4,30]{2,1,0:T(4,128)} %copy.42), calls=%async_computation.1 | async-start | bytes 131072 | tf_op jit(solution)/shard_map/all_to_all | solution.py:20
  61.9 0.8 convolution_add_fusion.1
  62.7 6.5 %all-to-all-done.1 = f32[32,4,30]{2,1,0:T(4,128)S(1)} async-done(((f32[32,4,30]{2,1,0:T(4,128)}), f32[32,4,30]{2,1,0:T(4,128)S(1)}, u32[]{:S(2)}, u32[]{:S(2)}) %all-to-all-start.1) | async-done | bytes 15392 | tf_op jit(solution)/shard_map/all_to_all | solution.py:20
  69.3 0.8 convolution_add_fusion
  70.1 1.5 fusion.46
  71.6 2.3 %collective-permute-done.8 = f32[36,9216]{1,0:T(8,128)S(1)} collective-permute-done((f32[36,9216]{1,0:T(8,128)S(1)}, f32[36,9216]{1,0:T(8,128)S(1)}, u32[]{:S(2)}, u32[]{:S(2)}) %collective-permute-start.8) | collective-permute-done | bytes 1327136 | tf_op jit(solution)/shard_map/ppermute | solution.py:16
  74.0 0.9 convolution_subtract_fusion
  74.9 13.7 %all_to_all.35 = f32[32,4,384]{2,1,0:T(4,128)S(1)} all-to-all(f32[32,4,384]{2,1,0:T(4,128)S(1)} %pad.38), channel_id=1, replica_groups=mesh['gx'=8,'gy'=4,'gz'=8] {'gy','gz'}, dimensions={0} | all-to-all | bytes 393216 | tf_op jit(solution)/shard_map/all_to_all | solution.py:20
  88.6 0.6 reduce_sum.38
  89.2 0.7 broadcast_in_dim.13
  89.9 15.8 %all_to_all.36 = f32[8,4,384]{2,1,0:T(4,128)S(1)} all-to-all(f32[8,4,384]{2,1,0:T(4,128)S(1)} %broadcast_in_dim.13), channel_id=1, replica_groups=mesh['gx'=8,'gy'=4,'gz'=8] {'gx'}, dimensions={0} | all-to-all | bytes 98304 | tf_op jit(solution)/shard_map/all_to_all | solution.py:20
  105.8 13.3 %all_to_all.37 = f32[32,4,384]{2,1,0:T(4,128)S(1)} all-to-all(f32[32,4,384]{2,1,0:T(4,128)S(1)} %broadcast_in_dim.14), channel_id=1, replica_groups=mesh['gx'=8,'gy'=4,'gz'=8] {'gy','gz'}, dimensions={0} | all-to-all | bytes 393216 | tf_op jit(solution)/shard_map/all_to_all | solution.py:20
  119.1 1.2 fusion.66
  120.4 1.2 fusion.67
  121.7 0.2 convolution_subtract_fusion.8
  121.9 10.9 %all_to_all.38 = f32[32,4,30]{2,1,0:T(4,128)S(1)} all-to-all(f32[32,4,30]{2,1,0:T(4,128)S(1)} %broadcast_in_dim.15), channel_id=1, replica_groups=mesh['gx'=8,'gy'=4,'gz'=8] {'gy','gz'}, dimensions={0} | all-to-all | bytes 30720 | tf_op jit(solution)/shard_map/all_to_all | solution.py:20
  132.9 0.2 fusion.62
  133.1 0.2 fusion.68
  133.3 0.2 convolution_subtract_fusion.7
  133.6 0.2 convolution_subtract_fusion.6
  133.8 7.4 %all_to_all.39 = f32[8,4,25]{2,1,0:T(4,128)S(1)} all-to-all(f32[8,4,25]{2,1,0:T(4,128)S(1)} %broadcast_in_dim.16), channel_id=1, replica_groups=mesh['gx'=8,'gy'=4,'gz'=8] {'gz'}, dimensions={0} | all-to-all | bytes 6400 | tf_op jit(solution)/shard_map/all_to_all | solution.py:20
  141.6 0.2 convolution_subtract_fusion.5
  141.8 0.2 convolution_subtract_fusion.4
  142.0 0.2 convolution_subtract_fusion.3
  142.2 0.2 fusion.4
  142.4 0.3 fusion
  142.7 0.2 copy.47
  143.0 1.3 collective-permute-start.9
  144.4 2.9 %collective-permute-done.9 = f32[1,6,24]{2,1,0:T(8,128)S(1)} collective-permute-done((f32[1,6,24]{2,1,0:T(8,128)S(1)}, f32[1,6,24]{2,1,0:T(8,128)S(1)}, u32[]{:S(2)}, u32[]{:S(2)}) %collective-permute-start.9) | collective-permute-done | bytes 608 | tf_op jit(solution)/shard_map/ppermute | solution.py:16
  147.4 1.3 collective-permute-start.10
  148.7 3.0 %collective-permute-done.10 = f32[7,1,24]{2,1,0:T(1,128)S(1)} collective-permute-done((f32[7,1,24]{2,1,0:T(1,128)S(1)}, f32[7,1,24]{2,1,0:T(1,128)S(1)}, u32[]{:S(2)}, u32[]{:S(2)}) %collective-permute-start.10) | collective-permute-done | bytes 704 | tf_op jit(solution)/shard_map/ppermute | solution.py:16
  151.7 4.9 %collective-permute-start.11 = (f32[7,7,4]{2,1,0:T(8,128)S(1)}, f32[7,7,4]{2,1,0:T(8,128)S(1)}, u32[]{:S(2)}, u32[]{:S(2)}) collective-permute-start(f32[7,7,4]{2,1,0:T(8,128)S(1)} %pad_maximum_fusion), channel_id=1, source_target_pairs={{1,0},{2,1},{3,2},{4,3},{5,4},{6,5},{7,6},{9,8},{10,9},{11,10},{12... | collective-permute-start | bytes 2360 | tf_op jit(solution)/shard_map/ppermute | solution.py:16
  156.7 1.7 %collective-permute-done.11 = f32[7,7,4]{2,1,0:T(8,128)S(1)} collective-permute-done((f32[7,7,4]{2,1,0:T(8,128)S(1)}, f32[7,7,4]{2,1,0:T(8,128)S(1)}, u32[]{:S(2)}, u32[]{:S(2)}) %collective-permute-start.11) | collective-permute-done | bytes 816 | tf_op jit(solution)/shard_map/ppermute | solution.py:16
  158.4 0.7 select_maximum_fusion.window
  159.1 2.6 %prolong_twice.1 = f32[4,24,24,24]{3,2,1,0:T(8,128)} custom-call(f32[7,8,32]{2,1,0:T(8,128)} %select_maximum_fusion.window, f32[168,56]{1,0:T(8,128)} %constant.39.clone.y_weights, f32[4,32,24]{2,1,0:T(8,128)} %constant.40.clone.z_weights), custom_call_target="tpu_custom_call" | custom-call | tf_op jit(solution)/shard_map/prolong_twice/pallas_call | solution.py:182
  (73 shorter events, 2.0 us)
Async XLA Ops:
  0.0 45.3 %copy-start = (f32[1,1,1,125,72]{3,4,2,1,0:T(8,128)S(1)}, f32[1,1,1,125,72]{3,4,2,1,0:T(8,128)}, u32[]{:S(2)}) copy-start(f32[1,1,1,125,72]{3,4,2,1,0:T(8,128)} %param.29) | copy-start | bytes 108004
  0.7 30.0 %copy-start.3 = (f32[1,1,25,200]{3,1,2,0:T(1,128)S(1)}, f32[1,1,25,200]{3,1,2,0:T(1,128)}, u32[]{:S(2)}) copy-start(f32[1,1,25,200]{3,1,2,0:T(1,128)} %param.30) | copy-start | bytes 60004
  0.7 34.2 %copy-start.2 = (f32[1,30,960]{2,0,1:T(1,128)S(1)}, f32[1,30,960]{2,0,1:T(1,128)}, u32[]{:S(2)}) copy-start(f32[1,30,960]{2,0,1:T(1,128)} %param.33) | copy-start | bytes 345604
  0.7 38.1 %copy-start.1 = (f32[36,9216]{1,0:T(8,128)S(1)}, f32[36,9216]{1,0:T(8,128)}, u32[]{:S(2)}) copy-start(f32[36,9216]{1,0:T(8,128)} %param.35) | copy-start | bytes 3981316
  0.7 44.3 %copy-start.4 = (f32[1,1,1,125,125]{4,2,3,1,0:T(1,128)S(1)}, f32[1,1,1,125,125]{4,2,3,1,0:T(1,128)}, u32[]{:S(2)}) copy-start(f32[1,1,1,125,125]{4,2,3,1,0:T(1,128)} %param.26) | copy-start | bytes 187504
  0.7 44.5 %copy-start.9 = (f32[1,1,1,125,50]{3,2,4,1,0:T(1,128)S(1)}, f32[1,1,1,125,50]{3,2,4,1,0:T(1,128)}, u32[]{:S(2)}) copy-start(f32[1,1,1,125,50]{3,2,4,1,0:T(1,128)} %param.27) | copy-start | bytes 75004
  0.7 50.1 %copy-start.5 = (f32[1,1,1,125,60]{3,2,4,1,0:T(1,128)S(1)}, f32[1,1,1,125,60]{3,2,4,1,0:T(1,128)}, u32[]{:S(2)}) copy-start(f32[1,1,1,125,60]{3,2,4,1,0:T(1,128)} %param.28) | copy-start | bytes 90004
  0.7 54.7 %copy-start.11 = (f32[1,1,1,25,60]{4,2,3,1,0:T(1,128)S(1)}, f32[1,1,1,25,60]{4,2,3,1,0:T(1,128)}, u32[]{:S(2)}) copy-start(f32[1,1,1,25,60]{4,2,3,1,0:T(1,128)} %param.31) | copy-start | bytes 18004
  5.1 5.7 %collective-permute-start = (f32[1,8,32]{2,1,0:T(8,128)S(1)}, f32[1,8,32]{2,1,0:T(8,128)S(1)}, u32[]{:S(2)}, u32[]{:S(2)}) collective-permute-start(f32[1,8,32]{2,1,0:T(8,128)S(1)} %get-tuple-element.9), channel_id=1, source_target_pairs={{0,32},{32,64},{64,96},{96,128},{128,160},{160,192},{192,224},{1,3... | collective-permute-start | bytes 3080 | tf_op jit(solution)/shard_map/ppermute | solution.py:16
  9.4 4.5 %collective-permute-start.1 = (f32[1,8,32]{2,1,0:T(8,128)S(1)}, f32[1,8,32]{2,1,0:T(8,128)S(1)}, u32[]{:S(2)}, u32[]{:S(2)}) collective-permute-start(f32[1,8,32]{2,1,0:T(8,128)S(1)} %get-tuple-element.10), channel_id=1, source_target_pairs={{32,0},{64,32},{96,64},{128,96},{160,128},{192,160},{224,192},{33,... | collective-permute-start | bytes 3080 | tf_op jit(solution)/shard_map/ppermute | solution.py:16
  14.7 4.5 %collective-permute-start.2 = (f32[6,1,32]{2,1,0:T(1,128)S(1)}, f32[6,1,32]{2,1,0:T(1,128)S(1)}, u32[]{:S(2)}, u32[]{:S(2)}) collective-permute-start(f32[6,1,32]{2,1,0:T(1,128)S(1)} %get-tuple-element.13), channel_id=1, source_target_pairs={{0,8},{8,16},{16,24},{1,9},{9,17},{17,25},{2,10},{10,18},{18,26},{... | collective-permute-start | bytes 2312 | tf_op jit(solution)/shard_map/ppermute | solution.py:16
  17.9 4.3 %collective-permute-start.3 = (f32[6,1,32]{2,1,0:T(1,128)S(1)}, f32[6,1,32]{2,1,0:T(1,128)S(1)}, u32[]{:S(2)}, u32[]{:S(2)}) collective-permute-start(f32[6,1,32]{2,1,0:T(1,128)S(1)} %get-tuple-element.14), channel_id=1, source_target_pairs={{8,0},{16,8},{24,16},{9,1},{17,9},{25,17},{10,2},{18,10},{26,18},{... | collective-permute-start | bytes 2312 | tf_op jit(solution)/shard_map/ppermute | solution.py:16
  22.4 20.1 %collective-permute-start.4 = (f32[6,6,4]{2,1,0:T(8,128)S(1)}, f32[6,6,4]{2,1,0:T(8,128)S(1)}, u32[]{:S(2)}, u32[]{:S(2)}) collective-permute-start(f32[6,6,4]{2,1,0:T(8,128)S(1)} %get-tuple-element.11), channel_id=1, source_target_pairs={{0,1},{1,2},{2,3},{3,4},{4,5},{5,6},{6,7},{8,9},{9,10},{10,11},{11... | collective-permute-start | bytes 1736 | tf_op jit(solution)/shard_map/ppermute | solution.py:16
  28.7 13.8 %collective-permute-start.5 = (f32[6,6,4]{2,1,0:T(8,128)S(1)}, f32[6,6,4]{2,1,0:T(8,128)S(1)}, u32[]{:S(2)}, u32[]{:S(2)}) collective-permute-start(f32[6,6,4]{2,1,0:T(8,128)S(1)} %get-tuple-element.12), channel_id=1, source_target_pairs={{1,0},{2,1},{3,2},{4,3},{5,4},{6,5},{7,6},{9,8},{10,9},{11,10},{12... | collective-permute-start | bytes 1736 | tf_op jit(solution)/shard_map/ppermute | solution.py:16
  31.3 14.4 %collective-permute-start.6 = (f32[25,200]{1,0:T(8,128)}, f32[25,200]{1,0:T(8,128)S(1)}, u32[]{:S(2)}, u32[]{:S(2)}) collective-permute-start(f32[25,200]{1,0:T(8,128)} %bitcast.81), channel_id=1, source_target_pairs={{0,1},{1,2},{2,3},{3,4},{4,5},{5,6},{6,7},{8,9},{9,10},{10,11},{11... | collective-permute-start | bytes 60008 | tf_op jit(solution)/shard_map/ppermute | solution.py:16
  35.6 20.9 %collective-permute-start.7 = (f32[30,960]{1,0:T(8,128)}, f32[30,960]{1,0:T(8,128)S(1)}, u32[]{:S(2)}, u32[]{:S(2)}) collective-permute-start(f32[30,960]{1,0:T(8,128)} %bitcast.80), channel_id=1, source_target_pairs={{0,8},{8,16},{16,24},{1,9},{9,17},{17,25},{2,10},{10,18},{18,26},{... | collective-permute-start | bytes 345608 | tf_op jit(solution)/shard_map/ppermute | solution.py:16
  38.8 35.2 %collective-permute-start.8 = (f32[36,9216]{1,0:T(8,128)S(1)}, f32[36,9216]{1,0:T(8,128)S(1)}, u32[]{:S(2)}, u32[]{:S(2)}) collective-permute-start(f32[36,9216]{1,0:T(8,128)S(1)} %copy-done.1), channel_id=1, source_target_pairs={{0,32},{32,64},{64,96},{96,128},{128,160},{160,192},{192,224},{1,3... | collective-permute-start | bytes 3981320 | tf_op jit(solution)/shard_map/ppermute | solution.py:16
  44.9 0.8 copy-start.14
  45.7 29.1 %copy-start.7 = (f32[25,200]{1,0:T(8,128)}, f32[25,200]{1,0:T(8,128)S(1)}, u32[]{:S(2)}) copy-start(f32[25,200]{1,0:T(8,128)S(1)} %collective-permute-done.6) | copy-start | bytes 60004
  46.6 8.8 %all-to-all-start = ((f32[8,4,25]{2,1,0:T(4,128)}), f32[8,4,25]{2,1,0:T(4,128)S(1)}, u32[]{:S(2)}, u32[]{:S(2)}) async-start(f32[8,4,25]{2,1,0:T(4,128)} %bitcast.82), calls=%async_computation | async-start | bytes 32768 | tf_op jit(solution)/shard_map/all_to_all | solution.py:20
  57.5 11.7 %all-to-all-start.1 = ((f32[32,4,30]{2,1,0:T(4,128)}), f32[32,4,30]{2,1,0:T(4,128)S(1)}, u32[]{:S(2)}, u32[]{:S(2)}) async-start(f32[32,4,30]{2,1,0:T(4,128)} %copy.42), calls=%async_computation.1 | async-start | bytes 131072 | tf_op jit(solution)/shard_map/all_to_all | solution.py:20
  69.2 5.6 %copy-start.15 = (f32[4,30]{1,0:T(4,128)}, f32[4,30]{1,0:T(4,128)S(1)}, u32[]{:S(2)}) copy-start(f32[4,30]{1,0:T(4,128)S(1)} %reduce_sum.37) | copy-start | bytes 1444
  119.1 2.6 %copy-start.13 = (f32[1,1,1,30,72]{4,2,3,1,0:T(1,128)S(1)}, f32[1,1,1,30,72]{4,2,3,1,0:T(1,128)}, u32[]{:S(2)}) copy-start(f32[1,1,1,30,72]{4,2,3,1,0:T(1,128)} %param.34) | copy-start | bytes 25924
  119.1 2.6 %copy-start.16 = (f32[4,30]{1,0:T(4,128)S(1)}, f32[4,30]{1,0:T(4,128)}, u32[]{:S(2)}) copy-start(f32[4,30]{1,0:T(4,128)} %copy-done.15) | copy-start | bytes 1444
  120.4 13.2 %copy-start.12 = (f32[1,1,1,25,72]{4,2,3,1,0:T(1,128)S(1)}, f32[1,1,1,25,72]{4,2,3,1,0:T(1,128)}, u32[]{:S(2)}) copy-start(f32[1,1,1,25,72]{4,2,3,1,0:T(1,128)} %param.32) | copy-start | bytes 21604
  120.4 21.1 %copy-start.8 = (f32[25,200]{1,0:T(8,128)S(1)}, f32[25,200]{1,0:T(8,128)}, u32[]{:S(2)}) copy-start(f32[25,200]{1,0:T(8,128)} %copy-done.7) | copy-start | bytes 60004
  120.4 21.2 %copy-start.10 = (f32[1,1,1,125,50]{3,2,4,1,0:T(1,128)S(1)}, f32[1,1,1,125,50]{3,2,4,1,0:T(1,128)}, u32[]{:S(2)}) copy-start(f32[1,1,1,125,50]{3,2,4,1,0:T(1,128)} %param.27) | copy-start | bytes 75004
  120.4 21.4 %copy-start.6 = (f32[1,1,1,125,60]{3,2,4,1,0:T(1,128)S(1)}, f32[1,1,1,125,60]{3,2,4,1,0:T(1,128)}, u32[]{:S(2)}) copy-start(f32[1,1,1,125,60]{3,2,4,1,0:T(1,128)} %param.28) | copy-start | bytes 90004
  120.4 22.0 %copy-start.17 = (s32[1,1,1,216]{3,2,1,0:T(1,128)S(1)}, s32[1,1,1,216]{3,2,1,0:T(1,128)}, u32[]{:S(2)}) copy-start(s32[1,1,1,216]{3,2,1,0:T(1,128)} %param.25) | copy-start | bytes 2596
  143.0 4.3 %collective-permute-start.9 = (f32[1,6,24]{2,1,0:T(8,128)S(1)}, f32[1,6,24]{2,1,0:T(8,128)S(1)}, u32[]{:S(2)}, u32[]{:S(2)}) collective-permute-start(f32[1,6,24]{2,1,0:T(8,128)S(1)} %slice.93), channel_id=1, source_target_pairs={{32,0},{64,32},{96,64},{128,96},{160,128},{192,160},{224,192},{33,... | collective-permute-start | bytes 1736 | tf_op jit(solution)/shard_map/ppermute | solution.py:16
  147.4 4.3 %collective-permute-start.10 = (f32[7,1,24]{2,1,0:T(1,128)S(1)}, f32[7,1,24]{2,1,0:T(1,128)S(1)}, u32[]{:S(2)}, u32[]{:S(2)}) collective-permute-start(f32[7,1,24]{2,1,0:T(1,128)S(1)} %slice.108), channel_id=1, source_target_pairs={{8,0},{16,8},{24,16},{9,1},{17,9},{25,17},{10,2},{18,10},{26,18},{... | collective-permute-start | bytes 2024 | tf_op jit(solution)/shard_map/ppermute | solution.py:16
  151.7 6.6 %collective-permute-start.11 = (f32[7,7,4]{2,1,0:T(8,128)S(1)}, f32[7,7,4]{2,1,0:T(8,128)S(1)}, u32[]{:S(2)}, u32[]{:S(2)}) collective-permute-start(f32[7,7,4]{2,1,0:T(8,128)S(1)} %pad_maximum_fusion), channel_id=1, source_target_pairs={{1,0},{2,1},{3,2},{4,3},{5,4},{6,5},{7,6},{9,8},{10,9},{11,10},{12... | collective-permute-start | bytes 2360 | tf_op jit(solution)/shard_map/ppermute | solution.py:16

commit v2 on v1

--- a/solution.py
+++ b/solution.py
@@ -244,15 +244,14 @@
     second_to_top = second_top[0, 0, 0]
     leaf_block = leaf_inverse[0, 0, 0]
 
+    top_below = shifted(top_inverse, "gx", 1)
+    first_below = shifted(first_rows, "gz", 1)
+    second_below = shifted(second_rows, "gy", 1)
     edge = jnp.stack([lax.axis_index(a) == 0 for a in ("gx", "gy", "gz")]).astype(jnp.float32)
     partial = restricted(edge, right_side, iterate, coefficient)
-    coarse = with_neighbours(partial, "gx", 0, 1)
-    first_below = shifted(first_rows, "gz", 1)
-    second_below = shifted(second_rows, "gy", 1)
-    top_rows, coarse = lax.optimization_barrier((top_inverse, coarse))
-    top_below = shifted(top_rows, "gx", 1)
+    coarse = with_neighbours(partial, "gz", 2, count)
     coarse = with_neighbours(coarse, "gy", 1, 1)
-    coarse = with_neighbours(coarse, "gz", 2, count)
+    coarse = with_neighbours(coarse, "gx", 0, 1)
     natural = coarse.reshape(cells, count).T
 
     chosen_at = ordering.reshape(-1)[:, None] == jnp.arange(cells, dtype=jnp.int32)[None, :]

time: 163 us -> 164 us (level)
  waiting for transfers between devices: 27.3 us -> 30.5 us
  starting transfers between devices: 44.8 us -> 42.9 us
  blocking collectives: 61.1 us -> 62.8 us
    ppermute x12, waiting for transfers between devices: 16.3 us -> 19.5 us  [shifted(): return lax.ppermute(shard, axis, pairs)]
    ppermute x12, starting transfers between devices: 36.3 us -> 34.4 us  [shifted(): return lax.ppermute(shard, axis, pairs)]
    all_to_all x5, blocking collectives: 61.1 us -> 62.8 us  [exchanged(): return lax.all_to_all(pieces, axis, split_axis=0, concat_axis=0, tiled=True)]
  transfers between devices with their start and end apart: 14 -> 14, of which waited for: 8 -> 8; matrix products, arithmetic and copies ran while one was open for 7% -> 5% of each run, Pallas kernels for 0% -> 0%
where the time goes in v2:
time: 164 us; the launch traced here: 163 us
  blocking collectives  62.8 us (38%)
  starting transfers between devices  42.9 us (26%)
  waiting for transfers between devices  30.5 us (19%)
  matrix products  11.8 us (7%)
  Pallas kernels  6.3 us (4%)
  local copies, waits for them, and re-layouts  5.32 us (3%)
  other arithmetic  2.95 us (2%)
    all_to_all x5, blocking collectives, exchanged(): return lax.all_to_all(pieces, axis, split_axis=0, concat_axis=0, tiled=True)  62.8 us
    ppermute x12, starting transfers between devices, shifted(): return lax.ppermute(shard, axis, pairs)  34.4 us
    ppermute x12, waiting for transfers between devices, shifted(): return lax.ppermute(shard, axis, pairs)  19.5 us
    all_to_all x2, waiting for transfers between devices, exchanged(): return lax.all_to_all(pieces, axis, split_axis=0, concat_axis=0, tiled=True)  11 us
    all_to_all x2, starting transfers between devices, exchanged(): return lax.all_to_all(pieces, axis, split_axis=0, concat_axis=0, tiled=True)  8.47 us
    dot_general x14, matrix products, product(): jnp.dot(operand, matrix, precision=precise, preferred_element_type=jnp.fl...  6.15 us
    dot_general x14, matrix products, product_back(): lax.dot_general(operand, matrix, (((1,), (1,)), ((), ())), precision=prec...  5.68 us
    pallas_call x1, Pallas kernels, restricted(): pl.pallas_call(body, out_shape=jax.ShapeDtypeStruct((coarse, coarse, coar...  3.66 us
  transfers between devices with their start and end apart: 14, of which 8 were waited for; matrix products, arithmetic and copies ran while one was open for 5% of the time, Pallas kernels for 0%

profile of v2, /device:TPU:1, one launch (start us, length us, event | category | flops | bytes accessed | tf_op | source)
XLA Modules:
  0.0 163.0 jit_solution(1492670954104775937)
XLA Ops:
  0.0 0.7 add_convert_fusion.refs_0_
  0.7 3.7 %restrict_twice.1 = f32[8,8,32]{2,1,0:T(8,128)} custom-call(f32[3]{0:T(128)} %add_convert_fusion.refs_0_, f32[4,24,24,24]{3,2,1,0:T(8,128)} %refs_1_.1, f32[4,24,24,24]{3,2,1,0:T(8,128)} %refs_2_.1, f32[24,24,24]{2,1,0:T(8,128)} %refs_3_.1, f32[4,24,32]{2,1,0:T(8,128)} %constant.33.clone.refs_4_, f32[4,24,32]{2,1,0:T(8,128)} %constant.34.clone.refs_5_, ...), custom_call_target="tpu_custom_call" | custom-call | tf_op jit(solution)/shard_map/restrict_twice/pallas_call | solution.py:146
  4.4 0.9 fusion.66
  5.3 4.5 %collective-permute-start = (f32[8,8,4]{2,1,0:T(8,128)S(1)}, f32[8,8,4]{2,1,0:T(8,128)S(1)}, u32[]{:S(2)}, u32[]{:S(2)}) collective-permute-start(f32[8,8,4]{2,1,0:T(8,128)S(1)} %get-tuple-element.9), channel_id=1, source_target_pairs={{0,1},{1,2},{2,3},{3,4},{4,5},{5,6},{6,7},{8,9},{9,10},{10,11},{11... | collective-permute-start | bytes 3080 | tf_op jit(solution)/shard_map/ppermute | solution.py:16
  9.8 1.9 %collective-permute-start.1 = (f32[8,8,4]{2,1,0:T(8,128)S(1)}, f32[8,8,4]{2,1,0:T(8,128)S(1)}, u32[]{:S(2)}, u32[]{:S(2)}) collective-permute-start(f32[8,8,4]{2,1,0:T(8,128)S(1)} %get-tuple-element.10), channel_id=1, source_target_pairs={{1,0},{2,1},{3,2},{4,3},{5,4},{6,5},{7,6},{9,8},{10,9},{11,10},{12... | collective-permute-start | bytes 3080 | tf_op jit(solution)/shard_map/ppermute | solution.py:16
  11.7 3.3 %collective-permute-done.1 = f32[8,8,4]{2,1,0:T(8,128)S(1)} collective-permute-done((f32[8,8,4]{2,1,0:T(8,128)S(1)}, f32[8,8,4]{2,1,0:T(8,128)S(1)}, u32[]{:S(2)}, u32[]{:S(2)}) %collective-permute-start.1) | collective-permute-done | bytes 1056 | tf_op jit(solution)/shard_map/ppermute | solution.py:16
  15.0 0.8 fusion.14
  15.9 3.2 %collective-permute-start.2 = (f32[8,1,24]{2,1,0:T(1,128)S(1)}, f32[8,1,24]{2,1,0:T(1,128)S(1)}, u32[]{:S(2)}, u32[]{:S(2)}) collective-permute-start(f32[8,1,24]{2,1,0:T(1,128)S(1)} %get-tuple-element.7), channel_id=1, source_target_pairs={{0,8},{8,16},{16,24},{1,9},{9,17},{17,25},{2,10},{10,18},{18,26},{... | collective-permute-start | bytes 2312 | tf_op jit(solution)/shard_map/ppermute | solution.py:16
  19.1 1.3 collective-permute-start.3
  20.4 3.0 %collective-permute-done.3 = f32[8,1,24]{2,1,0:T(1,128)S(1)} collective-permute-done((f32[8,1,24]{2,1,0:T(1,128)S(1)}, f32[8,1,24]{2,1,0:T(1,128)S(1)}, u32[]{:S(2)}, u32[]{:S(2)}) %collective-permute-start.3) | collective-permute-done | bytes 800 | tf_op jit(solution)/shard_map/ppermute | solution.py:16
  23.5 3.5 %collective-permute-start.4 = (f32[1,6,24]{2,1,0:T(8,128)S(1)}, f32[1,6,24]{2,1,0:T(8,128)S(1)}, u32[]{:S(2)}, u32[]{:S(2)}) collective-permute-start(f32[1,6,24]{2,1,0:T(8,128)S(1)} %get-tuple-element.5), channel_id=1, source_target_pairs={{0,32},{32,64},{64,96},{96,128},{128,160},{160,192},{192,224},{1,3... | collective-permute-start | bytes 1736 | tf_op jit(solution)/shard_map/ppermute | solution.py:16
  27.0 1.3 collective-permute-start.5
  28.3 0.6 copy.114
  28.9 3.6 %collective-permute-start.6 = (f32[25,200]{1,0:T(8,128)}, f32[25,200]{1,0:T(8,128)}, u32[]{:S(2)}, u32[]{:S(2)}) collective-permute-start(f32[25,200]{1,0:T(8,128)} %bitcast.81), channel_id=1, source_target_pairs={{0,1},{1,2},{2,3},{3,4},{4,5},{5,6},{6,7},{8,9},{9,10},{10,11},{11... | collective-permute-start | bytes 60008 | tf_op jit(solution)/shard_map/ppermute | solution.py:16
  32.6 0.7 copy.113
  33.3 3.2 %collective-permute-start.7 = (f32[30,960]{1,0:T(8,128)}, f32[30,960]{1,0:T(8,128)S(1)}, u32[]{:S(2)}, u32[]{:S(2)}) collective-permute-start(f32[30,960]{1,0:T(8,128)} %bitcast.80), channel_id=1, source_target_pairs={{0,8},{8,16},{16,24},{1,9},{9,17},{17,25},{2,10},{10,18},{18,26},{... | collective-permute-start | bytes 345608 | tf_op jit(solution)/shard_map/ppermute | solution.py:16
  36.5 4.4 %collective-permute-start.8 = (f32[36,9216]{1,0:T(8,128)S(1)}, f32[36,9216]{1,0:T(8,128)S(1)}, u32[]{:S(2)}, u32[]{:S(2)}) collective-permute-start(f32[36,9216]{1,0:T(8,128)S(1)} %copy-done.1), channel_id=1, source_target_pairs={{0,32},{32,64},{64,96},{96,128},{128,160},{160,192},{192,224},{1,3... | collective-permute-start | bytes 3981320 | tf_op jit(solution)/shard_map/ppermute | solution.py:16
  41.0 0.3 fusion.1
  41.3 0.2 fusion.6
  41.6 0.2 fusion.11
  41.8 0.2 fusion.46
  42.0 1.0 convolution_subtract_fusion.2
  43.1 0.6 copy.115
  43.7 4.1 %all-to-all-start = ((f32[8,4,25]{2,1,0:T(4,128)}), f32[8,4,25]{2,1,0:T(4,128)S(1)}, u32[]{:S(2)}, u32[]{:S(2)}) async-start(f32[8,4,25]{2,1,0:T(4,128)} %bitcast.82), calls=%async_computation | async-start | bytes 32768 | tf_op jit(solution)/shard_map/all_to_all | solution.py:20
  47.9 4.5 %all-to-all-done = f32[8,4,25]{2,1,0:T(4,128)S(1)} async-done(((f32[8,4,25]{2,1,0:T(4,128)}), f32[8,4,25]{2,1,0:T(4,128)S(1)}, u32[]{:S(2)}, u32[]{:S(2)}) %all-to-all-start) | async-done | bytes 3232 | tf_op jit(solution)/shard_map/all_to_all | solution.py:20
  52.6 0.2 fusion.48
  52.9 0.2 convolution_subtract_fusion.1
  53.2 0.7 copy.42
  53.9 4.4 %all-to-all-start.1 = ((f32[32,4,30]{2,1,0:T(4,128)}), f32[32,4,30]{2,1,0:T(4,128)S(1)}, u32[]{:S(2)}, u32[]{:S(2)}) async-start(f32[32,4,30]{2,1,0:T(4,128)} %copy.42), calls=%async_computation.1 | async-start | bytes 131072 | tf_op jit(solution)/shard_map/all_to_all | solution.py:20
  58.3 0.8 convolution_add_fusion.1
  59.1 6.5 %all-to-all-done.1 = f32[32,4,30]{2,1,0:T(4,128)S(1)} async-done(((f32[32,4,30]{2,1,0:T(4,128)}), f32[32,4,30]{2,1,0:T(4,128)S(1)}, u32[]{:S(2)}, u32[]{:S(2)}) %all-to-all-start.1) | async-done | bytes 15392 | tf_op jit(solution)/shard_map/all_to_all | solution.py:20
  65.6 0.8 convolution_add_fusion
  66.5 0.9 fusion.47
  67.4 5.4 %collective-permute-done.8 = f32[36,9216]{1,0:T(8,128)S(1)} collective-permute-done((f32[36,9216]{1,0:T(8,128)S(1)}, f32[36,9216]{1,0:T(8,128)S(1)}, u32[]{:S(2)}, u32[]{:S(2)}) %collective-permute-start.8) | collective-permute-done | bytes 1327136 | tf_op jit(solution)/shard_map/ppermute | solution.py:16
  72.8 0.9 convolution_subtract_fusion
  73.7 13.2 %all_to_all.35 = f32[32,4,384]{2,1,0:T(4,128)S(1)} all-to-all(f32[32,4,384]{2,1,0:T(4,128)S(1)} %pad.38), channel_id=1, replica_groups=mesh['gx'=8,'gy'=4,'gz'=8] {'gy','gz'}, dimensions={0} | all-to-all | bytes 393216 | tf_op jit(solution)/shard_map/all_to_all | solution.py:20
  87.0 0.6 reduce_sum.38
  87.6 0.7 broadcast_in_dim.13
  88.3 18.0 %all_to_all.36 = f32[8,4,384]{2,1,0:T(4,128)S(1)} all-to-all(f32[8,4,384]{2,1,0:T(4,128)S(1)} %broadcast_in_dim.13), channel_id=1, replica_groups=mesh['gx'=8,'gy'=4,'gz'=8] {'gx'}, dimensions={0} | all-to-all | bytes 98304 | tf_op jit(solution)/shard_map/all_to_all | solution.py:20
  106.4 13.3 %all_to_all.37 = f32[32,4,384]{2,1,0:T(4,128)S(1)} all-to-all(f32[32,4,384]{2,1,0:T(4,128)S(1)} %broadcast_in_dim.14), channel_id=1, replica_groups=mesh['gx'=8,'gy'=4,'gz'=8] {'gy','gz'}, dimensions={0} | all-to-all | bytes 393216 | tf_op jit(solution)/shard_map/all_to_all | solution.py:20
  119.7 1.2 fusion.67
  121.0 1.2 fusion.68
  122.2 0.2 convolution_subtract_fusion.8
  122.5 10.9 %all_to_all.38 = f32[32,4,30]{2,1,0:T(4,128)S(1)} all-to-all(f32[32,4,30]{2,1,0:T(4,128)S(1)} %broadcast_in_dim.15), channel_id=1, replica_groups=mesh['gx'=8,'gy'=4,'gz'=8] {'gy','gz'}, dimensions={0} | all-to-all | bytes 30720 | tf_op jit(solution)/shard_map/all_to_all | solution.py:20
  133.5 0.2 fusion.63
  133.7 0.2 fusion.69
  133.9 0.2 convolution_subtract_fusion.7
  134.2 0.2 convolution_subtract_fusion.6
  134.4 7.4 %all_to_all.39 = f32[8,4,25]{2,1,0:T(4,128)S(1)} all-to-all(f32[8,4,25]{2,1,0:T(4,128)S(1)} %broadcast_in_dim.16), channel_id=1, replica_groups=mesh['gx'=8,'gy'=4,'gz'=8] {'gz'}, dimensions={0} | all-to-all | bytes 6400 | tf_op jit(solution)/shard_map/all_to_all | solution.py:20
  142.0 0.9 fusion.70
  142.9 0.2 convolution_subtract_fusion.5
  143.1 0.2 convolution_subtract_fusion.4
  143.3 0.2 convolution_subtract_fusion.3
  143.6 0.2 fusion.4
  143.7 0.3 fusion
  144.0 0.2 copy.47
  144.4 1.3 collective-permute-start.9
  145.8 2.9 %collective-permute-done.9 = f32[1,6,24]{2,1,0:T(8,128)S(1)} collective-permute-done((f32[1,6,24]{2,1,0:T(8,128)S(1)}, f32[1,6,24]{2,1,0:T(8,128)S(1)}, u32[]{:S(2)}, u32[]{:S(2)}) %collective-permute-start.9) | collective-permute-done | bytes 608 | tf_op jit(solution)/shard_map/ppermute | solution.py:16
  148.7 1.3 collective-permute-start.10
  150.0 3.0 %collective-permute-done.10 = f32[7,1,24]{2,1,0:T(1,128)S(1)} collective-permute-done((f32[7,1,24]{2,1,0:T(1,128)S(1)}, f32[7,1,24]{2,1,0:T(1,128)S(1)}, u32[]{:S(2)}, u32[]{:S(2)}) %collective-permute-start.10) | collective-permute-done | bytes 704 | tf_op jit(solution)/shard_map/ppermute | solution.py:16
  153.1 4.9 %collective-permute-start.11 = (f32[7,7,4]{2,1,0:T(8,128)S(1)}, f32[7,7,4]{2,1,0:T(8,128)S(1)}, u32[]{:S(2)}, u32[]{:S(2)}) collective-permute-start(f32[7,7,4]{2,1,0:T(8,128)S(1)} %pad_maximum_fusion), channel_id=1, source_target_pairs={{1,0},{2,1},{3,2},{4,3},{5,4},{6,5},{7,6},{9,8},{10,9},{11,10},{12... | collective-permute-start | bytes 2360 | tf_op jit(solution)/shard_map/ppermute | solution.py:16
  158.0 1.7 %collective-permute-done.11 = f32[7,7,4]{2,1,0:T(8,128)S(1)} collective-permute-done((f32[7,7,4]{2,1,0:T(8,128)S(1)}, f32[7,7,4]{2,1,0:T(8,128)S(1)}, u32[]{:S(2)}, u32[]{:S(2)}) %collective-permute-start.11) | collective-permute-done | bytes 816 | tf_op jit(solution)/shard_map/ppermute | solution.py:16
  159.7 0.7 select_maximum_fusion.window
  160.4 2.6 %prolong_twice.1 = f32[4,24,24,24]{3,2,1,0:T(8,128)} custom-call(f32[7,8,32]{2,1,0:T(8,128)} %select_maximum_fusion.window, f32[168,56]{1,0:T(8,128)} %constant.39.clone.y_weights, f32[4,32,24]{2,1,0:T(8,128)} %constant.40.clone.z_weights), custom_call_target="tpu_custom_call" | custom-call | tf_op jit(solution)/shard_map/prolong_twice/pallas_call | solution.py:182
  (69 shorter events, 1.7 us)
Async XLA Ops:
  0.0 41.6 %copy-start = (f32[1,1,1,125,72]{3,4,2,1,0:T(8,128)S(1)}, f32[1,1,1,125,72]{3,4,2,1,0:T(8,128)}, u32[]{:S(2)}) copy-start(f32[1,1,1,125,72]{3,4,2,1,0:T(8,128)} %param.29) | copy-start | bytes 108004
  0.7 27.7 %copy-start.3 = (f32[1,1,25,200]{3,1,2,0:T(1,128)S(1)}, f32[1,1,25,200]{3,1,2,0:T(1,128)}, u32[]{:S(2)}) copy-start(f32[1,1,25,200]{3,1,2,0:T(1,128)} %param.30) | copy-start | bytes 60004
  0.7 31.9 %copy-start.2 = (f32[1,30,960]{2,0,1:T(1,128)S(1)}, f32[1,30,960]{2,0,1:T(1,128)}, u32[]{:S(2)}) copy-start(f32[1,30,960]{2,0,1:T(1,128)} %param.33) | copy-start | bytes 345604
  0.7 35.8 %copy-start.1 = (f32[36,9216]{1,0:T(8,128)S(1)}, f32[36,9216]{1,0:T(8,128)}, u32[]{:S(2)}) copy-start(f32[36,9216]{1,0:T(8,128)} %param.35) | copy-start | bytes 3981316
  0.7 40.3 %copy-start.14 = (s32[1,1,1,216]{3,2,1,0:T(1,128)S(1)}, s32[1,1,1,216]{3,2,1,0:T(1,128)}, u32[]{:S(2)}) copy-start(s32[1,1,1,216]{3,2,1,0:T(1,128)} %param.25) | copy-start | bytes 2596
  0.7 40.6 %copy-start.4 = (f32[1,1,1,125,125]{4,2,3,1,0:T(1,128)S(1)}, f32[1,1,1,125,125]{4,2,3,1,0:T(1,128)}, u32[]{:S(2)}) copy-start(f32[1,1,1,125,125]{4,2,3,1,0:T(1,128)} %param.26) | copy-start | bytes 187504
  0.7 40.7 %copy-start.7 = (f32[1,1,1,125,50]{3,2,4,1,0:T(1,128)S(1)}, f32[1,1,1,125,50]{3,2,4,1,0:T(1,128)}, u32[]{:S(2)}) copy-start(f32[1,1,1,125,50]{3,2,4,1,0:T(1,128)} %param.27) | copy-start | bytes 75004
  0.7 47.1 %copy-start.5 = (f32[1,1,1,125,60]{3,2,4,1,0:T(1,128)S(1)}, f32[1,1,1,125,60]{3,2,4,1,0:T(1,128)}, u32[]{:S(2)}) copy-start(f32[1,1,1,125,60]{3,2,4,1,0:T(1,128)} %param.28) | copy-start | bytes 90004
  0.7 51.8 %copy-start.9 = (f32[1,1,1,25,60]{4,2,3,1,0:T(1,128)S(1)}, f32[1,1,1,25,60]{4,2,3,1,0:T(1,128)}, u32[]{:S(2)}) copy-start(f32[1,1,1,25,60]{4,2,3,1,0:T(1,128)} %param.31) | copy-start | bytes 18004
  5.3 6.4 %collective-permute-start = (f32[8,8,4]{2,1,0:T(8,128)S(1)}, f32[8,8,4]{2,1,0:T(8,128)S(1)}, u32[]{:S(2)}, u32[]{:S(2)}) collective-permute-start(f32[8,8,4]{2,1,0:T(8,128)S(1)} %get-tuple-element.9), channel_id=1, source_target_pairs={{0,1},{1,2},{2,3},{3,4},{4,5},{5,6},{6,7},{8,9},{9,10},{10,11},{11... | collective-permute-start | bytes 3080 | tf_op jit(solution)/shard_map/ppermute | solution.py:16
  9.8 5.2 %collective-permute-start.1 = (f32[8,8,4]{2,1,0:T(8,128)S(1)}, f32[8,8,4]{2,1,0:T(8,128)S(1)}, u32[]{:S(2)}, u32[]{:S(2)}) collective-permute-start(f32[8,8,4]{2,1,0:T(8,128)S(1)} %get-tuple-element.10), channel_id=1, source_target_pairs={{1,0},{2,1},{3,2},{4,3},{5,4},{6,5},{7,6},{9,8},{10,9},{11,10},{12... | collective-permute-start | bytes 3080 | tf_op jit(solution)/shard_map/ppermute | solution.py:16
  15.9 4.5 %collective-permute-start.2 = (f32[8,1,24]{2,1,0:T(1,128)S(1)}, f32[8,1,24]{2,1,0:T(1,128)S(1)}, u32[]{:S(2)}, u32[]{:S(2)}) collective-permute-start(f32[8,1,24]{2,1,0:T(1,128)S(1)} %get-tuple-element.7), channel_id=1, source_target_pairs={{0,8},{8,16},{16,24},{1,9},{9,17},{17,25},{2,10},{10,18},{18,26},{... | collective-permute-start | bytes 2312 | tf_op jit(solution)/shard_map/ppermute | solution.py:16
  19.1 4.4 %collective-permute-start.3 = (f32[8,1,24]{2,1,0:T(1,128)S(1)}, f32[8,1,24]{2,1,0:T(1,128)S(1)}, u32[]{:S(2)}, u32[]{:S(2)}) collective-permute-start(f32[8,1,24]{2,1,0:T(1,128)S(1)} %get-tuple-element.8), channel_id=1, source_target_pairs={{8,0},{16,8},{24,16},{9,1},{17,9},{25,17},{10,2},{18,10},{26,18},{... | collective-permute-start | bytes 2312 | tf_op jit(solution)/shard_map/ppermute | solution.py:16
  23.5 17.4 %collective-permute-start.4 = (f32[1,6,24]{2,1,0:T(8,128)S(1)}, f32[1,6,24]{2,1,0:T(8,128)S(1)}, u32[]{:S(2)}, u32[]{:S(2)}) collective-permute-start(f32[1,6,24]{2,1,0:T(8,128)S(1)} %get-tuple-element.5), channel_id=1, source_target_pairs={{0,32},{32,64},{64,96},{96,128},{128,160},{160,192},{192,224},{1,3... | collective-permute-start | bytes 1736 | tf_op jit(solution)/shard_map/ppermute | solution.py:16
  27.0 13.8 %collective-permute-start.5 = (f32[1,6,24]{2,1,0:T(8,128)S(1)}, f32[1,6,24]{2,1,0:T(8,128)S(1)}, u32[]{:S(2)}, u32[]{:S(2)}) collective-permute-start(f32[1,6,24]{2,1,0:T(8,128)S(1)} %get-tuple-element.6), channel_id=1, source_target_pairs={{32,0},{64,32},{96,64},{128,96},{160,128},{192,160},{224,192},{33,... | collective-permute-start | bytes 1736 | tf_op jit(solution)/shard_map/ppermute | solution.py:16
  28.9 13.1 %collective-permute-start.6 = (f32[25,200]{1,0:T(8,128)}, f32[25,200]{1,0:T(8,128)}, u32[]{:S(2)}, u32[]{:S(2)}) collective-permute-start(f32[25,200]{1,0:T(8,128)} %bitcast.81), channel_id=1, source_target_pairs={{0,1},{1,2},{2,3},{3,4},{4,5},{5,6},{6,7},{8,9},{9,10},{10,11},{11... | collective-permute-start | bytes 60008 | tf_op jit(solution)/shard_map/ppermute | solution.py:16
  33.3 19.6 %collective-permute-start.7 = (f32[30,960]{1,0:T(8,128)}, f32[30,960]{1,0:T(8,128)S(1)}, u32[]{:S(2)}, u32[]{:S(2)}) collective-permute-start(f32[30,960]{1,0:T(8,128)} %bitcast.80), channel_id=1, source_target_pairs={{0,8},{8,16},{16,24},{1,9},{9,17},{17,25},{2,10},{10,18},{18,26},{... | collective-permute-start | bytes 345608 | tf_op jit(solution)/shard_map/ppermute | solution.py:16
  36.5 36.3 %collective-permute-start.8 = (f32[36,9216]{1,0:T(8,128)S(1)}, f32[36,9216]{1,0:T(8,128)S(1)}, u32[]{:S(2)}, u32[]{:S(2)}) collective-permute-start(f32[36,9216]{1,0:T(8,128)S(1)} %copy-done.1), channel_id=1, source_target_pairs={{0,32},{32,64},{64,96},{96,128},{128,160},{160,192},{192,224},{1,3... | collective-permute-start | bytes 3981320 | tf_op jit(solution)/shard_map/ppermute | solution.py:16
  43.7 8.8 %all-to-all-start = ((f32[8,4,25]{2,1,0:T(4,128)}), f32[8,4,25]{2,1,0:T(4,128)S(1)}, u32[]{:S(2)}, u32[]{:S(2)}) async-start(f32[8,4,25]{2,1,0:T(4,128)} %bitcast.82), calls=%async_computation | async-start | bytes 32768 | tf_op jit(solution)/shard_map/all_to_all | solution.py:20
  53.9 11.7 %all-to-all-start.1 = ((f32[32,4,30]{2,1,0:T(4,128)}), f32[32,4,30]{2,1,0:T(4,128)S(1)}, u32[]{:S(2)}, u32[]{:S(2)}) async-start(f32[32,4,30]{2,1,0:T(4,128)} %copy.42), calls=%async_computation.1 | async-start | bytes 131072 | tf_op jit(solution)/shard_map/all_to_all | solution.py:20
  65.6 8.1 %copy-start.12 = (f32[4,30]{1,0:T(4,128)}, f32[4,30]{1,0:T(4,128)S(1)}, u32[]{:S(2)}) copy-start(f32[4,30]{1,0:T(4,128)S(1)} %reduce_sum.37) | copy-start | bytes 1444
  119.7 2.5 %copy-start.11 = (f32[1,1,1,30,72]{4,2,3,1,0:T(1,128)S(1)}, f32[1,1,1,30,72]{4,2,3,1,0:T(1,128)}, u32[]{:S(2)}) copy-start(f32[1,1,1,30,72]{4,2,3,1,0:T(1,128)} %param.34) | copy-start | bytes 25924
  119.7 2.5 %copy-start.13 = (f32[4,30]{1,0:T(4,128)S(1)}, f32[4,30]{1,0:T(4,128)}, u32[]{:S(2)}) copy-start(f32[4,30]{1,0:T(4,128)} %copy-done.12) | copy-start | bytes 1444
  120.9 13.2 %copy-start.10 = (f32[1,1,1,25,72]{4,2,3,1,0:T(1,128)S(1)}, f32[1,1,1,25,72]{4,2,3,1,0:T(1,128)}, u32[]{:S(2)}) copy-start(f32[1,1,1,25,72]{4,2,3,1,0:T(1,128)} %param.32) | copy-start | bytes 21604
  120.9 22.0 %copy-start.8 = (f32[1,1,1,125,50]{3,2,4,1,0:T(1,128)S(1)}, f32[1,1,1,125,50]{3,2,4,1,0:T(1,128)}, u32[]{:S(2)}) copy-start(f32[1,1,1,125,50]{3,2,4,1,0:T(1,128)} %param.27) | copy-start | bytes 75004
  120.9 22.2 %copy-start.6 = (f32[1,1,1,125,60]{3,2,4,1,0:T(1,128)S(1)}, f32[1,1,1,125,60]{3,2,4,1,0:T(1,128)}, u32[]{:S(2)}) copy-start(f32[1,1,1,125,60]{3,2,4,1,0:T(1,128)} %param.28) | copy-start | bytes 90004
  121.0 22.8 %copy-start.15 = (s32[1,1,1,216]{3,2,1,0:T(1,128)S(1)}, s32[1,1,1,216]{3,2,1,0:T(1,128)}, u32[]{:S(2)}) copy-start(s32[1,1,1,216]{3,2,1,0:T(1,128)} %param.25) | copy-start | bytes 2596
  144.4 4.3 %collective-permute-start.9 = (f32[1,6,24]{2,1,0:T(8,128)S(1)}, f32[1,6,24]{2,1,0:T(8,128)S(1)}, u32[]{:S(2)}, u32[]{:S(2)}) collective-permute-start(f32[1,6,24]{2,1,0:T(8,128)S(1)} %slice.93), channel_id=1, source_target_pairs={{32,0},{64,32},{96,64},{128,96},{160,128},{192,160},{224,192},{33,... | collective-permute-start | bytes 1736 | tf_op jit(solution)/shard_map/ppermute | solution.py:16
  148.7 4.3 %collective-permute-start.10 = (f32[7,1,24]{2,1,0:T(1,128)S(1)}, f32[7,1,24]{2,1,0:T(1,128)S(1)}, u32[]{:S(2)}, u32[]{:S(2)}) collective-permute-start(f32[7,1,24]{2,1,0:T(1,128)S(1)} %slice.111), channel_id=1, source_target_pairs={{8,0},{16,8},{24,16},{9,1},{17,9},{25,17},{10,2},{18,10},{26,18},{... | collective-permute-start | bytes 2024 | tf_op jit(solution)/shard_map/ppermute | solution.py:16
  153.1 6.6 %collective-permute-start.11 = (f32[7,7,4]{2,1,0:T(8,128)S(1)}, f32[7,7,4]{2,1,0:T(8,128)S(1)}, u32[]{:S(2)}, u32[]{:S(2)}) collective-permute-start(f32[7,7,4]{2,1,0:T(8,128)S(1)} %pad_maximum_fusion), channel_id=1, source_target_pairs={{1,0},{2,1},{3,2},{4,3},{5,4},{6,5},{7,6},{9,8},{10,9},{11,10},{12... | collective-permute-start | bytes 2360 | tf_op jit(solution)/shard_map/ppermute | solution.py:16

commit v3 on v2

v3 whole, which is shorter than its diff:
```python
import functools

import numpy as np
import jax
import jax.numpy as jnp
from jax import lax
from jax.experimental import pallas as pl
from jax.experimental.pallas import tpu as pltpu
from jax.sharding import PartitionSpec as P

PLANE = ("gy", "gz")
precise = lax.Precision.HIGHEST
VMEM = pl.BlockSpec(memory_space=pltpu.VMEM)
SMEM = pl.BlockSpec(memory_space=pltpu.SMEM)
LIMIT = pltpu.CompilerParams(vmem_limit_bytes=16 * 1024 * 1024)


def shifted(shard, axis, by):
    peers = lax.axis_size(axis)
    pairs = [(i, i + by) for i in range(peers) if 0 <= i + by < peers]
    return lax.ppermute(shard, axis, pairs)


def exchanged(pieces, axis):
    return lax.all_to_all(pieces, axis, split_axis=0, concat_axis=0, tiled=True)


def sent_to_all(shard, axis):
    copies = jnp.broadcast_to(shard, (lax.axis_size(axis), *shard.shape))
    return exchanged(copies, axis)


def product(operand, matrix):
    return jnp.dot(operand, matrix, precision=precise, preferred_element_type=jnp.float32)


def product_back(operand, matrix):
    return lax.dot_general(
        operand,
        matrix,
        (((1,), (1,)), ((), ())),
        precision=precise,
        preferred_element_type=jnp.float32,
    )


def two_restrictions(distance):
    return np.maximum(0.0, 4.0 - np.abs(distance)) / 16.0


def restriction_weights(fine):
    cell = 4.0 * (np.arange(fine // 4 + 2) - 1)[:, None]
    at = np.arange(fine)[None, :]
    own = two_restrictions(cell - at)
    through_before = two_restrictions(cell - (at - 1))
    beside = through_before + two_restrictions(cell - (at + 1))
    before = np.where(at == 0, through_before, 0.0)
    return own, beside, before


def prolongation_weights(fine):
    at = np.arange(fine)[:, None] / 4.0
    cell = np.arange(fine // 4 + 1)[None, :]
    return np.maximum(0.0, 1.0 - np.abs(at - cell))


def by_lane(weights, count):
    coarse, fine = weights.shape
    out = np.zeros((count, fine, coarse, count), np.float32)
    for r in range(count):
        out[r, :, :, r] = weights.T
    return out.reshape(count, fine, coarse * count)


def parts_of(values):
    first = values.astype(jnp.bfloat16)
    rest = values - first.astype(jnp.float32)
    second = rest.astype(jnp.bfloat16)
    third = (rest - second.astype(jnp.float32)).astype(jnp.bfloat16)
    return first, second, third


def dot(left, right):
    return jnp.dot(left, right, preferred_element_type=jnp.float32)


def dot_back(left, right):
    return lax.dot_general(
        left, right, (((1,), (1,)), ((), ())), preferred_element_type=jnp.float32
    )


def times_weights_back(values, weights):
    first, second, third = parts_of(values)
    return dot_back(first, weights) + (dot_back(second, weights) + dot_back(third, weights))


def weights_times_back(weights, values):
    first, second, third = parts_of(values)
    return dot_back(weights, first) + (dot_back(weights, second) + dot_back(weights, third))


def times_weights(values, weights):
    first, second, third = parts_of(values)
    return dot(first, weights) + (dot(second, weights) + dot(third, weights))


def weights_times(weights, values):
    first, second, third = parts_of(values)
    return dot(weights, first) + (dot(weights, second) + dot(weights, third))


def restrict_body(
    own, beside, before, at, rhs, iterate, coefficient, z_own, z_beside, z_before,
    y_own, y_beside, y_before, inner, upper, lower,
):
    count, fine = rhs.shape[:2]
    coarse = own.shape[0]
    at_x, at_y, at_z = [jnp.where(at[d] == 0, 1.0, 0.0) for d in range(3)]
    beside_sum = None
    own_sum = None
    for r in range(count):
        planes = [iterate[r, x] for x in range(fine)]
        gaps = [rhs[r, x] - (6.0 + coefficient[x]) * planes[x] for x in range(fine)]
        values, cells = [], []
        for i in range(coarse):
            value = cell = None
            for x in range(fine):
                if own[i, x]:
                    term = float(own[i, x]) * gaps[x]
                    value = term if value is None else value + term
                    term = float(own[i, x]) * planes[x]
                    cell = term if cell is None else cell + term
                if beside[i, x]:
                    weight = float(beside[i, x])
                    if before[i, x]:
                        weight = weight - at_x * float(before[i, x])
                    term = weight * planes[x]
                    value = term if value is None else value + term
            values.append(value)
            cells.append(jnp.zeros_like(planes[0]) if cell is None else cell)
        value = jnp.concatenate(values, axis=0)
        cell = jnp.concatenate(cells, axis=0)
        z_pair = (z_beside[r] - at_z * z_before[r]).astype(jnp.bfloat16)
        z_cell = z_own[r].astype(jnp.bfloat16)
        term = times_weights(value, z_cell) + times_weights(cell, z_pair)
        beside_sum = term if beside_sum is None else beside_sum + term
        term = times_weights(cell, z_cell)
        own_sum = term if own_sum is None else own_sum + term
    y_pair = (y_beside[...] - at_y * y_before[...]).astype(jnp.bfloat16)
    y_cell = y_own[...].astype(jnp.bfloat16)
    result = weights_times(y_cell, beside_sum) + weights_times(y_pair, own_sum)
    result = result.reshape(coarse, coarse, coarse * count)
    inner[...] = result[1:-1]
    lower[...] = result[0]
    upper[...] = result[coarse - 1]


def restricted(at, right_side, iterate, coefficient):
    count, fine = right_side.shape[:2]
    own, beside, before = restriction_weights(fine)
    coarse = own.shape[0]
    lanes = [by_lane(w, count) for w in (own, beside, before)]
    rows = [np.kron(np.eye(coarse), w).astype(np.float32) for w in (own, beside, before)]

    def body(*refs):
        restrict_body(own, beside, before, *refs)

    layer = jax.ShapeDtypeStruct((coarse, coarse * count), jnp.float32)
    inner = jax.ShapeDtypeStruct((coarse - 2, coarse, coarse * count), jnp.float32)
    return pl.pallas_call(
        body,
        out_shape=(inner, layer, layer),
        in_specs=[SMEM] + [VMEM] * 9,
        out_specs=(VMEM,) * 3,
        compiler_params=LIMIT,
        name="restrict_twice",
    )(at, right_side, iterate, coefficient, *lanes, *rows)


def numbers(side, kind):
    lane = lax.broadcasted_iota(jnp.int32, (side * 8, 1), 0)
    x, y = lane >> 3, lane & 7
    if kind == "in":
        number = jnp.where((y >= 1) & (y <= side), x * side * side + (y - 1) * side, -1000)
    elif kind == "out":
        number = jnp.where(y < side, x * side * side + y * side, -1000)
    else:
        number = jnp.where(y == 0, x * side * side + (side - 1) * side, -1000)
    return number.astype(jnp.float32)


def one_hot(number, order):
    return jnp.where(number == order, 1.0, 0.0).astype(jnp.bfloat16)


def eye(size):
    rows = lax.broadcasted_iota(jnp.int32, (size, size), 0)
    return jnp.where(rows == lax.broadcasted_iota(jnp.int32, (size, size), 1), 1.0, 0.0).astype(
        jnp.bfloat16
    )


def picked(cells, count, side, number, order, layers=None):
    total = None
    for z in range(side) if layers is None else layers:
        layer = cells[(z + 1) * count : (z + 2) * count]
        term = times_weights(layer, one_hot(number + float(z), order))
        total = term if total is None else total + term
    return total


def split_order(order, sizes):
    out, start = [], 0
    for size in sizes:
        out.append(order[:, start : start + size])
        start += size
    return out


def prepare_body(sizes, side, order, leaf, to_first, first, second, up, down, beside):
    order = order[...].astype(jnp.float32)
    leaf_order = split_order(order, sizes)[0]
    first_size = sizes[1]
    reach = side * 8
    first = first[:, 0, :]
    up[...] = jnp.zeros_like(up)
    up[0:first_size, 0 : first.shape[1]] = first
    up[first_size : first_size + 1, 0 : order.shape[1]] = order
    face = one_hot(numbers(side, "in"), leaf_order)
    rows = weights_times(face, leaf[:, 0, :])
    down[...] = jnp.zeros_like(down)
    down[0:reach, 0 : 2 * first_size] = product_back(rows, to_first[:, 0, :])
    down[reach : reach + first_size, 0 : first.shape[1]] = first
    beside[...] = jnp.zeros_like(beside)
    beside[0 : sizes[2], :] = second[:, 0, :]
    beside[sizes[2] : sizes[2] + 1, 0 : order.shape[1]] = order


def first_body(
    sizes, side, at, inner, arrived, order, leaf, to_first, first, below, above, cells_out, pieces
):
    count = pieces.shape[1] // 4
    peers = pieces.shape[0]
    first_size = sizes[1]
    reach = side * 8
    order = order[...].astype(jnp.float32)
    leaf_order, first_order = split_order(order, sizes)[:2]
    values = inner[...]
    row = lax.broadcasted_iota(jnp.int32, values.shape, 1)
    values = values + jnp.where(row == 1, arrived[...][:, None, :], 0.0)
    lanes = values.shape[2]
    cells = weights_times_back(eye(lanes), values.reshape(reach, lanes))
    cells_out[...] = cells
    number = numbers(side, "in")
    leaf_rhs = picked(cells, count, side, number, leaf_order)
    first_rhs = picked(cells, count, side, number, first_order, [side - 1])
    after = cells[(side + 1) * count : (side + 2) * count]
    before = cells[0:count]
    toward = product_back(product(leaf_rhs, leaf[:, 0, :]), to_first[:, 0, :])
    own_rows = first[:, 0, :]
    whole = own_rows.shape[1]
    below_rows = below[0:first_size, 0:whole]
    below_order = below[first_size : first_size + 1, 0 : order.shape[1]]
    below_order = split_order(below_order, sizes)[1]
    from_before = times_weights(before, one_hot(number + float(side - 1), below_order))
    through = product(after, above[0:reach, 0 : 2 * first_size])
    above_rows = above[reach : reach + first_size, 0:whole]
    terms = product(first_rhs - toward[:, :first_size] - through[:, first_size:], own_rows)
    terms = terms + product(from_before - toward[:, first_size:], below_rows)
    terms = terms - product(through[:, :first_size], above_rows)
    pieces[...] = jnp.zeros_like(pieces)
    place = at[2]
    for p in range(peers):
        pieces[p, 0:count, 0:first_size] = terms[:, p * first_size : (p + 1) * first_size]
        pieces[p, count : 2 * count, 0:reach] = jnp.where(place + 1 == p, after, 0.0)
        pieces[p, 2 * count : 3 * count, 0:reach] = jnp.where(place - 1 == p, before, 0.0)


def second_body(
    sizes, side, gz, at, received, cells, order, leaf, to_second, to_top, first_second, first_top,
    second, below, pieces, leaf_out, first_out, toward_out, top_out,
):
    peers, rows = pieces.shape[:2]
    count = rows // 2
    _, first_size, second_size, top_size = sizes
    reach = side * 8
    total = received[0]
    for p in range(1, received.shape[0]):
        total = total + received[p]
    first_own = total[0:count, 0:first_size]
    cells = cells[...]
    after = total[count : 2 * count, 0:reach]
    before = total[2 * count : 3 * count, 0:reach]
    cells = jnp.concatenate(
        [
            cells[0:count],
            cells[count : 2 * count] + after,
            cells[2 * count : side * count],
            cells[side * count : (side + 1) * count] + before,
            cells[(side + 1) * count :],
        ],
        axis=0,
    )
    order = order[...].astype(jnp.float32)
    leaf_order, _, second_order, top_order = split_order(order, sizes)
    number = numbers(side, "in")
    leaf_solved = product(picked(cells, count, side, number, leaf_order), leaf[:, 0, :])
    second_rhs = picked(cells, count, side, number, second_order)
    top_out[...] = picked(cells, count, side, number, top_order)
    below_order = below[second_size : second_size + 1, 0 : order.shape[1]]
    _, _, below_second, below_top = split_order(below_order, sizes)
    number = numbers(side, "before")
    from_before = picked(cells, count, side, number, below_second)
    top_before = picked(cells, count, side, number, below_top)
    toward = product_back(leaf_solved, to_second[:, 0, :])
    toward = toward + product(first_own, first_second[:, 0, :])
    terms = product(second_rhs - toward[:, :second_size], second[:, 0, :])
    terms = terms + product(from_before - toward[:, second_size:], below[0:second_size, :])
    pieces[...] = jnp.zeros_like(pieces)
    place = (at[1] - 1) * gz + at[2]
    for p in range(peers):
        pieces[p, 0:count, 0:second_size] = terms[:, p * second_size : (p + 1) * second_size]
        pieces[p, count : 2 * count, 0:top_size] = jnp.where(place == p, top_before, 0.0)
    leaf_out[...] = leaf_solved
    first_out[...] = first_own
    toward_out[...] = product_back(leaf_solved, to_top[...]) + product(
        first_own, first_top[:, 0, :]
    )


def top_body(used, received, toward, rhs, second_top, top, below, pieces, second_out):
    count = toward.shape[0]
    second_size = second_out.shape[1]
    top_size = rhs.shape[1]
    total = received[0]
    for p in range(1, received.shape[0]):
        total = total + received[p]
    second_own = total[0:count, 0:second_size]
    second_out[...] = second_own
    toward = toward[...] + product(second_own, second_top[:, 0, :])
    own = rhs[...] + total[count : 2 * count, 0:top_size] - toward[:, :top_size]
    other = toward[:, top_size:]
    width = pieces.shape[2]
    for p in range(used):
        at = slice(p * width, (p + 1) * width)
        pieces[p] = product(own, top[:, at]) - product(other, below[:, at])
    for p in range(used, pieces.shape[0]):
        pieces[p] = jnp.zeros(pieces.shape[1:], jnp.float32)


def spread_sum_body(received, out):
    total = received[0]
    for p in range(1, received.shape[0]):
        total = total + received[p]
    for p in range(out.shape[0]):
        out[p] = total


def top_back_body(
    used, whole, top, below, second_own, first_own, leaf_solved, second_top, first_top, to_top,
    pair_out, second_gap, first_gap, leaf_gap,
):
    count = whole.shape[1]
    width = whole.shape[2]
    top_size = top.shape[0]

    def step(p, sums):
        piece = whole[p]
        start = pl.multiple_of(p * width, 128)
        out = list(sums)
        for t in range(width // 128):
            at = pl.ds(start + t * 128, 128)
            rows, lower = top[:, at], below[:, at]
            for r in range(count):
                line = piece[r : r + 1, t * 128 : (t + 1) * 128]
                out[r] = out[r] + rows * line
                out[count + r] = out[count + r] + lower * line
        return tuple(out)

    zero = jnp.zeros((top_size, 128), jnp.float32)
    sums = lax.fori_loop(0, used, step, (zero,) * (2 * count))
    line = lax.broadcasted_iota(jnp.int32, (count, 128), 0)
    halves = []
    for half in range(2):
        total = None
        for r in range(count):
            ones = jnp.where(line == r, 1.0, 0.0).astype(jnp.bfloat16)
            term = weights_times_back(ones, sums[half * count + r])
            total = term if total is None else total + term
        halves.append(total)
    own, lower = halves
    pair_out[...] = own

    def against(matrix):
        return product_back(own, matrix[:, :top_size]) + product_back(lower, matrix[:, top_size:])

    second_gap[...] = second_own[...] - against(second_top[:, 0, :])
    first_gap[...] = first_own[...] - against(first_top[:, 0, :])
    rows = to_top[...]
    leaf_gap[...] = leaf_solved[...] - (
        product(own, rows[:top_size]) + product(lower, rows[top_size:])
    )


def second_back_body(
    sizes, side, whole, second, below, first_gap, leaf_gap, top_back, order, leaf, to_second,
    first_second, sent, base_out, second_out,
):
    count = whole.shape[0]
    _, first_size, second_size, _ = sizes
    reach = side * 8
    own = product_back(whole[...], second[:, 0, :])
    lower = product_back(whole[...], below[0:second_size, :])
    second_out[...] = own
    weights = first_second[:, 0, :]
    gap = first_gap[...] - product_back(own, weights[:, :second_size])
    gap = gap - product_back(lower, weights[:, second_size:])
    rows = to_second[:, 0, :]
    rest = leaf_gap[...] - product(own, rows[:second_size]) - product(lower, rows[second_size:])
    base = product_back(rest, leaf[:, 0, :])
    base_out[...] = base
    order = order[...].astype(jnp.float32)
    leaf_order, _, second_order, top_order = split_order(order, sizes)
    number = numbers(side, "out")
    face = times_weights_back(base, one_hot(number, leaf_order))
    face = face + times_weights_back(own, one_hot(number, second_order))
    face = face + times_weights_back(top_back[...], one_hot(number, top_order))
    sent[...] = jnp.zeros_like(sent)
    sent[0:count, 0:first_size] = gap
    sent[count : 2 * count, 0:reach] = face


def leaf_back_body(
    sizes, side, at, received, base, second_back, top_back, order, leaf, to_first, first, below,
    above, window,
):
    count = base.shape[0]
    peers = received.shape[0]
    _, first_size, _, _ = sizes
    reach = side * 8
    whole = jnp.concatenate([received[p, 0:count, 0:first_size] for p in range(peers)], axis=1)
    total = whole.shape[1]
    own = product_back(whole, first[:, 0, :])
    lower = product_back(whole, below[0:first_size, 0:total])
    following = product_back(whole, above[reach : reach + first_size, 0:total])
    rows = to_first[:, 0, :]
    rest = product(own, rows[:first_size]) + product(lower, rows[first_size:])
    leaf_back = base[...] - product_back(rest, leaf[:, 0, :])
    face = jnp.zeros((count, reach), jnp.float32)
    for p in range(peers):
        face = face + jnp.where(at[2] + 1 == p, received[p, count : 2 * count, 0:reach], 0.0)
    through = above[0:reach, 0 : 2 * first_size]
    moved = product_back(following, through[:, :first_size])
    moved = moved + product_back(own, through[:, first_size:])
    lane = lax.broadcasted_iota(jnp.int32, (reach, reach), 0)
    shift = jnp.where(lane == lax.broadcasted_iota(jnp.int32, (reach, reach), 1) + 1, 1.0, 0.0)
    face = face - times_weights(moved, shift.astype(jnp.bfloat16))
    order = order[...].astype(jnp.float32)
    orders = split_order(order, sizes)
    number = numbers(side, "out")
    layers = []
    for z in range(side):
        layer = times_weights_back(leaf_back, one_hot(number + float(z), orders[0]))
        layer = layer + times_weights_back(
            second_back[...], one_hot(number + float(z), orders[2])
        )
        layer = layer + times_weights_back(top_back[...], one_hot(number + float(z), orders[3]))
        if z == side - 1:
            layer = layer + times_weights_back(own, one_hot(number + float(z), orders[1]))
        layers.append(layer)
    layers.append(face)
    layers.append(jnp.zeros_like(face))
    cells = jnp.concatenate(layers, axis=0)
    turned = weights_times_back(eye(reach), cells)
    window[...] = turned.reshape(window.shape)


def prolong_body(inner, after_x, after_y, y_weights, z_weights, out):
    count, fine = out.shape[:2]
    cells = inner.shape[0] + 1
    window = jnp.concatenate([inner[...], after_x[...][None]], axis=0)
    row = lax.broadcasted_iota(jnp.int32, window.shape, 1)
    window = jnp.where(row == cells - 1, after_y[...][:, None, :], window)
    flat = window.reshape(cells * window.shape[1], window.shape[2])
    along_y = weights_times(y_weights[...].astype(jnp.bfloat16), flat)
    for r in range(count):
        along_z = times_weights(along_y, z_weights[r].astype(jnp.bfloat16))
        planes = [along_z[i * fine : (i + 1) * fine] for i in range(cells)]
        for i in range(cells - 1):
            for q in range(4):
                value = planes[i]
                if q:
                    value = (1.0 - q / 4.0) * value + (q / 4.0) * planes[i + 1]
                out[r, 4 * i + q] = value


def prolonged(inner, after_x, after_y, count, fine):
    cells = inner.shape[0] + 1
    weights = prolongation_weights(fine)
    along_y = np.zeros((fine, inner.shape[1]))
    along_y[:, :cells] = weights
    rows = np.kron(np.eye(cells), along_y).astype(np.float32)
    lanes = np.zeros((count, inner.shape[2], fine), np.float32)
    for r in range(count):
        for k in range(cells):
            lanes[r, k * count + r] = weights[:, k]
    return pl.pallas_call(
        prolong_body,
        out_shape=jax.ShapeDtypeStruct((count, fine, fine, fine), jnp.float32),
        in_specs=[VMEM] * 5,
        out_specs=VMEM,
        compiler_params=LIMIT,
        name="prolong_twice",
    )(inner, after_x, after_y, rows, lanes)


def padded(values, dim, before, after):
    widths = [(0, 0)] * values.ndim
    widths[dim] = (before, after)
    return jnp.pad(values, widths)


def call(body, scalars, outs, *operands):
    shapes = tuple(jax.ShapeDtypeStruct(o, jnp.float32) for o in outs)
    return pl.pallas_call(
        body,
        out_shape=shapes,
        in_specs=[SMEM] * scalars + [VMEM] * (len(operands) - scalars),
        out_specs=(VMEM,) * len(shapes),
        compiler_params=LIMIT,
    )(*operands)


def per_device(
    right_side,
    iterate,
    coefficient,
    ordering,
    leaf_inverse,
    leaf_first,
    leaf_second,
    leaf_top,
    first_inverse,
    first_second,
    first_top,
    second_inverse,
    second_top,
    top_inverse,
):
    count, fine = right_side.shape[:2]
    leaf_size = leaf_inverse.shape[-1]
    first_size = first_second.shape[3]
    second_size = second_top.shape[3]
    top_size, top_total = top_inverse.shape
    sizes = (leaf_size, first_size, second_size, top_size)
    side = fine // 4
    cells = side**3
    reach = side * 8
    lanes = (side + 2) * count
    gz = lax.axis_size("gz")
    plane_peers = lax.axis_size(PLANE)

    def rows_of(block):
        return jnp.transpose(block, (0, 1, 3, 2, 4)).reshape(block.shape[3], 1, block.shape[4])

    def columns_of(block):
        return jnp.transpose(block, (0, 1, 4, 2, 3)).reshape(block.shape[4], 1, block.shape[3])

    leaf = rows_of(leaf_inverse)
    to_first = columns_of(leaf_first)
    to_second = columns_of(leaf_second)
    to_top = jnp.swapaxes(leaf_top[0, 0, 0], 0, 1)
    first_to_second = rows_of(first_second)
    first_to_top = rows_of(first_top)
    second_to_top = rows_of(second_top)
    first = jnp.transpose(first_inverse, (0, 2, 1, 3)).reshape(first_size, 1, -1)
    second = jnp.transpose(second_inverse, (1, 0, 2))
    order = ordering.reshape(1, cells)

    at = jnp.stack([lax.axis_index(a) for a in ("gx", "gy", "gz")]).astype(jnp.int32)
    inner, upper, lower = restricted(at, right_side, iterate, coefficient)
    from_below = shifted(upper, "gx", 1)
    from_above = shifted(lower, "gx", -1)
    whole_first = -(-max(first.shape[2], cells) // 128) * 128
    up, down, beside = call(
        functools.partial(prepare_body, sizes, side),
        0,
        [(32, whole_first), (reach + 32, whole_first), (32, second.shape[2])],
        order,
        leaf,
        to_first,
        first,
        second,
    )
    first_below = shifted(up, "gz", 1)
    first_above = shifted(down, "gz", -1)
    second_below = shifted(beside, "gy", 1)
    top_below = shifted(top_inverse, "gx", 1)
    inner = inner + padded(from_below[None], 0, 0, side - 1)
    inner = inner + padded(from_above[None], 0, side - 1, 0)
    arrived = shifted(inner[:, side + 1], "gy", 1)

    turned, pieces = call(
        functools.partial(first_body, sizes, side),
        1,
        [(lanes, reach), (gz, 4 * count, 128)],
        at,
        inner,
        arrived,
        order,
        leaf,
        to_first,
        first,
        first_below,
        first_above,
    )
    received = exchanged(pieces, "gz")
    pieces, leaf_solved, first_own, toward, top_rhs = call(
        functools.partial(second_body, sizes, side, gz),
        1,
        [
            (plane_peers, 2 * count, 128),
            (count, leaf_size),
            (count, first_size),
            (count, 2 * top_size),
            (count, top_size),
        ],
        at,
        received,
        turned,
        order,
        leaf,
        to_second,
        to_top,
        first_to_second,
        first_to_top,
        second,
        second_below,
    )
    received = exchanged(pieces, PLANE)
    width = 128 * -(-top_total // (128 * plane_peers))
    used = top_total // width
    pieces, second_own = call(
        functools.partial(top_body, used),
        0,
        [(plane_peers, count, width), (count, second_size)],
        received,
        toward,
        top_rhs,
        second_to_top,
        top_inverse,
        top_below,
    )
    received = exchanged(pieces, PLANE)
    (pieces,) = call(spread_sum_body, 0, [(lax.axis_size("gx"), count, width)], received)
    received = exchanged(pieces, "gx")
    (pieces,) = call(spread_sum_body, 0, [(plane_peers, count, width)], received)
    received = exchanged(pieces, PLANE)
    top_back, second_gap, first_gap, leaf_gap = call(
        functools.partial(top_back_body, used),
        0,
        [(count, top_size), (count, second_size), (count, first_size), (count, leaf_size)],
        received,
        top_inverse,
        top_below,
        second_own,
        first_own,
        leaf_solved,
        second_to_top,
        first_to_top,
        to_top,
    )
    second_whole = jnp.moveaxis(sent_to_all(second_gap, PLANE), 0, 1).reshape(count, -1)
    sent, base, second_back = call(
        functools.partial(second_back_body, sizes, side),
        0,
        [(2 * count, 128), (count, leaf_size), (count, second_size)],
        second_whole,
        second,
        second_below,
        first_gap,
        leaf_gap,
        top_back,
        order,
        leaf,
        to_second,
        first_to_second,
    )
    received = sent_to_all(sent, "gz")
    (window,) = call(
        functools.partial(leaf_back_body, sizes, side),
        1,
        [(side, 8, lanes)],
        at,
        received,
        base,
        second_back,
        top_back,
        order,
        leaf,
        to_first,
        first,
        first_below,
        first_above,
    )
    after_x = shifted(window[0], "gx", -1)
    layer = jnp.concatenate([window[:, 0], after_x[0:1]], axis=0)
    after_y = shifted(layer, "gy", -1)
    return prolonged(window, after_x, after_y, count, fine)


def solution(mesh):
    blocks = P("gx", "gy", "gz")
    return jax.shard_map(
        per_device,
        mesh=mesh,
        in_specs=(
            P(None, "gx", "gy", "gz"),
            P(None, "gx", "gy", "gz"),
            blocks,
            blocks,
            blocks,
            blocks,
            blocks,
            blocks,
            blocks,
            blocks,
            blocks,
            P("gx", PLANE, None),
            blocks,
            P(("gx", "gy", "gz"), None),
        ),
        out_specs=P(None, "gx", "gy", "gz"),
        check_vma=False,
    )
```

time: 164 us -> 157 us (0.957)
  matrix products: 11.8 us -> 0 us
  blocking collectives: 62.8 us -> 74.4 us
  starting transfers between devices: 42.9 us -> 31.5 us
  waiting for transfers between devices: 30.5 us -> 20.5 us
  Pallas kernels: 6.3 us -> 14.8 us
  local copies, waits for them, and re-layouts: 5.32 us -> 13.5 us
  other arithmetic: 2.95 us -> 0.1 us
    unnamed x35 -> x59, local copies, waits for them, and re-layouts: 1.38 us -> 13.3 us
    dot_general x28 -> x0, matrix products: 11.8 us -> none  [the longest x14 6.15 us: product(): jnp.dot(operand, matrix, precision=precise, preferred_element_type=jnp.fl...]
    all_to_all x5 -> x6, blocking collectives: 62.8 us -> 74.4 us  [exchanged(): return lax.all_to_all(pieces, axis, split_axis=0, concat_axis=0, tiled=True)]
    ppermute x12 -> x9, starting transfers between devices: 34.4 us -> 24.5 us  [shifted(): return lax.ppermute(shard, axis, pairs)]
    pallas_call x1 -> x10, Pallas kernels: 3.66 us -> 13.1 us  [the longest x9 11.4 us: call(): pl.pallas_call(body, out_shape=shapes, in_specs=[SMEM] * scalars + [VMEM]...]
    all_to_all x2 -> x1, waiting for transfers between devices: 11 us -> 4.85 us  [exchanged(): return lax.all_to_all(pieces, axis, split_axis=0, concat_axis=0, tiled=True)]
    ppermute x12 -> x9, waiting for transfers between devices: 19.5 us -> 15.6 us  [shifted(): return lax.ppermute(shard, axis, pairs)]
    all_to_all x2 -> x1, starting transfers between devices: 8.47 us -> 7 us  [exchanged(): return lax.all_to_all(pieces, axis, split_axis=0, concat_axis=0, tiled=True)]
  transfers between devices with their start and end apart: 14 -> 10, of which waited for: 8 -> 5; matrix products, arithmetic and copies ran while one was open for 5% -> 0% of each run, Pallas kernels for 0% -> 4%
where the time goes in v3:
time: 157 us; the launch traced here: 155 us
  blocking collectives  74.4 us (47%)
  starting transfers between devices  31.5 us (20%)
  waiting for transfers between devices  20.5 us (13%)
  Pallas kernels  14.8 us (9%)
  local copies, waits for them, and re-layouts  13.5 us (9%)
    all_to_all x6, blocking collectives, exchanged(): return lax.all_to_all(pieces, axis, split_axis=0, concat_axis=0, tiled=True)  74.4 us
    ppermute x9, starting transfers between devices, shifted(): return lax.ppermute(shard, axis, pairs)  24.5 us
    ppermute x9, waiting for transfers between devices, shifted(): return lax.ppermute(shard, axis, pairs)  15.6 us
    unnamed x59, local copies, waits for them, and re-layouts  13.3 us
    pallas_call x9, Pallas kernels, call(): pl.pallas_call(body, out_shape=shapes, in_specs=[SMEM] * scalars + [VMEM]...  11.4 us
    all_to_all x1, starting transfers between devices, exchanged(): return lax.all_to_all(pieces, axis, split_axis=0, concat_axis=0, tiled=True)  7 us
    all_to_all x1, waiting for transfers between devices, exchanged(): return lax.all_to_all(pieces, axis, split_axis=0, concat_axis=0, tiled=True)  4.85 us
  transfers between devices with their start and end apart: 10, of which 5 were waited for; matrix products, arithmetic and copies ran while one was open for 0% of the time, Pallas kernels for 4%

profile of v3, /device:TPU:1, one launch (start us, length us, event | category | flops | bytes accessed | tf_op | source)
XLA Modules:
  0.0 155.1 jit_solution(16961520898877352262)
XLA Ops:
  0.0 4.4 %collective-permute-start.6 = (f32[36,9216]{1,0:T(8,128)}, f32[36,9216]{1,0:T(8,128)S(1)}, u32[]{:S(2)}, u32[]{:S(2)}) collective-permute-start(f32[36,9216]{1,0:T(8,128)} %top.3), channel_id=1, source_target_pairs={{0,32},{32,64},{64,96},{96,128},{128,160},{160,192},{192,224},{1,3... | collective-permute-start | bytes 3981320 | tf_op jit(solution)/shard_map/ppermute | solution.py:21
  4.5 0.1 pad_add_fusion.refs_0_.at
  4.5 1.3 copy-done.2
  5.8 1.3 copy-done.3
  7.1 1.0 copy-done.5
  8.0 0.8 copy-done.12
  8.9 0.8 copy-done.13
  9.7 0.8 copy-done.14
  10.6 0.8 copy-done.23
  11.4 0.8 copy-done.24
  12.2 0.8 copy-done.25
  13.0 0.0 copy-start.26
  13.0 0.0 copy-start.8
  13.0 1.7 %restrict_twice.1 = (f32[6,8,32]{2,1,0:T(8,128)S(1)}, f32[8,32]{1,0:T(8,128)S(1)}, f32[8,32]{1,0:T(8,128)S(1)}) custom-call(s32[3]{0:T(128)S(1)} %pad_add_fusion.refs_0_.at, f32[4,24,24,24]{3,2,1,0:T(8,128)S(1)} %copy-done.2, f32[4,24,24,24]{3,2,1,0:T(8,128)S(1)} %copy-done.3, f32[24,24,24]{2,1,0:T(8,128)S(1)} %copy-done.5, f32[4,24,32]{2,1,0:T(8,128)S(1)} %copy-done.25, ...), custom_call_target="tpu_custom_call" | custom-call | tf_op jit(solution)/shard_map/restrict_twice/pallas_call | solution.py:171
  14.7 0.0 copy-start
  14.7 3.6 %collective-permute-start = (f32[8,32]{1,0:T(8,128)S(1)}, f32[8,32]{1,0:T(8,128)S(1)}, u32[]{:S(2)}, u32[]{:S(2)}) collective-permute-start(f32[8,32]{1,0:T(8,128)S(1)} %get-tuple-element.28), channel_id=1, source_target_pairs={{0,32},{32,64},{64,96},{96,128},{128,160},{160,192},{192,224},{1,3... | collective-permute-start | bytes 3080 | tf_op jit(solution)/shard_map/ppermute | solution.py:21
  18.3 1.3 collective-permute-start.1
  19.6 0.0 copy-done.1
  19.6 0.0 copy-done.4
  19.6 0.0 copy-done.6
  19.7 0.0 copy-done.7
  19.7 0.0 copy-done.26
  19.7 1.0 shard_map.208
  20.7 4.2 %collective-permute-start.3 = (f32[32,256]{1,0:T(8,128)S(1)}, f32[32,256]{1,0:T(8,128)S(1)}, u32[]{:S(2)}, u32[]{:S(2)}) collective-permute-start(f32[32,256]{1,0:T(8,128)S(1)} %get-tuple-element.30), channel_id=1, source_target_pairs={{0,1},{1,2},{2,3},{3,4},{4,5},{5,6},{6,7},{8,9},{9,10},{10,11},{11... | collective-permute-start | bytes 98312 | tf_op jit(solution)/shard_map/ppermute | solution.py:21
  24.9 1.9 %collective-permute-start.4 = (f32[80,256]{1,0:T(8,128)S(1)}, f32[80,256]{1,0:T(8,128)S(1)}, u32[]{:S(2)}, u32[]{:S(2)}) collective-permute-start(f32[80,256]{1,0:T(8,128)S(1)} %get-tuple-element.31), channel_id=1, source_target_pairs={{1,0},{2,1},{3,2},{4,3},{5,4},{6,5},{7,6},{9,8},{10,9},{11,10},{12... | collective-permute-start | bytes 245768 | tf_op jit(solution)/shard_map/ppermute | solution.py:21
  26.8 8.8 %collective-permute-done = f32[8,32]{1,0:T(8,128)S(1)} collective-permute-done((f32[8,32]{1,0:T(8,128)S(1)}, f32[8,32]{1,0:T(8,128)S(1)}, u32[]{:S(2)}, u32[]{:S(2)}) %collective-permute-start) | collective-permute-done | bytes 1056 | tf_op jit(solution)/shard_map/ppermute | solution.py:21
  35.6 3.2 %collective-permute-start.5 = (f32[32,960]{1,0:T(8,128)}, f32[32,960]{1,0:T(8,128)S(1)}, u32[]{:S(2)}, u32[]{:S(2)}) collective-permute-start(f32[32,960]{1,0:T(8,128)} %get-tuple-element.34), channel_id=1, source_target_pairs={{0,8},{8,16},{16,24},{1,9},{9,17},{17,25},{2,10},{10,18},{18,26},{... | collective-permute-start | bytes 368648 | tf_op jit(solution)/shard_map/ppermute | solution.py:21
  38.8 0.0 collective-permute-done.1
  38.9 3.2 %collective-permute-start.2 = (f32[6,32]{1,0:T(8,128)S(1)}, f32[6,32]{1,0:T(8,128)S(1)}, u32[]{:S(2)}, u32[]{:S(2)}) collective-permute-start(f32[6,32]{1,0:T(8,128)S(1)} %slice_bitcast_fusion.1), channel_id=1, source_target_pairs={{0,8},{8,16},{16,24},{1,9},{9,17},{17,25},{2,10},{10,18},{18,26},{... | collective-permute-start | bytes 2312 | tf_op jit(solution)/shard_map/ppermute | solution.py:21
  42.1 0.7 collective-permute-done.2.arrived
  42.8 0.0 collective-permute-done.3.below
  42.8 0.0 collective-permute-done.4.above
  42.8 1.7 %shard_map.209 = (f32[32,48]{1,0:T(8,128)S(1)}, f32[8,16,128]{2,1,0:T(8,128)S(1)}) custom-call(s32[3]{0:T(128)S(1)} %pad_add_fusion.refs_0_.at, f32[6,8,32]{2,1,0:T(8,128)S(1)} %copy.30.inner, f32[6,32]{1,0:T(8,128)S(1)} %collective-permute-done.2.arrived, s32[1,216]{1,0:T(1,128)S(1)} %bitcast.54, f32[125,1,125]{2,1,0:T(1,128)S(1)} %bitcast.30, ...), custom_call_target="tpu_custom_call" | custom-call | tf_op jit(solution)/shard_map/pallas_call | solution.py:526
  44.5 0.6 copy-done.15
  45.1 0.6 copy-done.27
  45.7 7.0 %all-to-all-start = ((f32[8,16,128]{2,1,0:T(8,128)}), f32[8,16,128]{2,1,0:T(8,128)S(1)}, u32[]{:S(2)}, u32[]{:S(2)}) async-start(f32[8,16,128]{2,1,0:T(8,128)} %copy-done.15), calls=%async_computation | async-start | bytes 131072 | tf_op jit(solution)/shard_map/all_to_all | solution.py:25
  52.7 0.0 collective-permute-done.5.below
  52.7 4.8 %all-to-all-done.received = f32[8,16,128]{2,1,0:T(8,128)S(1)} async-done(((f32[8,16,128]{2,1,0:T(8,128)}), f32[8,16,128]{2,1,0:T(8,128)S(1)}, u32[]{:S(2)}, u32[]{:S(2)}) %all-to-all-start) | async-done | bytes 65568 | tf_op jit(solution)/shard_map/all_to_all | solution.py:25
  57.6 0.0 copy-done.8
  57.6 0.8 copy-done.9
  58.3 0.7 copy-done.19
  59.0 0.7 copy-done.21
  59.7 0.7 copy-done.28
  60.5 1.9 %shard_map.210 = (f32[32,8,128]{2,1,0:T(8,128)S(1)}, f32[4,125]{1,0:T(4,128)S(1)}, f32[4,25]{1,0:T(4,128)S(1)}, f32[4,72]{1,0:T(4,128)S(1)}, f32[4,36]{1,0:T(4,128)S(1)}) custom-call(s32[3]{0:T(128)S(1)} %pad_add_fusion.refs_0_.at, f32[8,16,128]{2,1,0:T(8,128)S(1)} %all-to-all-done.received, f32[32,48]{1,0:T(8,128)S(1)} %copy-done.28, ...), custom_call_target="tpu_custom_call" | custom-call | tf_op jit(solution)/shard_map/pallas_call | solution.py:526
  62.4 13.8 %all_to_all.35.received = f32[32,8,128]{2,1,0:T(8,128)S(1)} all-to-all(f32[32,8,128]{2,1,0:T(8,128)S(1)} %get-tuple-element.35), channel_id=1, replica_groups=mesh['gx'=8,'gy'=4,'gz'=8] {'gy','gz'}, dimensions={0} | all-to-all | bytes 262144 | tf_op jit(solution)/shard_map/all_to_all | solution.py:25
  76.2 0.0 collective-permute-done.6.below
  76.2 0.0 copy-done
  76.2 0.7 copy-done.17
  76.9 2.2 %shard_map.211 = (f32[32,4,384]{2,1,0:T(4,128)S(1)}, f32[4,30]{1,0:T(4,128)S(1)}) custom-call(f32[32,8,128]{2,1,0:T(8,128)S(1)} %all_to_all.35.received, f32[4,72]{1,0:T(4,128)S(1)} %get-tuple-element.36.toward, f32[4,36]{1,0:T(4,128)S(1)} %get-tuple-element.37.rhs, f32[30,1,72]{2,1,0:T(1,128)S(1)} %bitcast.47, f32[36,9216]{1,0:T(8,128)S(1)} %copy-done, ...), custom_call_target="tpu_custom_call" | custom-call | tf_op jit(solution)/shard_map/pallas_call | solution.py:526
  79.2 12.1 %all_to_all.36.received = f32[32,4,384]{2,1,0:T(4,128)S(1)} all-to-all(f32[32,4,384]{2,1,0:T(4,128)S(1)} %get-tuple-element.38), channel_id=1, replica_groups=mesh['gx'=8,'gy'=4,'gz'=8] {'gy','gz'}, dimensions={0} | all-to-all | bytes 393216 | tf_op jit(solution)/shard_map/all_to_all | solution.py:25
  91.3 16.7 %all_to_all.37.received = f32[8,4,384]{2,1,0:T(4,128)S(1)} all-to-all(f32[8,4,384]{2,1,0:T(4,128)S(1)} %shard_map.212), channel_id=1, replica_groups=mesh['gx'=8,'gy'=4,'gz'=8] {'gx'}, dimensions={0} | all-to-all | bytes 98304 | tf_op jit(solution)/shard_map/all_to_all | solution.py:25
  108.0 13.3 %all_to_all.38.whole = f32[32,4,384]{2,1,0:T(4,128)S(1)} all-to-all(f32[32,4,384]{2,1,0:T(4,128)S(1)} %shard_map.213), channel_id=1, replica_groups=mesh['gx'=8,'gy'=4,'gz'=8] {'gy','gz'}, dimensions={0} | all-to-all | bytes 393216 | tf_op jit(solution)/shard_map/all_to_all | solution.py:25
  121.3 1.7 %shard_map.214 = (f32[4,36]{1,0:T(4,128)S(1)}, f32[4,30]{1,0:T(4,128)S(1)}, f32[4,25]{1,0:T(4,128)S(1)}, f32[4,125]{1,0:T(4,128)S(1)}) custom-call(f32[32,4,384]{2,1,0:T(4,128)S(1)} %all_to_all.38.whole, f32[36,9216]{1,0:T(8,128)S(1)} %copy-done, f32[36,9216]{1,0:T(8,128)S(1)} %collective-permute-done.6.below, f32[4,30]{1,0:T(4,128)S(1)} %get-tuple-element.39.second_own, ...), custom_call_target="tpu_custom_call" | custom-call | tf_op jit(solution)/shard_map/pallas_call | solution.py:526
  123.1 11.1 %all_to_all.39 = f32[32,4,30]{2,1,0:T(4,128)S(1)} all-to-all(f32[32,4,30]{2,1,0:T(4,128)S(1)} %broadcast_in_dim.14), channel_id=1, replica_groups=mesh['gx'=8,'gy'=4,'gz'=8] {'gy','gz'}, dimensions={0} | all-to-all | bytes 30720 | tf_op jit(solution)/shard_map/all_to_all | solution.py:25
  134.1 0.1 reshape.15.whole
  134.2 0.0 copy-done.10
  134.2 1.0 shard_map.215
  135.2 7.5 %all_to_all.40.received = f32[8,8,128]{2,1,0:T(8,128)S(1)} all-to-all(f32[8,8,128]{2,1,0:T(8,128)S(1)} %broadcast_in_dim.15), channel_id=1, replica_groups=mesh['gx'=8,'gy'=4,'gz'=8] {'gz'}, dimensions={0} | all-to-all | bytes 65536 | tf_op jit(solution)/shard_map/all_to_all | solution.py:25
  142.7 1.9 %shard_map.216.inner = f32[6,8,32]{2,1,0:T(8,128)S(1)} custom-call(s32[3]{0:T(128)S(1)} %pad_add_fusion.refs_0_.at, f32[8,8,128]{2,1,0:T(8,128)S(1)} %all_to_all.40.received, f32[4,125]{1,0:T(4,128)S(1)} %get-tuple-element.47.base, f32[4,30]{1,0:T(4,128)S(1)} %get-tuple-element.48.second_back, f32[4,36]{1,0:T(4,128)S(1)} %get-tuple-element.45.top_back, ...), custom_call_target="tpu_custom_call" | custom-call | tf_op jit(solution)/shard_map/pallas_call | solution.py:526
  144.6 1.3 collective-permute-start.7
  145.9 3.0 %collective-permute-done.7.after_x = f32[8,32]{1,0:T(8,128)S(1)} collective-permute-done((f32[8,32]{1,0:T(8,128)S(1)}, f32[8,32]{1,0:T(8,128)S(1)}, u32[]{:S(2)}, u32[]{:S(2)}) %collective-permute-start.7) | collective-permute-done | bytes 1056 | tf_op jit(solution)/shard_map/ppermute | solution.py:21
  149.0 1.3 collective-permute-start.8
  150.3 3.1 %collective-permute-done.8.after_y = f32[7,32]{1,0:T(8,128)S(1)} collective-permute-done((f32[7,32]{1,0:T(8,128)S(1)}, f32[7,32]{1,0:T(8,128)S(1)}, u32[]{:S(2)}, u32[]{:S(2)}) %collective-permute-start.8) | collective-permute-done | bytes 928 | tf_op jit(solution)/shard_map/ppermute | solution.py:21
  153.3 1.7 %prolong_twice.1 = f32[4,24,24,24]{3,2,1,0:T(8,128)} custom-call(f32[6,8,32]{2,1,0:T(8,128)S(1)} %shard_map.216.inner, f32[8,32]{1,0:T(8,128)S(1)} %collective-permute-done.7.after_x, f32[7,32]{1,0:T(8,128)S(1)} %collective-permute-done.8.after_y, f32[168,56]{1,0:T(8,128)S(1)} %copy-done.11, f32[4,32,24]{2,1,0:T(8,128)S(1)} %copy-done.16), custom_call_target="tpu_custom_call" | custom-call | tf_op jit(solution)/shard_map/prolong_twice/pallas_call | solution.py:508
  (44 shorter events, 0.2 us)
Async XLA Ops:
  0.0 76.2 %collective-permute-start.6 = (f32[36,9216]{1,0:T(8,128)}, f32[36,9216]{1,0:T(8,128)S(1)}, u32[]{:S(2)}, u32[]{:S(2)}) collective-permute-start(f32[36,9216]{1,0:T(8,128)} %top.3), channel_id=1, source_target_pairs={{0,32},{32,64},{64,96},{96,128},{128,160},{160,192},{192,224},{1,3... | collective-permute-start | bytes 3981320 | tf_op jit(solution)/shard_map/ppermute | solution.py:21
  4.5 1.3 copy-start.2
  5.8 1.3 copy-start.3
  7.1 1.0 copy-start.5
  8.0 0.8 copy-start.12
  8.9 0.8 copy-start.13
  9.7 0.8 copy-start.14
  10.6 0.8 copy-start.23
  11.4 0.8 copy-start.24
  12.2 0.8 copy-start.25
  13.0 6.7 %copy-start.1 = (f32[1,1,1,125,125]{4,2,3,1,0:T(1,128)S(1)}, f32[1,1,1,125,125]{4,2,3,1,0:T(1,128)}, u32[]{:S(2)}) copy-start(f32[1,1,1,125,125]{4,2,3,1,0:T(1,128)} %param.26) | copy-start | bytes 187504
  13.0 6.7 %copy-start.4 = (f32[1,30,960]{2,0,1:T(1,128)S(1)}, f32[1,30,960]{2,0,1:T(1,128)}, u32[]{:S(2)}) copy-start(f32[1,30,960]{2,0,1:T(1,128)} %param.33) | copy-start | bytes 345604
  13.0 6.7 %copy-start.6 = (f32[1,1,1,125,50]{3,2,4,1,0:T(1,128)S(1)}, f32[1,1,1,125,50]{3,2,4,1,0:T(1,128)}, u32[]{:S(2)}) copy-start(f32[1,1,1,125,50]{3,2,4,1,0:T(1,128)} %param.27) | copy-start | bytes 75004
  13.0 6.7 %copy-start.7 = (f32[1,1,25,200]{3,1,2,0:T(1,128)S(1)}, f32[1,1,25,200]{3,1,2,0:T(1,128)}, u32[]{:S(2)}) copy-start(f32[1,1,25,200]{3,1,2,0:T(1,128)} %param.30) | copy-start | bytes 60004
  13.0 6.7 %copy-start.26 = (s32[1,1,1,216]{3,2,1,0:T(1,128)S(1)}, s32[1,1,1,216]{3,2,1,0:T(1,128)}, u32[]{:S(2)}) copy-start(s32[1,1,1,216]{3,2,1,0:T(1,128)} %param.25) | copy-start | bytes 2596
  13.0 44.6 %copy-start.8 = (f32[1,1,1,125,72]{3,4,2,1,0:T(8,128)S(1)}, f32[1,1,1,125,72]{3,4,2,1,0:T(8,128)}, u32[]{:S(2)}) copy-start(f32[1,1,1,125,72]{3,4,2,1,0:T(8,128)} %param.29) | copy-start | bytes 108004
  14.7 61.5 %copy-start = (f32[36,9216]{1,0:T(8,128)S(1)}, f32[36,9216]{1,0:T(8,128)}, u32[]{:S(2)}) copy-start(f32[36,9216]{1,0:T(8,128)} %top.3) | copy-start | bytes 3981316
  14.7 20.9 %collective-permute-start = (f32[8,32]{1,0:T(8,128)S(1)}, f32[8,32]{1,0:T(8,128)S(1)}, u32[]{:S(2)}, u32[]{:S(2)}) collective-permute-start(f32[8,32]{1,0:T(8,128)S(1)} %get-tuple-element.28), channel_id=1, source_target_pairs={{0,32},{32,64},{64,96},{96,128},{128,160},{160,192},{192,224},{1,3... | collective-permute-start | bytes 3080 | tf_op jit(solution)/shard_map/ppermute | solution.py:21
  18.3 20.5 %collective-permute-start.1 = (f32[8,32]{1,0:T(8,128)S(1)}, f32[8,32]{1,0:T(8,128)S(1)}, u32[]{:S(2)}, u32[]{:S(2)}) collective-permute-start(f32[8,32]{1,0:T(8,128)S(1)} %get-tuple-element.29), channel_id=1, source_target_pairs={{32,0},{64,32},{96,64},{128,96},{160,128},{192,160},{224,192},{33,... | collective-permute-start | bytes 3080 | tf_op jit(solution)/shard_map/ppermute | solution.py:21
  20.7 22.2 %collective-permute-start.3 = (f32[32,256]{1,0:T(8,128)S(1)}, f32[32,256]{1,0:T(8,128)S(1)}, u32[]{:S(2)}, u32[]{:S(2)}) collective-permute-start(f32[32,256]{1,0:T(8,128)S(1)} %get-tuple-element.30), channel_id=1, source_target_pairs={{0,1},{1,2},{2,3},{3,4},{4,5},{5,6},{6,7},{8,9},{9,10},{10,11},{11... | collective-permute-start | bytes 98312 | tf_op jit(solution)/shard_map/ppermute | solution.py:21
  24.9 17.9 %collective-permute-start.4 = (f32[80,256]{1,0:T(8,128)S(1)}, f32[80,256]{1,0:T(8,128)S(1)}, u32[]{:S(2)}, u32[]{:S(2)}) collective-permute-start(f32[80,256]{1,0:T(8,128)S(1)} %get-tuple-element.31), channel_id=1, source_target_pairs={{1,0},{2,1},{3,2},{4,3},{5,4},{6,5},{7,6},{9,8},{10,9},{11,10},{12... | collective-permute-start | bytes 245768 | tf_op jit(solution)/shard_map/ppermute | solution.py:21
  35.6 17.1 %collective-permute-start.5 = (f32[32,960]{1,0:T(8,128)}, f32[32,960]{1,0:T(8,128)S(1)}, u32[]{:S(2)}, u32[]{:S(2)}) collective-permute-start(f32[32,960]{1,0:T(8,128)} %get-tuple-element.34), channel_id=1, source_target_pairs={{0,8},{8,16},{16,24},{1,9},{9,17},{17,25},{2,10},{10,18},{18,26},{... | collective-permute-start | bytes 368648 | tf_op jit(solution)/shard_map/ppermute | solution.py:21
  38.9 3.9 %collective-permute-start.2 = (f32[6,32]{1,0:T(8,128)S(1)}, f32[6,32]{1,0:T(8,128)S(1)}, u32[]{:S(2)}, u32[]{:S(2)}) collective-permute-start(f32[6,32]{1,0:T(8,128)S(1)} %slice_bitcast_fusion.1), channel_id=1, source_target_pairs={{0,8},{8,16},{16,24},{1,9},{9,17},{17,25},{2,10},{10,18},{18,26},{... | collective-permute-start | bytes 2312 | tf_op jit(solution)/shard_map/ppermute | solution.py:21
  44.5 0.6 copy-start.15
  45.1 0.6 copy-start.27
  45.7 11.9 %all-to-all-start = ((f32[8,16,128]{2,1,0:T(8,128)}), f32[8,16,128]{2,1,0:T(8,128)S(1)}, u32[]{:S(2)}, u32[]{:S(2)}) async-start(f32[8,16,128]{2,1,0:T(8,128)} %copy-done.15), calls=%async_computation | async-start | bytes 131072 | tf_op jit(solution)/shard_map/all_to_all | solution.py:25
  57.6 0.8 copy-start.9
  58.3 0.7 copy-start.19
  59.0 0.7 copy-start.21
  59.7 0.7 copy-start.28
  76.2 0.7 copy-start.17
  79.2 42.1 %copy-start.18 = (f32[1,1,1,30,72]{4,2,3,1,0:T(1,128)S(1)}, f32[1,1,1,30,72]{4,2,3,1,0:T(1,128)}, u32[]{:S(2)}) copy-start(f32[1,1,1,30,72]{4,2,3,1,0:T(1,128)} %param.34) | copy-start | bytes 25924
  79.2 42.1 %copy-start.20 = (f32[1,1,1,25,72]{4,2,3,1,0:T(1,128)S(1)}, f32[1,1,1,25,72]{4,2,3,1,0:T(1,128)}, u32[]{:S(2)}) copy-start(f32[1,1,1,25,72]{4,2,3,1,0:T(1,128)} %param.32) | copy-start | bytes 21604
  121.3 12.9 %copy-start.10 = (f32[1,1,1,125,60]{3,2,4,1,0:T(1,128)S(1)}, f32[1,1,1,125,60]{3,2,4,1,0:T(1,128)}, u32[]{:S(2)}) copy-start(f32[1,1,1,125,60]{3,2,4,1,0:T(1,128)} %param.28) | copy-start | bytes 90004
  121.3 12.9 %copy-start.22 = (f32[1,1,1,25,60]{4,2,3,1,0:T(1,128)S(1)}, f32[1,1,1,25,60]{4,2,3,1,0:T(1,128)}, u32[]{:S(2)}) copy-start(f32[1,1,1,25,60]{4,2,3,1,0:T(1,128)} %param.31) | copy-start | bytes 18004
  123.0 30.3 %copy-start.11 = (f32[168,56]{1,0:T(8,128)S(1)}, f32[168,56]{1,0:T(8,128)}, u32[]{:S(2)}) copy-start(f32[168,56]{1,0:T(8,128)} %constant.37.clone.y_weights) | copy-start | bytes 112900
  123.0 30.3 %copy-start.16 = (f32[4,32,24]{2,1,0:T(8,128)S(1)}, f32[4,32,24]{2,1,0:T(8,128)}, u32[]{:S(2)}) copy-start(f32[4,32,24]{2,1,0:T(8,128)} %constant.38.clone.z_weights) | copy-start | bytes 36868
  144.6 4.4 %collective-permute-start.7 = (f32[8,32]{1,0:T(8,128)S(1)}, f32[8,32]{1,0:T(8,128)S(1)}, u32[]{:S(2)}, u32[]{:S(2)}) collective-permute-start(f32[8,32]{1,0:T(8,128)S(1)} %slice_bitcast_fusion), channel_id=1, source_target_pairs={{32,0},{64,32},{96,64},{128,96},{160,128},{192,160},{224,192},{33,... | collective-permute-start | bytes 3080 | tf_op jit(solution)/shard_map/ppermute | solution.py:21
  149.0 4.4 %collective-permute-start.8 = (f32[7,32]{1,0:T(8,128)S(1)}, f32[7,32]{1,0:T(8,128)S(1)}, u32[]{:S(2)}, u32[]{:S(2)}) collective-permute-start(f32[7,32]{1,0:T(8,128)S(1)} %pad_maximum_fusion), channel_id=1, source_target_pairs={{8,0},{16,8},{24,16},{9,1},{17,9},{25,17},{10,2},{18,10},{26,18},{... | collective-permute-start | bytes 2696 | tf_op jit(solution)/shard_map/ppermute | solution.py:21

commit v4 on v3

v4 whole, which is shorter than its diff:
```python
import functools

import numpy as np
import jax
import jax.numpy as jnp
from jax import lax
from jax.experimental import pallas as pl
from jax.experimental.pallas import tpu as pltpu
from jax.sharding import PartitionSpec as P

PLANE = ("gy", "gz")
AXES = ("gx", "gy", "gz")
precise = lax.Precision.HIGHEST
VMEM = pl.BlockSpec(memory_space=pltpu.VMEM)
HBM = pl.BlockSpec(memory_space=pltpu.HBM)
FULL = pltpu.CompilerParams(vmem_limit_bytes=67043328 - 1000 * 1024)
LIMIT = pltpu.CompilerParams(vmem_limit_bytes=16 * 1024 * 1024)


def shifted(shard, axis, by):
    peers = lax.axis_size(axis)
    pairs = [(i, i + by) for i in range(peers) if 0 <= i + by < peers]
    return lax.ppermute(shard, axis, pairs)


def exchanged(pieces, axis):
    return lax.all_to_all(pieces, axis, split_axis=0, concat_axis=0, tiled=True)


def sent_to_all(shard, axis):
    copies = jnp.broadcast_to(shard, (lax.axis_size(axis), *shard.shape))
    return exchanged(copies, axis)


def product(operand, matrix):
    return jnp.dot(operand, matrix, precision=precise, preferred_element_type=jnp.float32)


def product_back(operand, matrix):
    return lax.dot_general(
        operand,
        matrix,
        (((1,), (1,)), ((), ())),
        precision=precise,
        preferred_element_type=jnp.float32,
    )


def two_restrictions(distance):
    return np.maximum(0.0, 4.0 - np.abs(distance)) / 16.0


def restriction_weights(fine):
    cell = 4.0 * (np.arange(fine // 4 + 2) - 1)[:, None]
    at = np.arange(fine)[None, :]
    own = two_restrictions(cell - at)
    through_before = two_restrictions(cell - (at - 1))
    beside = through_before + two_restrictions(cell - (at + 1))
    before = np.where(at == 0, through_before, 0.0)
    return own, beside, before


def weight_rows(coarse, fine, kind, missing):
    rows = lax.broadcasted_iota(jnp.int32, (coarse * coarse, coarse * fine), 0)
    columns = lax.broadcasted_iota(jnp.int32, (coarse * coarse, coarse * fine), 1)
    at = columns - (rows >> 3) * fine
    weights = weights_at(4 * ((rows & 7) - 1), at, kind, missing)
    return jnp.where((at >= 0) & (at < fine), weights, 0.0).astype(jnp.bfloat16)


def weight_lanes(coarse, fine, count, r, kind, missing):
    at = lax.broadcasted_iota(jnp.int32, (fine, coarse * count), 0)
    lane = lax.broadcasted_iota(jnp.int32, (fine, coarse * count), 1)
    weights = weights_at(4 * ((lane >> 2) - 1), at, kind, missing)
    return jnp.where((lane & 3) == r, weights, 0.0).astype(jnp.bfloat16)


def weights_at(cell, at, kind, missing):
    def weight(distance):
        return jnp.maximum(4.0 - jnp.abs(distance).astype(jnp.float32), 0.0) * 0.0625

    if kind == "own":
        return weight(cell - at)
    before = jnp.where(at == 0, missing, 0.0)
    return weight(cell - at - 1) + (1.0 - before) * weight(cell - at + 1)


def parts_of(values):
    first = values.astype(jnp.bfloat16)
    rest = values - first.astype(jnp.float32)
    second = rest.astype(jnp.bfloat16)
    third = (rest - second.astype(jnp.float32)).astype(jnp.bfloat16)
    return first, second, third


def dot(left, right):
    return jnp.dot(left, right, preferred_element_type=jnp.float32)


def dot_back(left, right):
    return lax.dot_general(
        left, right, (((1,), (1,)), ((), ())), preferred_element_type=jnp.float32
    )


def times_weights_back(values, weights):
    first, second, third = parts_of(values)
    return dot_back(first, weights) + (dot_back(second, weights) + dot_back(third, weights))


def weights_times_back(weights, values):
    first, second, third = parts_of(values)
    return dot_back(weights, first) + (dot_back(weights, second) + dot_back(weights, third))


def times_weights(values, weights):
    first, second, third = parts_of(values)
    return dot(first, weights) + (dot(second, weights) + dot(third, weights))


def weights_times(weights, values):
    first, second, third = parts_of(values)
    return dot(weights, first) + (dot(weights, second) + dot(weights, third))


def restrict_body(
    own, beside, before, order, rhs_in, iterate_in, coefficient_in, inner, upper,
    rhs, iterate, coefficient, arrived,
):
    count, fine = rhs.shape[:2]
    coarse = own.shape[0]
    half = fine // 2
    copies = [pltpu.make_async_copy(coefficient_in, coefficient, arrived.at[0])]
    for r in range(count):
        for source, room in ((iterate_in, iterate), (rhs_in, rhs)):
            for start in (0, half):
                part = pl.ds(start, half)
                copies.append(
                    pltpu.make_async_copy(
                        source.at[r, part], room.at[r, part], arrived.at[len(copies)]
                    )
                )
    for copy in copies:
        copy.start()
    at_x, at_y, at_z = [jnp.where(lax.axis_index(a) == 0, 1.0, 0.0) for a in AXES]
    layer, lanes = inner.shape[1:]
    top_size = coarse - 2
    top_size = top_size * top_size
    upper[...] = jnp.zeros_like(upper)
    orders = order[...].astype(jnp.float32)
    upper[layer : layer + 1, 0:top_size] = orders[:, orders.shape[1] - top_size :]
    y_cell = weight_rows(coarse, fine, "own", None)
    y_pair = weight_rows(coarse, fine, "beside", at_y)
    z_cells = [weight_lanes(coarse, fine, count, r, "own", None) for r in range(count)]
    z_pairs = [weight_lanes(coarse, fine, count, r, "beside", at_z) for r in range(count)]
    copies[0].wait()
    beside_sum = None
    own_sum = None
    for r in range(count):
        for copy in copies[4 * r + 1 : 4 * r + 5]:
            copy.wait()
        planes = [iterate[r, x] for x in range(fine)]
        gaps = [rhs[r, x] - (6.0 + coefficient[x]) * planes[x] for x in range(fine)]
        values, cells = [], []
        for i in range(coarse):
            value = cell = None
            for x in range(fine):
                if own[i, x]:
                    term = float(own[i, x]) * gaps[x]
                    value = term if value is None else value + term
                    term = float(own[i, x]) * planes[x]
                    cell = term if cell is None else cell + term
                if beside[i, x]:
                    weight = float(beside[i, x])
                    if before[i, x]:
                        weight = weight - at_x * float(before[i, x])
                    term = weight * planes[x]
                    value = term if value is None else value + term
            values.append(value)
            cells.append(jnp.zeros_like(planes[0]) if cell is None else cell)
        value = jnp.concatenate(values, axis=0)
        cell = jnp.concatenate(cells, axis=0)
        term = times_weights(value, z_cells[r]) + times_weights(cell, z_pairs[r])
        beside_sum = term if beside_sum is None else beside_sum + term
        term = times_weights(cell, z_cells[r])
        own_sum = term if own_sum is None else own_sum + term
    result = weights_times(y_cell, beside_sum) + weights_times(y_pair, own_sum)
    result = result.reshape(coarse, coarse, coarse * count)
    inner[...] = result[:-1]
    upper[0:layer, 0:lanes] = result[coarse - 1]


def restricted(order, right_side, iterate, coefficient):
    count, fine = right_side.shape[:2]
    own, beside, before = restriction_weights(fine)
    coarse = own.shape[0]

    def body(*refs):
        restrict_body(own, beside, before, *refs)

    inner = jax.ShapeDtypeStruct((coarse - 1, coarse, coarse * count), jnp.float32)
    upper = jax.ShapeDtypeStruct((2 * coarse, 128), jnp.float32)
    return pl.pallas_call(
        body,
        out_shape=(inner, upper),
        in_specs=[VMEM] + [HBM] * 3,
        out_specs=(VMEM,) * 2,
        scratch_shapes=[
            pltpu.VMEM(right_side.shape, jnp.float32),
            pltpu.VMEM(iterate.shape, jnp.float32),
            pltpu.VMEM(coefficient.shape, jnp.float32),
            pltpu.SemaphoreType.DMA((4 * count + 1,)),
        ],
        compiler_params=FULL,
        name="restrict_twice",
    )(order, right_side, iterate, coefficient)


def numbers(side, kind):
    lane = lax.broadcasted_iota(jnp.int32, (lanes_of(side, kind), 1), 0)
    x, y = lane >> 3, lane & 7
    if kind == "out":
        number = jnp.where(y < side, x * side * side + y * side, -1000)
        return number.astype(jnp.float32)
    x, y = x - 1, y - 1
    last = side - 1
    along_y = (y >= 0) & (y < side)
    if kind == "in":
        number = jnp.where((x >= 0) & along_y, x * side * side + y * side, -1000)
    elif kind == "before_y":
        number = jnp.where((x >= 0) & (y < 0), x * side * side + last * side, -1000)
    else:
        number = jnp.where((x < 0) & along_y, last * side * side + y * side, -1000)
    return number.astype(jnp.float32)


def lanes_of(side, kind="in"):
    return side * 8 if kind == "out" else (side + 1) * 8


def one_hot(number, order):
    return jnp.where(number == order, 1.0, 0.0).astype(jnp.bfloat16)


def eye(size):
    rows = lax.broadcasted_iota(jnp.int32, (size, size), 0)
    return jnp.where(rows == lax.broadcasted_iota(jnp.int32, (size, size), 1), 1.0, 0.0).astype(
        jnp.bfloat16
    )


def picked(cells, count, side, number, order, layers=None):
    total = None
    for z in range(side) if layers is None else layers:
        layer = cells[(z + 1) * count : (z + 2) * count]
        term = times_weights(layer, one_hot(number + float(z), order))
        total = term if total is None else total + term
    return total


LEAF, TO_FIRST, TO_SECOND, TO_TOP = 0, 128, 184, 248
FIRST_SECOND, FIRST_TOP, SECOND_TOP, ORDER, PACKED = 320, 352, 384, 416, 424


def split_order(order, sizes):
    out, start = [], 0
    for size in sizes:
        out.append(order[:, start : start + size])
        start += size
    return out


def packed_order(pack, sizes):
    leaf_size = sizes[0]
    leaf_order = pack[ORDER : ORDER + 1, 0:leaf_size]
    rest = pack[ORDER + 1 : ORDER + 2, 0 : sum(sizes[1:])]
    return [leaf_order] + split_order(rest, sizes[1:])


def prepare_body(sizes, side, *refs):
    sources, (up, down, beside, pack) = refs[:10], refs[10:14]
    held, arrived = refs[14:24], refs[24]
    copies = [
        pltpu.make_async_copy(source, room, arrived.at[n])
        for n, (source, room) in enumerate(zip(sources, held))
    ]
    for copy in copies:
        copy.start()
    up[...] = jnp.zeros_like(up)
    down[...] = jnp.zeros_like(down)
    beside[sizes[2] :, :] = jnp.zeros_like(beside[sizes[2] :, :])
    for copy in copies:
        copy.wait()
    order, leaf, to_first, first, second = held[:5]
    to_second, to_top, first_second, first_top, second_top = held[5:]
    order = order[...].astype(jnp.float32)
    leaf_size, first_size, second_size = sizes[:3]
    leaf_rows, first_columns = leaf[:, 0, :], to_first[:, 0, :]
    first_rows = first[:, 0, :]
    face = one_hot(numbers(side, "in"), order[:, :leaf_size])
    rows = weights_times(face, leaf_rows)
    up[0:first_size, 0 : first_rows.shape[1]] = first_rows
    up[first_size : first_size + 1, 0 : order.shape[1]] = order
    total = first_rows.shape[1]
    down[:, total : total + 2 * first_size] = product_back(rows, first_columns)
    down[0:first_size, 0:total] = first_rows
    beside[0:second_size, :] = second[:, 0, :]
    beside[second_size : second_size + 1, 0 : order.shape[1]] = order
    pack[ORDER : ORDER + 1, 0:leaf_size] = order[:, :leaf_size]
    pack[ORDER + 1 : ORDER + 2, 0 : order.shape[1] - leaf_size] = order[:, leaf_size:]
    for start, rows in (
        (LEAF, leaf_rows),
        (TO_FIRST, first_columns),
        (TO_SECOND, to_second[:, 0, :]),
        (TO_TOP, to_top[...]),
        (FIRST_SECOND, first_second[:, 0, :]),
        (FIRST_TOP, first_top[:, 0, :]),
        (SECOND_TOP, second_top[:, 0, :]),
    ):
        pack[start : start + rows.shape[0], 0 : rows.shape[1]] = rows


def prepared(sizes, side, width, *sources):
    leaf_size, first_size, second_size, top_size = sizes
    assert leaf_size <= 128 and first_size < 32 and second_size < 32 and top_size <= 36
    shapes = (
        (32, width),
        (lanes_of(side), width),
        (32, sources[4].shape[2]),
        (PACKED, 128),
    )
    return pl.pallas_call(
        functools.partial(prepare_body, sizes, side),
        out_shape=tuple(jax.ShapeDtypeStruct(o, jnp.float32) for o in shapes),
        in_specs=[HBM] * len(sources),
        out_specs=(VMEM,) * len(shapes),
        scratch_shapes=[pltpu.VMEM(x.shape, x.dtype) for x in sources]
        + [pltpu.SemaphoreType.DMA((len(sources),))],
        compiler_params=LIMIT,
        name="prepare",
    )(*sources)


def first_body(
    sizes, side, total, inner, from_x, from_y, pack, first, below, above, cells_out, pieces
):
    count = pieces.shape[1] // 4
    peers = pieces.shape[0]
    first_size = sizes[1]
    leaf_size = sizes[0]
    leaf_order, first_order = packed_order(pack, sizes)[:2]
    values = inner[...]
    across, along, lanes = values.shape
    reach = across * along
    row = lax.broadcasted_iota(jnp.int32, values.shape, 0)
    values = values + jnp.where(row == 1, from_x[0:along, 0:lanes][None], 0.0)
    row = lax.broadcasted_iota(jnp.int32, values.shape, 1)
    values = values + jnp.where(row == 1, from_y[...][:, None, :], 0.0)
    cells = weights_times_back(eye(lanes), values.reshape(reach, lanes))
    cells_out[...] = cells
    number = numbers(side, "in")
    leaf_rhs = picked(cells, count, side, number, leaf_order)
    first_rhs = picked(cells, count, side, number, first_order, [side - 1])
    after = cells[(side + 1) * count : (side + 2) * count]
    before = cells[0:count]
    leaf = pack[LEAF : LEAF + leaf_size, 0:leaf_size]
    to_first = pack[TO_FIRST : TO_FIRST + 2 * first_size, 0:leaf_size]
    toward = product_back(product(leaf_rhs, leaf), to_first)
    whole = total
    own_rows = first[0:first_size, 0:whole]
    below_rows = below[0:first_size, 0:whole]
    below_order = below[first_size : first_size + 1, 0 : sum(sizes)]
    below_order = split_order(below_order, sizes)[1]
    from_before = times_weights(before, one_hot(number + float(side - 1), below_order))
    through = product(after, above[:, whole : whole + 2 * first_size])
    above_rows = above[0:first_size, 0:whole]
    terms = product(first_rhs - toward[:, :first_size] - through[:, first_size:], own_rows)
    terms = terms + product(from_before - toward[:, first_size:], below_rows)
    terms = terms - product(through[:, :first_size], above_rows)
    pieces[...] = jnp.zeros_like(pieces)
    place = lax.axis_index("gz")
    for p in range(peers):
        pieces[p, 0:count, 0:first_size] = terms[:, p * first_size : (p + 1) * first_size]
        pieces[p, count : 2 * count, 0:reach] = jnp.where(place + 1 == p, after, 0.0)
        pieces[p, 2 * count : 3 * count, 0:reach] = jnp.where(place - 1 == p, before, 0.0)


def second_body(
    sizes, side, gz, received, cells, from_x, pack, second, below, pieces, leaf_out, first_out,
    toward_out, top_out,
):
    peers, rows = pieces.shape[:2]
    count = rows // 2
    leaf_size, first_size, second_size, top_size = sizes
    reach = cells.shape[1]
    total = received[0]
    for p in range(1, received.shape[0]):
        total = total + received[p]
    first_own = total[0:count, 0:first_size]
    cells = cells[...]
    after = total[count : 2 * count, 0:reach]
    before = total[2 * count : 3 * count, 0:reach]
    cells = jnp.concatenate(
        [
            cells[0:count],
            cells[count : 2 * count] + after,
            cells[2 * count : side * count],
            cells[side * count : (side + 1) * count] + before,
            cells[(side + 1) * count :],
        ],
        axis=0,
    )
    leaf_order, _, second_order, top_order = packed_order(pack, sizes)
    number = numbers(side, "in")
    leaf = pack[LEAF : LEAF + leaf_size, 0:leaf_size]
    to_second = pack[TO_SECOND : TO_SECOND + 2 * second_size, 0:leaf_size]
    to_top = pack[TO_TOP : TO_TOP + 2 * top_size, 0:leaf_size]
    first_second = pack[FIRST_SECOND : FIRST_SECOND + first_size, 0 : 2 * second_size]
    first_top = pack[FIRST_TOP : FIRST_TOP + first_size, 0 : 2 * top_size]
    leaf_solved = product(picked(cells, count, side, number, leaf_order), leaf)
    second_rhs = picked(cells, count, side, number, second_order)
    top_out[...] = picked(cells, count, side, number, top_order)
    below_order = below[second_size : second_size + 1, 0 : sum(sizes)]
    _, _, below_second, below_top = split_order(below_order, sizes)
    number = numbers(side, "before_y")
    from_before = picked(cells, count, side, number, below_second)
    top_before = picked(cells, count, side, number, below_top)
    toward = product_back(leaf_solved, to_second) + product(first_own, first_second)
    terms = product(second_rhs - toward[:, :second_size], second[0:second_size, :])
    terms = terms + product(from_before - toward[:, second_size:], below[0:second_size, :])
    pieces[...] = jnp.zeros_like(pieces)
    place = (lax.axis_index("gy") - 1) * gz + lax.axis_index("gz")
    for p in range(peers):
        pieces[p, 0:count, 0:second_size] = terms[:, p * second_size : (p + 1) * second_size]
        pieces[p, count : 2 * count, 0:top_size] = jnp.where(place == p, top_before, 0.0)
    leaf_out[...] = leaf_solved
    first_out[...] = first_own
    toward = product_back(leaf_solved, to_top) + product(first_own, first_top)
    order_x = from_x[8:9, 0:top_size]
    before_x = picked(cells, count, side, numbers(side, "before_x"), order_x)
    toward_out[:, :top_size] = toward[:, :top_size]
    toward_out[:, top_size:] = toward[:, top_size:] - before_x


def top_body(used, received, toward, rhs, pack, top, below, pieces, second_out):
    count = toward.shape[0]
    second_size = second_out.shape[1]
    top_size = rhs.shape[1]
    total = received[0]
    for p in range(1, received.shape[0]):
        total = total + received[p]
    second_own = total[0:count, 0:second_size]
    second_out[...] = second_own
    second_top = pack[SECOND_TOP : SECOND_TOP + second_size, 0 : 2 * top_size]
    toward = toward[...] + product(second_own, second_top)
    own = rhs[...] + total[count : 2 * count, 0:top_size] - toward[:, :top_size]
    other = toward[:, top_size:]
    width = pieces.shape[2]
    for p in range(used):
        at = slice(p * width, (p + 1) * width)
        pieces[p] = product(own, top[:, at]) - product(other, below[:, at])
    for p in range(used, pieces.shape[0]):
        pieces[p] = jnp.zeros(pieces.shape[1:], jnp.float32)


def spread_sum_body(received, out):
    total = received[0]
    for p in range(1, received.shape[0]):
        total = total + received[p]
    for p in range(out.shape[0]):
        out[p] = total


def top_back_body(
    used, whole, top, below, second_own, first_own, leaf_solved, pack, pair_out, second_gap,
    first_gap, leaf_gap,
):
    count = whole.shape[1]
    width = whole.shape[2]
    top_size = top.shape[0]

    def step(p, sums):
        piece = whole[p]
        start = pl.multiple_of(p * width, 128)
        out = list(sums)
        for t in range(width // 128):
            at = pl.ds(start + t * 128, 128)
            rows, lower = top[:, at], below[:, at]
            for r in range(count):
                line = piece[r : r + 1, t * 128 : (t + 1) * 128]
                out[r] = out[r] + rows * line
                out[count + r] = out[count + r] + lower * line
        return tuple(out)

    zero = jnp.zeros((top_size, 128), jnp.float32)
    sums = lax.fori_loop(0, used, step, (zero,) * (2 * count))
    line = lax.broadcasted_iota(jnp.int32, (count, 128), 0)
    halves = []
    for half in range(2):
        total = None
        for r in range(count):
            ones = jnp.where(line == r, 1.0, 0.0).astype(jnp.bfloat16)
            term = weights_times_back(ones, sums[half * count + r])
            total = term if total is None else total + term
        halves.append(total)
    own, lower = halves
    pair_out[...] = own

    def against(matrix):
        return product_back(own, matrix[:, :top_size]) + product_back(lower, matrix[:, top_size:])

    second_rows, first_rows = second_own.shape[1], first_own.shape[1]
    second_gap[...] = second_own[...] - against(
        pack[SECOND_TOP : SECOND_TOP + second_rows, 0 : 2 * top_size]
    )
    first_gap[...] = first_own[...] - against(
        pack[FIRST_TOP : FIRST_TOP + first_rows, 0 : 2 * top_size]
    )
    rows = pack[TO_TOP : TO_TOP + 2 * top_size, 0 : leaf_solved.shape[1]]
    leaf_gap[...] = leaf_solved[...] - (
        product(own, rows[:top_size]) + product(lower, rows[top_size:])
    )


def second_back_body(
    sizes, side, whole, second, below, first_gap, leaf_gap, top_back, pack, sent, base_out,
    second_out,
):
    count = whole.shape[0]
    leaf_size, first_size, second_size, _ = sizes
    reach = side * 8
    own = product_back(whole[...], second[0:second_size, :])
    lower = product_back(whole[...], below[0:second_size, :])
    second_out[...] = own
    weights = pack[FIRST_SECOND : FIRST_SECOND + first_size, 0 : 2 * second_size]
    gap = first_gap[...] - product_back(own, weights[:, :second_size])
    gap = gap - product_back(lower, weights[:, second_size:])
    rows = pack[TO_SECOND : TO_SECOND + 2 * second_size, 0:leaf_size]
    rest = leaf_gap[...] - product(own, rows[:second_size]) - product(lower, rows[second_size:])
    base = product_back(rest, pack[LEAF : LEAF + leaf_size, 0:leaf_size])
    base_out[...] = base
    leaf_order, _, second_order, top_order = packed_order(pack, sizes)
    number = numbers(side, "out")
    face = times_weights_back(base, one_hot(number, leaf_order))
    face = face + times_weights_back(own, one_hot(number, second_order))
    face = face + times_weights_back(top_back[...], one_hot(number, top_order))
    sent[...] = jnp.zeros_like(sent)
    sent[0:count, 0:first_size] = gap
    sent[count : 2 * count, 0:reach] = face


def leaf_back_body(
    sizes, side, received, base, second_back, top_back, pack, first, below, above, window,
):
    count = base.shape[0]
    peers = received.shape[0]
    leaf_size, first_size, _, _ = sizes
    reach = side * 8
    whole = jnp.concatenate([received[p, 0:count, 0:first_size] for p in range(peers)], axis=1)
    total = whole.shape[1]
    own = product_back(whole, first[0:first_size, 0:total])
    lower = product_back(whole, below[0:first_size, 0:total])
    following = product_back(whole, above[0:first_size, 0:total])
    rows = pack[TO_FIRST : TO_FIRST + 2 * first_size, 0:leaf_size]
    rest = product(own, rows[:first_size]) + product(lower, rows[first_size:])
    leaf_back = base[...] - product_back(rest, pack[LEAF : LEAF + leaf_size, 0:leaf_size])
    face = jnp.zeros((count, reach), jnp.float32)
    place = lax.axis_index("gz") + 1
    for p in range(peers):
        face = face + jnp.where(place == p, received[p, count : 2 * count, 0:reach], 0.0)
    through = above[:, total : total + 2 * first_size]
    moved = product_back(following, through[:, :first_size])
    moved = moved + product_back(own, through[:, first_size:])
    lane = lax.broadcasted_iota(jnp.int32, (through.shape[0], reach), 0)
    other = lax.broadcasted_iota(jnp.int32, (through.shape[0], reach), 1)
    shift = jnp.where(lane == other + 9, 1.0, 0.0)
    face = face - times_weights(moved, shift.astype(jnp.bfloat16))
    orders = packed_order(pack, sizes)
    number = numbers(side, "out")
    layers = []
    for z in range(side):
        layer = times_weights_back(leaf_back, one_hot(number + float(z), orders[0]))
        layer = layer + times_weights_back(
            second_back[...], one_hot(number + float(z), orders[2])
        )
        layer = layer + times_weights_back(top_back[...], one_hot(number + float(z), orders[3]))
        if z == side - 1:
            layer = layer + times_weights_back(own, one_hot(number + float(z), orders[1]))
        layers.append(layer)
    layers.append(face)
    layers.append(jnp.zeros_like(face))
    cells = jnp.concatenate(layers, axis=0)
    turned = weights_times_back(eye(reach), cells)
    window[...] = turned.reshape(window.shape)


def tent(at, cell):
    distance = jnp.abs(at - 4 * cell).astype(jnp.float32)
    return jnp.maximum(1.0 - 0.25 * distance, 0.0)


def prolong_body(inner, after_x, after_y, target, out, sent):
    count, fine = out.shape[:2]
    copies = []
    cells = inner.shape[0] + 1
    window = jnp.concatenate([inner[...], after_x[...][None]], axis=0)
    row = lax.broadcasted_iota(jnp.int32, window.shape, 1)
    window = jnp.where(row == cells - 1, after_y[...][:, None, :], window)
    flat = window.reshape(cells * window.shape[1], window.shape[2])
    rows = lax.broadcasted_iota(jnp.int32, (cells * fine, cells * 8), 0)
    columns = lax.broadcasted_iota(jnp.int32, (cells * fine, cells * 8), 1)
    at = rows - (columns >> 3) * fine
    inside = (at >= 0) & (at < fine) & ((columns & 7) < cells)
    y_weights = jnp.where(inside, tent(at, columns & 7), 0.0).astype(jnp.bfloat16)
    along_y = weights_times(y_weights, flat)
    lane = lax.broadcasted_iota(jnp.int32, (window.shape[2], fine), 0)
    at = lax.broadcasted_iota(jnp.int32, (window.shape[2], fine), 1)
    for r in range(count):
        inside = ((lane & 3) == r) & ((lane >> 2) < cells)
        z_weights = jnp.where(inside, tent(at, lane >> 2), 0.0).astype(jnp.bfloat16)
        along_z = times_weights(along_y, z_weights)
        planes = [along_z[i * fine : (i + 1) * fine] for i in range(cells)]
        for i in range(cells - 1):
            for q in range(4):
                value = planes[i]
                if q:
                    value = (1.0 - q / 4.0) * value + (q / 4.0) * planes[i + 1]
                out[r, 4 * i + q] = value
        copies.append(pltpu.make_async_copy(out.at[r], target.at[r], sent.at[r]))
        copies[r].start()
    for copy in copies:
        copy.wait()


def prolonged(inner, after_x, after_y, count, fine):
    return pl.pallas_call(
        prolong_body,
        out_shape=jax.ShapeDtypeStruct((count, fine, fine, fine), jnp.float32),
        in_specs=[VMEM] * 3,
        out_specs=HBM,
        scratch_shapes=[
            pltpu.VMEM((count, fine, fine, fine), jnp.float32),
            pltpu.SemaphoreType.DMA((count,)),
        ],
        compiler_params=LIMIT,
        name="prolong_twice",
    )(inner, after_x, after_y)


def padded(values, dim, before, after):
    widths = [(0, 0)] * values.ndim
    widths[dim] = (before, after)
    return jnp.pad(values, widths)


def call(body, outs, *operands):
    shapes = tuple(jax.ShapeDtypeStruct(o, jnp.float32) for o in outs)
    return pl.pallas_call(
        body,
        out_shape=shapes,
        in_specs=[VMEM] * len(operands),
        out_specs=(VMEM,) * len(shapes),
        compiler_params=LIMIT,
    )(*operands)


def per_device(
    right_side,
    iterate,
    coefficient,
    ordering,
    leaf_inverse,
    leaf_first,
    leaf_second,
    leaf_top,
    first_inverse,
    first_second,
    first_top,
    second_inverse,
    second_top,
    top_inverse,
):
    count, fine = right_side.shape[:2]
    leaf_size = leaf_inverse.shape[-1]
    first_size = first_second.shape[3]
    second_size = second_top.shape[3]
    top_size, top_total = top_inverse.shape
    sizes = (leaf_size, first_size, second_size, top_size)
    side = fine // 4
    cells = side**3
    lanes = (side + 2) * count
    gz = lax.axis_size("gz")
    plane_peers = lax.axis_size(PLANE)

    def rows_of(block):
        return jnp.transpose(block, (0, 1, 3, 2, 4)).reshape(block.shape[3], 1, block.shape[4])

    def columns_of(block):
        return jnp.transpose(block, (0, 1, 4, 2, 3)).reshape(block.shape[4], 1, block.shape[3])

    leaf = rows_of(leaf_inverse)
    to_first = columns_of(leaf_first)
    to_second = columns_of(leaf_second)
    to_top = jnp.swapaxes(leaf_top[0, 0, 0], 0, 1)
    first_to_second = rows_of(first_second)
    first_to_top = rows_of(first_top)
    second_to_top = rows_of(second_top)
    first = jnp.transpose(first_inverse, (0, 2, 1, 3)).reshape(first_size, 1, -1)
    second = jnp.transpose(second_inverse, (1, 0, 2))
    order = ordering.reshape(1, cells)

    inner, upper = restricted(order, right_side, iterate, coefficient)
    from_x = shifted(upper, "gx", 1)
    whole_first = -(-max(first.shape[2] + 2 * first_size, cells) // 128) * 128
    up, down, beside, pack = prepared(
        sizes,
        side,
        whole_first,
        order,
        leaf,
        to_first,
        first,
        second,
        to_second,
        to_top,
        first_to_second,
        first_to_top,
        second_to_top,
    )
    first_below = shifted(up, "gz", 1)
    first_above = shifted(down, "gz", -1)
    second_below = shifted(beside, "gy", 1)
    top_below = shifted(top_inverse, "gx", 1)
    last = side + 1
    row = inner[:, last] + padded(from_x[last : last + 1, :lanes], 0, 1, side - 1)
    from_y = shifted(row, "gy", 1)

    turned, pieces = call(
        functools.partial(first_body, sizes, side, first.shape[2]),
        [(lanes, lanes_of(side)), (gz, 4 * count, 128)],
        inner,
        from_x,
        from_y,
        pack,
        up,
        first_below,
        first_above,
    )
    pieces, second_below = lax.optimization_barrier((pieces, second_below))
    received = exchanged(pieces, "gz")
    pieces, leaf_solved, first_own, toward, top_rhs = call(
        functools.partial(second_body, sizes, side, gz),
        [
            (plane_peers, 2 * count, 128),
            (count, leaf_size),
            (count, first_size),
            (count, 2 * top_size),
            (count, top_size),
        ],
        received,
        turned,
        from_x,
        pack,
        beside,
        second_below,
    )
    received = exchanged(pieces, PLANE)
    width = 128 * -(-top_total // (128 * plane_peers))
    used = top_total // width
    pieces, second_own = call(
        functools.partial(top_body, used),
        [(plane_peers, count, width), (count, second_size)],
        received,
        toward,
        top_rhs,
        pack,
        top_inverse,
        top_below,
    )
    received = exchanged(pieces, PLANE)
    (pieces,) = call(spread_sum_body, [(lax.axis_size("gx"), count, width)], received)
    received = exchanged(pieces, "gx")
    (pieces,) = call(spread_sum_body, [(plane_peers, count, width)], received)
    received = exchanged(pieces, PLANE)
    top_back, second_gap, first_gap, leaf_gap = call(
        functools.partial(top_back_body, used),
        [(count, top_size), (count, second_size), (count, first_size), (count, leaf_size)],
        received,
        top_inverse,
        top_below,
        second_own,
        first_own,
        leaf_solved,
        pack,
    )
    second_whole = jnp.moveaxis(sent_to_all(second_gap, PLANE), 0, 1).reshape(count, -1)
    sent, base, second_back = call(
        functools.partial(second_back_body, sizes, side),
        [(2 * count, 128), (count, leaf_size), (count, second_size)],
        second_whole,
        beside,
        second_below,
        first_gap,
        leaf_gap,
        top_back,
        pack,
    )
    received = sent_to_all(sent, "gz")
    (window,) = call(
        functools.partial(leaf_back_body, sizes, side),
        [(side, 8, lanes)],
        received,
        base,
        second_back,
        top_back,
        pack,
        up,
        first_below,
        first_above,
    )
    after_x = shifted(window[0], "gx", -1)
    layer = jnp.concatenate([window[:, 0], after_x[0:1]], axis=0)
    after_y = shifted(layer, "gy", -1)
    return prolonged(window, after_x, after_y, count, fine)


def solution(mesh):
    blocks = P("gx", "gy", "gz")
    return jax.shard_map(
        per_device,
        mesh=mesh,
        in_specs=(
            P(None, "gx", "gy", "gz"),
            P(None, "gx", "gy", "gz"),
            blocks,
            blocks,
            blocks,
            blocks,
            blocks,
            blocks,
            blocks,
            blocks,
            blocks,
            P("gx", PLANE, None),
            blocks,
            P(("gx", "gy", "gz"), None),
        ),
        out_specs=P(None, "gx", "gy", "gz"),
        check_vma=False,
    )
```

time: 157 us -> 150 us (0.955)
  local copies, waits for them, and re-layouts: 13.5 us -> 1.71 us
  blocking collectives: 74.4 us -> 85.9 us
  starting transfers between devices: 31.5 us -> 23.2 us
  Pallas kernels: 14.8 us -> 18.7 us
  waiting for transfers between devices: 20.5 us -> 18.6 us
    unnamed x59 -> x25, local copies, waits for them, and re-layouts: 13.3 us -> 0.8 us
    all_to_all x6 -> x7, blocking collectives: 74.4 us -> 85.9 us  [exchanged(): return lax.all_to_all(pieces, axis, split_axis=0, concat_axis=0, tiled=True)]
    all_to_all x1 -> x0, starting transfers between devices: 7 us -> none  [exchanged(): return lax.all_to_all(pieces, axis, split_axis=0, concat_axis=0, tiled=True)]
    all_to_all x1 -> x0, waiting for transfers between devices: 4.85 us -> none  [exchanged(): return lax.all_to_all(pieces, axis, split_axis=0, concat_axis=0, tiled=True)]
    pallas_call x10, Pallas kernels: 13.1 us -> 17.2 us  [the longest x8 11.7 us: call(): pl.pallas_call(body, out_shape=shapes, in_specs=[VMEM] * len(operands), o...]
    ppermute x9 -> x8, waiting for transfers between devices: 15.6 us -> 18.6 us  [shifted(): return lax.ppermute(shard, axis, pairs)]
    ppermute x9 -> x8, starting transfers between devices: 24.5 us -> 23.2 us  [shifted(): return lax.ppermute(shard, axis, pairs)]
  transfers between devices with their start and end apart: 10 -> 8, of which waited for: 5 -> 4; matrix products, arithmetic and copies ran while one was open for 0% -> 1% of each run, Pallas kernels for 4% -> 5%
where the time goes in v4:
time: 150 us; the launch traced here: 148 us
  blocking collectives  85.9 us (57%)
  starting transfers between devices  23.2 us (15%)
  Pallas kernels  18.7 us (12%)
  waiting for transfers between devices  18.6 us (12%)
  local copies, waits for them, and re-layouts  1.71 us (1%)
    all_to_all x7, blocking collectives, exchanged(): return lax.all_to_all(pieces, axis, split_axis=0, concat_axis=0, tiled=True)  85.9 us
    ppermute x8, starting transfers between devices, shifted(): return lax.ppermute(shard, axis, pairs)  23.2 us
    ppermute x8, waiting for transfers between devices, shifted(): return lax.ppermute(shard, axis, pairs)  18.6 us
    pallas_call x8, Pallas kernels, call(): pl.pallas_call(body, out_shape=shapes, in_specs=[VMEM] * len(operands), o...  11.7 us
    pallas_call x1, Pallas kernels, restricted(): pl.pallas_call(body, out_shape=(inner, upper), in_specs=[VMEM] + [HBM] *...  4.22 us
  transfers between devices with their start and end apart: 8, of which 4 were waited for; matrix products, arithmetic and copies ran while one was open for 1% of the time, Pallas kernels for 5%

profile of v4, /device:TPU:1, one launch (start us, length us, event | category | flops | bytes accessed | tf_op | source)
XLA Modules:
  0.0 148.5 jit_solution(6790855829627067219)
XLA Ops:
  0.0 5.5 %collective-permute-start.5 = (f32[36,9216]{1,0:T(8,128)}, f32[36,9216]{1,0:T(8,128)}, u32[]{:S(2)}, u32[]{:S(2)}) collective-permute-start(f32[36,9216]{1,0:T(8,128)} %top.3), channel_id=1, source_target_pairs={{0,32},{32,64},{64,96},{96,128},{128,160},{160,192},{192,224},{1,3... | collective-permute-start | bytes 3981320 | tf_op jit(solution)/shard_map/ppermute | solution.py:23
  5.5 0.0 copy-start.1
  5.5 0.0 copy-start.3
  5.5 0.0 copy-start.4
  5.5 0.0 copy-start.5
  5.5 0.0 copy-start.6
  5.5 0.0 copy-start.7
  5.5 0.0 copy-start.8
  5.5 0.0 copy-start.9
  5.5 0.0 copy-start.10
  5.6 0.0 copy-start.11
  5.6 4.2 %restrict_twice.1 = (f32[7,8,32]{2,1,0:T(8,128)}, f32[16,128]{1,0:T(8,128)}) custom-call(s32[1,216]{1,0:T(1,128)} %bitcast.35, f32[4,24,24,24]{3,2,1,0:T(8,128)} %refs_1_.1, f32[4,24,24,24]{3,2,1,0:T(8,128)} %refs_2_.1, f32[24,24,24]{2,1,0:T(8,128)} %refs_3_.1), custom_call_target="tpu_custom_call" | custom-call | tf_op jit(solution)/shard_map/restrict_twice/pallas_call | solution.py:203
  9.8 0.0 copy-start
  9.8 2.6 %collective-permute-start = (f32[16,128]{1,0:T(8,128)}, f32[16,128]{1,0:T(8,128)S(1)}, u32[]{:S(2)}, u32[]{:S(2)}) collective-permute-start(f32[16,128]{1,0:T(8,128)} %get-tuple-element.30), channel_id=1, source_target_pairs={{0,32},{32,64},{64,96},{96,128},{128,160},{160,192},{192,224},{1,3... | collective-permute-start | bytes 24584 | tf_op jit(solution)/shard_map/ppermute | solution.py:23
  12.4 0.0 copy-done.1
  12.4 0.0 copy-done.3
  12.4 0.0 copy-done.4
  12.4 0.0 copy-done.5
  12.4 0.0 copy-done.6
  12.4 0.0 copy-done.7
  12.4 0.0 copy-done.8
  12.5 0.0 copy-done.9
  12.5 0.0 copy-done.10
  12.5 0.0 copy-done.11
  12.5 1.3 prepare.1
  13.8 4.2 %collective-permute-start.2 = (f32[32,256]{1,0:T(8,128)S(1)}, f32[32,256]{1,0:T(8,128)S(1)}, u32[]{:S(2)}, u32[]{:S(2)}) collective-permute-start(f32[32,256]{1,0:T(8,128)S(1)} %get-tuple-element.32.first), channel_id=1, source_target_pairs={{0,1},{1,2},{2,3},{3,4},{4,5},{5,6},{6,7},{8,9},{9,10},{10,11},{11... | collective-permute-start | bytes 98312 | tf_op jit(solution)/shard_map/ppermute | solution.py:23
  18.0 1.9 %collective-permute-start.3 = (f32[56,256]{1,0:T(8,128)S(1)}, f32[56,256]{1,0:T(8,128)S(1)}, u32[]{:S(2)}, u32[]{:S(2)}) collective-permute-start(f32[56,256]{1,0:T(8,128)S(1)} %get-tuple-element.33), channel_id=1, source_target_pairs={{1,0},{2,1},{3,2},{4,3},{5,4},{6,5},{7,6},{9,8},{10,9},{11,10},{12... | collective-permute-start | bytes 172040 | tf_op jit(solution)/shard_map/ppermute | solution.py:23
  19.9 3.2 %collective-permute-start.4 = (f32[32,960]{1,0:T(8,128)S(1)}, f32[32,960]{1,0:T(8,128)S(1)}, u32[]{:S(2)}, u32[]{:S(2)}) collective-permute-start(f32[32,960]{1,0:T(8,128)S(1)} %get-tuple-element.35.second), channel_id=1, source_target_pairs={{0,8},{8,16},{16,24},{1,9},{9,17},{17,25},{2,10},{10,18},{18,26},{... | collective-permute-start | bytes 368648 | tf_op jit(solution)/shard_map/ppermute | solution.py:23
  23.2 0.8 copy.19
  23.9 11.8 %collective-permute-done.from_x = f32[16,128]{1,0:T(8,128)S(1)} collective-permute-done((f32[16,128]{1,0:T(8,128)}, f32[16,128]{1,0:T(8,128)S(1)}, u32[]{:S(2)}, u32[]{:S(2)}) %collective-permute-start) | collective-permute-done | bytes 8224 | tf_op jit(solution)/shard_map/ppermute | solution.py:23
  35.7 3.2 %collective-permute-start.1 = (f32[7,32]{1,0:T(8,128)S(1)}, f32[7,32]{1,0:T(8,128)S(1)}, u32[]{:S(2)}, u32[]{:S(2)}) collective-permute-start(f32[7,32]{1,0:T(8,128)S(1)} %fusion), channel_id=1, source_target_pairs={{0,8},{8,16},{16,24},{1,9},{9,17},{17,25},{2,10},{10,18},{18,26},{... | collective-permute-start | bytes 2696 | tf_op jit(solution)/shard_map/ppermute | solution.py:23
  38.9 0.7 collective-permute-done.1.from_y
  39.7 0.0 collective-permute-done.2.below
  39.7 0.0 collective-permute-done.3.above
  39.7 0.0 copy-start.2
  39.7 0.7 copy-done.2
  40.4 1.1 shard_map.136
  41.6 0.0 collective-permute-done.4.below
  41.6 11.4 %all_to_all.35.received = f32[8,16,128]{2,1,0:T(8,128)S(1)} all-to-all(f32[8,16,128]{2,1,0:T(8,128)S(1)} %get-tuple-element.36), channel_id=1, replica_groups=mesh['gx'=8,'gy'=4,'gz'=8] {'gz'}, dimensions={0} | all-to-all | bytes 131072 | tf_op jit(solution)/shard_map/all_to_all | solution.py:27
  52.9 1.5 %shard_map.137 = (f32[32,8,128]{2,1,0:T(8,128)S(1)}, f32[4,125]{1,0:T(4,128)S(1)}, f32[4,25]{1,0:T(4,128)S(1)}, f32[4,72]{1,0:T(4,128)S(1)}, f32[4,36]{1,0:T(4,128)S(1)}) custom-call(f32[8,16,128]{2,1,0:T(8,128)S(1)} %all_to_all.35.received, f32[32,56]{1,0:T(8,128)S(1)} %get-tuple-element.37.cells, f32[16,128]{1,0:T(8,128)S(1)} %collective-permute-done.from_x, ...), custom_call_target="tpu_custom_call" | custom-call | tf_op jit(solution)/shard_map/pallas_call | solution.py:658
  54.4 14.1 %all_to_all.36.received = f32[32,8,128]{2,1,0:T(8,128)S(1)} all-to-all(f32[32,8,128]{2,1,0:T(8,128)S(1)} %get-tuple-element.39), channel_id=1, replica_groups=mesh['gx'=8,'gy'=4,'gz'=8] {'gy','gz'}, dimensions={0} | all-to-all | bytes 262144 | tf_op jit(solution)/shard_map/all_to_all | solution.py:27
  68.5 0.0 collective-permute-done.5.below
  68.5 0.0 copy-done
  68.5 3.6 %shard_map.138 = (f32[32,4,384]{2,1,0:T(4,128)S(1)}, f32[4,30]{1,0:T(4,128)S(1)}) custom-call(f32[32,8,128]{2,1,0:T(8,128)S(1)} %all_to_all.36.received, f32[4,72]{1,0:T(4,128)S(1)} %get-tuple-element.40.toward, f32[4,36]{1,0:T(4,128)S(1)} %get-tuple-element.41.rhs, f32[424,128]{1,0:T(8,128)S(1)} %get-tuple-element.31.pack, f32[36,9216]{1,0:T(8,128)S(1)} %copy-done, ...), custom_call_target="tpu_custom_call" | custom-call | tf_op jit(solution)/shard_map/pallas_call | solution.py:658
  72.2 11.9 %all_to_all.37.received = f32[32,4,384]{2,1,0:T(4,128)S(1)} all-to-all(f32[32,4,384]{2,1,0:T(4,128)S(1)} %get-tuple-element.42), channel_id=1, replica_groups=mesh['gx'=8,'gy'=4,'gz'=8] {'gy','gz'}, dimensions={0} | all-to-all | bytes 393216 | tf_op jit(solution)/shard_map/all_to_all | solution.py:27
  84.1 16.8 %all_to_all.38.received = f32[8,4,384]{2,1,0:T(4,128)S(1)} all-to-all(f32[8,4,384]{2,1,0:T(4,128)S(1)} %shard_map.139), channel_id=1, replica_groups=mesh['gx'=8,'gy'=4,'gz'=8] {'gx'}, dimensions={0} | all-to-all | bytes 98304 | tf_op jit(solution)/shard_map/all_to_all | solution.py:27
  101.0 13.3 %all_to_all.39.whole = f32[32,4,384]{2,1,0:T(4,128)S(1)} all-to-all(f32[32,4,384]{2,1,0:T(4,128)S(1)} %shard_map.140), channel_id=1, replica_groups=mesh['gx'=8,'gy'=4,'gz'=8] {'gy','gz'}, dimensions={0} | all-to-all | bytes 393216 | tf_op jit(solution)/shard_map/all_to_all | solution.py:27
  114.2 3.1 %shard_map.141 = (f32[4,36]{1,0:T(4,128)S(1)}, f32[4,30]{1,0:T(4,128)S(1)}, f32[4,25]{1,0:T(4,128)S(1)}, f32[4,125]{1,0:T(4,128)S(1)}) custom-call(f32[32,4,384]{2,1,0:T(4,128)S(1)} %all_to_all.39.whole, f32[36,9216]{1,0:T(8,128)S(1)} %copy-done, f32[36,9216]{1,0:T(8,128)} %collective-permute-done.5.below, f32[4,30]{1,0:T(4,128)S(1)} %get-tuple-element.43.second_own, ...), custom_call_target="tpu_custom_call" | custom-call | tf_op jit(solution)/shard_map/pallas_call | solution.py:658
  117.3 10.9 %all_to_all.40 = f32[32,4,30]{2,1,0:T(4,128)S(1)} all-to-all(f32[32,4,30]{2,1,0:T(4,128)S(1)} %broadcast_in_dim.6), channel_id=1, replica_groups=mesh['gx'=8,'gy'=4,'gz'=8] {'gy','gz'}, dimensions={0} | all-to-all | bytes 30720 | tf_op jit(solution)/shard_map/all_to_all | solution.py:27
  128.3 0.1 reshape.15.whole
  128.4 1.0 shard_map.142
  129.4 7.5 %all_to_all.41.received = f32[8,8,128]{2,1,0:T(8,128)S(1)} all-to-all(f32[8,8,128]{2,1,0:T(8,128)S(1)} %broadcast_in_dim.7), channel_id=1, replica_groups=mesh['gx'=8,'gy'=4,'gz'=8] {'gz'}, dimensions={0} | all-to-all | bytes 65536 | tf_op jit(solution)/shard_map/all_to_all | solution.py:27
  136.9 1.3 shard_map.143.inner
  138.2 1.3 collective-permute-start.6
  139.5 3.0 %collective-permute-done.6.after_x = f32[8,32]{1,0:T(8,128)S(1)} collective-permute-done((f32[8,32]{1,0:T(8,128)S(1)}, f32[8,32]{1,0:T(8,128)S(1)}, u32[]{:S(2)}, u32[]{:S(2)}) %collective-permute-start.6) | collective-permute-done | bytes 1056 | tf_op jit(solution)/shard_map/ppermute | solution.py:23
  142.6 1.3 collective-permute-start.7
  143.9 3.1 %collective-permute-done.7.after_y = f32[7,32]{1,0:T(8,128)S(1)} collective-permute-done((f32[7,32]{1,0:T(8,128)S(1)}, f32[7,32]{1,0:T(8,128)S(1)}, u32[]{:S(2)}, u32[]{:S(2)}) %collective-permute-start.7) | collective-permute-done | bytes 928 | tf_op jit(solution)/shard_map/ppermute | solution.py:23
  146.9 1.5 %prolong_twice.1 = f32[4,24,24,24]{3,2,1,0:T(8,128)} custom-call(f32[6,8,32]{2,1,0:T(8,128)S(1)} %shard_map.143.inner, f32[8,32]{1,0:T(8,128)S(1)} %collective-permute-done.6.after_x, f32[7,32]{1,0:T(8,128)S(1)} %collective-permute-done.7.after_y), custom_call_target="tpu_custom_call" | custom-call | tf_op jit(solution)/shard_map/prolong_twice/pallas_call | solution.py:636
  (12 shorter events, 0.1 us)
Async XLA Ops:
  0.0 68.5 %collective-permute-start.5 = (f32[36,9216]{1,0:T(8,128)}, f32[36,9216]{1,0:T(8,128)}, u32[]{:S(2)}, u32[]{:S(2)}) collective-permute-start(f32[36,9216]{1,0:T(8,128)} %top.3), channel_id=1, source_target_pairs={{0,32},{32,64},{64,96},{96,128},{128,160},{160,192},{192,224},{1,3... | collective-permute-start | bytes 3981320 | tf_op jit(solution)/shard_map/ppermute | solution.py:23
  5.5 6.9 %copy-start.1 = (f32[1,30,960]{2,0,1:T(1,128)S(1)}, f32[1,30,960]{2,0,1:T(1,128)}, u32[]{:S(2)}) copy-start(f32[1,30,960]{2,0,1:T(1,128)} %param.25) | copy-start | bytes 345604
  5.5 6.9 %copy-start.3 = (f32[1,1,1,125,125]{4,2,3,1,0:T(1,128)S(1)}, f32[1,1,1,125,125]{4,2,3,1,0:T(1,128)}, u32[]{:S(2)}) copy-start(f32[1,1,1,125,125]{4,2,3,1,0:T(1,128)} %param.18) | copy-start | bytes 187504
  5.5 6.9 %copy-start.4 = (f32[1,1,1,125,72]{3,4,2,1,0:T(8,128)S(1)}, f32[1,1,1,125,72]{3,4,2,1,0:T(8,128)}, u32[]{:S(2)}) copy-start(f32[1,1,1,125,72]{3,4,2,1,0:T(8,128)} %param.21) | copy-start | bytes 108004
  5.5 6.9 %copy-start.5 = (f32[1,1,1,125,60]{3,2,4,1,0:T(1,128)S(1)}, f32[1,1,1,125,60]{3,2,4,1,0:T(1,128)}, u32[]{:S(2)}) copy-start(f32[1,1,1,125,60]{3,2,4,1,0:T(1,128)} %param.20) | copy-start | bytes 90004
  5.5 6.9 %copy-start.6 = (f32[1,1,1,125,50]{3,2,4,1,0:T(1,128)S(1)}, f32[1,1,1,125,50]{3,2,4,1,0:T(1,128)}, u32[]{:S(2)}) copy-start(f32[1,1,1,125,50]{3,2,4,1,0:T(1,128)} %param.19) | copy-start | bytes 75004
  5.5 6.9 %copy-start.7 = (f32[1,1,25,200]{3,1,2,0:T(1,128)S(1)}, f32[1,1,25,200]{3,1,2,0:T(1,128)}, u32[]{:S(2)}) copy-start(f32[1,1,25,200]{3,1,2,0:T(1,128)} %param.22) | copy-start | bytes 60004
  5.5 6.9 %copy-start.8 = (f32[1,1,1,30,72]{4,2,3,1,0:T(1,128)S(1)}, f32[1,1,1,30,72]{4,2,3,1,0:T(1,128)}, u32[]{:S(2)}) copy-start(f32[1,1,1,30,72]{4,2,3,1,0:T(1,128)} %param.26) | copy-start | bytes 25924
  5.5 6.9 %copy-start.9 = (f32[1,1,1,25,60]{4,2,3,1,0:T(1,128)S(1)}, f32[1,1,1,25,60]{4,2,3,1,0:T(1,128)}, u32[]{:S(2)}) copy-start(f32[1,1,1,25,60]{4,2,3,1,0:T(1,128)} %param.23) | copy-start | bytes 18004
  5.5 6.9 %copy-start.10 = (f32[1,1,1,25,72]{4,2,3,1,0:T(1,128)S(1)}, f32[1,1,1,25,72]{4,2,3,1,0:T(1,128)}, u32[]{:S(2)}) copy-start(f32[1,1,1,25,72]{4,2,3,1,0:T(1,128)} %param.24) | copy-start | bytes 21604
  5.6 6.9 %copy-start.11 = (s32[1,1,1,216]{3,2,1,0:T(1,128)S(1)}, s32[1,1,1,216]{3,2,1,0:T(1,128)}, u32[]{:S(2)}) copy-start(s32[1,1,1,216]{3,2,1,0:T(1,128)} %param.17) | copy-start | bytes 2596
  9.8 58.7 %copy-start = (f32[36,9216]{1,0:T(8,128)S(1)}, f32[36,9216]{1,0:T(8,128)}, u32[]{:S(2)}) copy-start(f32[36,9216]{1,0:T(8,128)} %top.3) | copy-start | bytes 3981316
  9.8 25.9 %collective-permute-start = (f32[16,128]{1,0:T(8,128)}, f32[16,128]{1,0:T(8,128)S(1)}, u32[]{:S(2)}, u32[]{:S(2)}) collective-permute-start(f32[16,128]{1,0:T(8,128)} %get-tuple-element.30), channel_id=1, source_target_pairs={{0,32},{32,64},{64,96},{96,128},{128,160},{160,192},{192,224},{1,3... | collective-permute-start | bytes 24584 | tf_op jit(solution)/shard_map/ppermute | solution.py:23
  13.8 25.9 %collective-permute-start.2 = (f32[32,256]{1,0:T(8,128)S(1)}, f32[32,256]{1,0:T(8,128)S(1)}, u32[]{:S(2)}, u32[]{:S(2)}) collective-permute-start(f32[32,256]{1,0:T(8,128)S(1)} %get-tuple-element.32.first), channel_id=1, source_target_pairs={{0,1},{1,2},{2,3},{3,4},{4,5},{5,6},{6,7},{8,9},{9,10},{10,11},{11... | collective-permute-start | bytes 98312 | tf_op jit(solution)/shard_map/ppermute | solution.py:23
  18.0 21.7 %collective-permute-start.3 = (f32[56,256]{1,0:T(8,128)S(1)}, f32[56,256]{1,0:T(8,128)S(1)}, u32[]{:S(2)}, u32[]{:S(2)}) collective-permute-start(f32[56,256]{1,0:T(8,128)S(1)} %get-tuple-element.33), channel_id=1, source_target_pairs={{1,0},{2,1},{3,2},{4,3},{5,4},{6,5},{7,6},{9,8},{10,9},{11,10},{12... | collective-permute-start | bytes 172040 | tf_op jit(solution)/shard_map/ppermute | solution.py:23
  19.9 21.6 %collective-permute-start.4 = (f32[32,960]{1,0:T(8,128)S(1)}, f32[32,960]{1,0:T(8,128)S(1)}, u32[]{:S(2)}, u32[]{:S(2)}) collective-permute-start(f32[32,960]{1,0:T(8,128)S(1)} %get-tuple-element.35.second), channel_id=1, source_target_pairs={{0,8},{8,16},{16,24},{1,9},{9,17},{17,25},{2,10},{10,18},{18,26},{... | collective-permute-start | bytes 368648 | tf_op jit(solution)/shard_map/ppermute | solution.py:23
  35.7 3.9 %collective-permute-start.1 = (f32[7,32]{1,0:T(8,128)S(1)}, f32[7,32]{1,0:T(8,128)S(1)}, u32[]{:S(2)}, u32[]{:S(2)}) collective-permute-start(f32[7,32]{1,0:T(8,128)S(1)} %fusion), channel_id=1, source_target_pairs={{0,8},{8,16},{16,24},{1,9},{9,17},{17,25},{2,10},{10,18},{18,26},{... | collective-permute-start | bytes 2696 | tf_op jit(solution)/shard_map/ppermute | solution.py:23
  39.7 0.8 copy-start.2
  138.2 4.4 %collective-permute-start.6 = (f32[8,32]{1,0:T(8,128)S(1)}, f32[8,32]{1,0:T(8,128)S(1)}, u32[]{:S(2)}, u32[]{:S(2)}) collective-permute-start(f32[8,32]{1,0:T(8,128)S(1)} %slice_bitcast_fusion), channel_id=1, source_target_pairs={{32,0},{64,32},{96,64},{128,96},{160,128},{192,160},{224,192},{33,... | collective-permute-start | bytes 3080 | tf_op jit(solution)/shard_map/ppermute | solution.py:23
  142.6 4.4 %collective-permute-start.7 = (f32[7,32]{1,0:T(8,128)S(1)}, f32[7,32]{1,0:T(8,128)S(1)}, u32[]{:S(2)}, u32[]{:S(2)}) collective-permute-start(f32[7,32]{1,0:T(8,128)S(1)} %pad_maximum_fusion), channel_id=1, source_target_pairs={{8,0},{16,8},{24,16},{9,1},{17,9},{25,17},{10,2},{18,10},{26,18},{... | collective-permute-start | bytes 2696 | tf_op jit(solution)/shard_map/ppermute | solution.py:23

commit v5 on v4

--- a/solution.py
+++ b/solution.py
@@ -10,11 +10,13 @@
 
 PLANE = ("gy", "gz")
 AXES = ("gx", "gy", "gz")
-precise = lax.Precision.HIGHEST
 VMEM = pl.BlockSpec(memory_space=pltpu.VMEM)
 HBM = pl.BlockSpec(memory_space=pltpu.HBM)
-FULL = pltpu.CompilerParams(vmem_limit_bytes=67043328 - 1000 * 1024)
 LIMIT = pltpu.CompilerParams(vmem_limit_bytes=16 * 1024 * 1024)
+
+
+def in_hbm(values):
+    return pltpu.with_memory_space_constraint(values, pltpu.HBM)
 
 
 def shifted(shard, axis, by):
@@ -32,18 +34,52 @@
     return exchanged(copies, axis)
 
 
+def parts_of(values):
+    first = values.astype(jnp.bfloat16)
+    second = (values - first.astype(jnp.float32)).astype(jnp.bfloat16)
+    return first, second
+
+
+def dot(left, right):
+    return jnp.dot(left, right, preferred_element_type=jnp.float32)
+
+
+def dot_back(left, right):
+    return lax.dot_general(
+        left, right, (((1,), (1,)), ((), ())), preferred_element_type=jnp.float32
+    )
+
+
 def product(operand, matrix):
-    return jnp.dot(operand, matrix, precision=precise, preferred_element_type=jnp.float32)
+    high, low = parts_of(operand)
+    first, second = parts_of(matrix)
+    return dot(high, first) + (dot(high, second) + dot(low, first))
 
 
 def product_back(operand, matrix):
-    return lax.dot_general(
-        operand,
-        matrix,
-        (((1,), (1,)), ((), ())),
-        precision=precise,
-        preferred_element_type=jnp.float32,
-    )
+    high, low = parts_of(operand)
+    first, second = parts_of(matrix)
+    return dot_back(high, first) + (dot_back(high, second) + dot_back(low, first))
+
+
+def times_weights(values, weights):
+    first, second = parts_of(values)
+    return dot(first, weights) + dot(second, weights)
+
+
+def weights_times(weights, values):
+    first, second = parts_of(values)
+    return dot(weights, first) + dot(weights, second)
+
+
+def times_weights_back(values, weights):
+    first, second = parts_of(values)
+    return dot_back(first, weights) + dot_back(second, weights)
+
+
+def weights_times_back(weights, values):
+    first, second = parts_of(values)
+    return dot_back(weights, first) + dot_back(weights, second)
 
 
 def two_restrictions(distance):
@@ -85,47 +121,9 @@
     return weight(cell - at - 1) + (1.0 - before) * weight(cell - at + 1)
 
 
-def parts_of(values):
-    first = values.astype(jnp.bfloat16)
-    rest = values - first.astype(jnp.float32)
-    second = rest.astype(jnp.bfloat16)
-    third = (rest - second.astype(jnp.float32)).astype(jnp.bfloat16)
-    return first, second, third
-
-
-def dot(left, right):
-    return jnp.dot(left, right, preferred_element_type=jnp.float32)
-
-
-def dot_back(left, right):
-    return lax.dot_general(
-        left, right, (((1,), (1,)), ((), ())), preferred_element_type=jnp.float32
-    )
-
-
-def times_weights_back(values, weights):
-    first, second, third = parts_of(values)
-    return dot_back(first, weights) + (dot_back(second, weights) + dot_back(third, weights))
-
-
-def weights_times_back(weights, values):
-    first, second, third = parts_of(values)
-    return dot_back(weights, first) + (dot_back(weights, second) + dot_back(weights, third))
-
-
-def times_weights(values, weights):
-    first, second, third = parts_of(values)
-    return dot(first, weights) + (dot(second, weights) + dot(third, weights))
-
-
-def weights_times(weights, values):
-    first, second, third = parts_of(values)
-    return dot(weights, first) + (dot(weights, second) + dot(weights, third))
-
-
 def restrict_body(
-    own, beside, before, order, rhs_in, iterate_in, coefficient_in, inner, upper,
-    rhs, iterate, coefficient, arrived,
+    own, beside, before, order_in, rhs_in, iterate_in, coefficient_in, inner, upper,
+    rhs, iterate, coefficient, order, arrived,
 ):
     count, fine = rhs.shape[:2]
     coarse = own.shape[0]
@@ -140,6 +138,7 @@
                         source.at[r, part], room.at[r, part], arrived.at[len(copies)]
                     )
                 )
+    copies.append(pltpu.make_async_copy(order_in, order, arrived.at[len(copies)]))
     for copy in copies:
         copy.start()
     at_x, at_y, at_z = [jnp.where(lax.axis_index(a) == 0, 1.0, 0.0) for a in AXES]
@@ -147,8 +146,6 @@
     top_size = coarse - 2
     top_size = top_size * top_size
     upper[...] = jnp.zeros_like(upper)
-    orders = order[...].astype(jnp.float32)
-    upper[layer : layer + 1, 0:top_size] = orders[:, orders.shape[1] - top_size :]
     y_cell = weight_rows(coarse, fine, "own", None)
     y_pair = weight_rows(coarse, fine, "beside", at_y)
     z_cells = [weight_lanes(coarse, fine, count, r, "own", None) for r in range(count)]
@@ -188,6 +185,9 @@
     result = result.reshape(coarse, coarse, coarse * count)
     inner[...] = result[:-1]
     upper[0:layer, 0:lanes] = result[coarse - 1]
+    copies[-1].wait()
+    orders = order[...].astype(jnp.float32)
+    upper[layer : layer + 1, 0:top_size] = orders[:, orders.shape[1] - top_size :]
 
 
 def restricted(order, right_side, iterate, coefficient):
@@ -203,17 +203,18 @@
     return pl.pallas_call(
         body,
         out_shape=(inner, upper),
-        in_specs=[VMEM] + [HBM] * 3,
+        in_specs=[HBM] * 4,
         out_specs=(VMEM,) * 2,
         scratch_shapes=[
             pltpu.VMEM(right_side.shape, jnp.float32),
             pltpu.VMEM(iterate.shape, jnp.float32),
             pltpu.VMEM(coefficient.shape, jnp.float32),
-            pltpu.SemaphoreType.DMA((4 * count + 1,)),
+            pltpu.VMEM(order.shape, order.dtype),
+            pltpu.SemaphoreType.DMA((4 * count + 2,)),
         ],
-        compiler_params=FULL,
+        compiler_params=LIMIT,
         name="restrict_twice",
-    )(order, right_side, iterate, coefficient)
+    )(*map(in_hbm, (order, right_side, iterate, coefficient)))
 
 
 def numbers(side, kind):
@@ -326,7 +327,7 @@
     shapes = (
         (32, width),
         (lanes_of(side), width),
-        (32, sources[4].shape[2]),
+        (40, sources[4].shape[2]),
         (PACKED, 128),
     )
     return pl.pallas_call(
@@ -339,6 +340,29 @@
         compiler_params=LIMIT,
         name="prepare",
     )(*sources)
+
+
+LAYER = 32
+
+
+def message_body(inner, from_x, _, message):
+    along, lanes = inner.shape[1:]
+    rows = inner[:, along - 1, :]
+    row = lax.broadcasted_iota(jnp.int32, rows.shape, 0)
+    rows = rows + jnp.where(row == 1, from_x[along - 1 : along, 0:lanes], 0.0)
+    message[LAYER : LAYER + rows.shape[0], 0:lanes] = rows
+
+
+def with_layer(inner, from_x, beside):
+    return pl.pallas_call(
+        message_body,
+        out_shape=jax.ShapeDtypeStruct(beside.shape, jnp.float32),
+        in_specs=[VMEM] * 3,
+        out_specs=VMEM,
+        input_output_aliases={2: 0},
+        compiler_params=LIMIT,
+        name="y_message",
+    )(inner, from_x, beside)
 
 
 def first_body(
@@ -355,7 +379,8 @@
     row = lax.broadcasted_iota(jnp.int32, values.shape, 0)
     values = values + jnp.where(row == 1, from_x[0:along, 0:lanes][None], 0.0)
     row = lax.broadcasted_iota(jnp.int32, values.shape, 1)
-    values = values + jnp.where(row == 1, from_y[...][:, None, :], 0.0)
+    layer = from_y[LAYER : LAYER + across, 0:lanes]
+    values = values + jnp.where(row == 1, layer[:, None, :], 0.0)
     cells = weights_times_back(eye(lanes), values.reshape(reach, lanes))
     cells_out[...] = cells
     number = numbers(side, "in")
@@ -456,9 +481,20 @@
     own = rhs[...] + total[count : 2 * count, 0:top_size] - toward[:, :top_size]
     other = toward[:, top_size:]
     width = pieces.shape[2]
+    vectors = []
+    for vector in (own, -other):
+        high, low = parts_of(vector)
+        both = jnp.concatenate([high.astype(jnp.float32), low.astype(jnp.float32)], axis=0)
+        vectors.append((both.astype(jnp.bfloat16), high))
     for p in range(used):
         at = slice(p * width, (p + 1) * width)
-        pieces[p] = product(own, top[:, at]) - product(other, below[:, at])
+        total = None
+        for (both, high), rows in zip(vectors, (top, below)):
+            first, second = parts_of(rows[:, at])
+            term = dot(both, first)
+            term = term[:count] + (term[count:] + dot(high, second))
+            total = term if total is None else total + term
+        pieces[p] = total
     for p in range(used, pieces.shape[0]):
         pieces[p] = jnp.zeros(pieces.shape[1:], jnp.float32)
 
@@ -647,12 +683,6 @@
     )(inner, after_x, after_y)
 
 
-def padded(values, dim, before, after):
-    widths = [(0, 0)] * values.ndim
-    widths[dim] = (before, after)
-    return jnp.pad(values, widths)
-
-
 def call(body, outs, *operands):
     shapes = tuple(jax.ShapeDtypeStruct(o, jnp.float32) for o in outs)
     return pl.pallas_call(
@@ -729,24 +759,21 @@
     )
     first_below = shifted(up, "gz", 1)
     first_above = shifted(down, "gz", -1)
+    top_below = shifted(top_inverse, "gx", 1)
+    beside = with_layer(inner, from_x, beside)
     second_below = shifted(beside, "gy", 1)
-    top_below = shifted(top_inverse, "gx", 1)
-    last = side + 1
-    row = inner[:, last] + padded(from_x[last : last + 1, :lanes], 0, 1, side - 1)
-    from_y = shifted(row, "gy", 1)
 
     turned, pieces = call(
         functools.partial(first_body, sizes, side, first.shape[2]),
         [(lanes, lanes_of(side)), (gz, 4 * count, 128)],
         inner,
         from_x,
-        from_y,
+        second_below,
         pack,
         up,
         first_below,
         first_above,
     )
-    pieces, second_below = lax.optimization_barrier((pieces, second_below))
     received = exchanged(pieces, "gz")
     pieces, leaf_solved, first_own, toward, top_rhs = call(
         functools.partial(second_body, sizes, side, gz),

time: 150 us -> 148 us (0.987)
  waiting for transfers between devices: 18.6 us -> 30.6 us
  Pallas kernels: 18.7 us -> 11.5 us
  starting transfers between devices: 23.2 us -> 20.6 us
  blocking collectives: 85.9 us -> 83.7 us
  local copies, waits for them, and re-layouts: 1.71 us -> 0.21 us
    ppermute x8 -> x7, waiting for transfers between devices: 18.6 us -> 30.6 us  [shifted(): return lax.ppermute(shard, axis, pairs)]
    pallas_call x8, Pallas kernels: 11.7 us -> 6.19 us  [call(): pl.pallas_call(body, out_shape=shapes, in_specs=[VMEM] * len(operands), o...]
    ppermute x8 -> x7, starting transfers between devices: 23.2 us -> 20.6 us  [shifted(): return lax.ppermute(shard, axis, pairs)]
    all_to_all x7, blocking collectives: 85.9 us -> 83.7 us  [exchanged(): return lax.all_to_all(pieces, axis, split_axis=0, concat_axis=0, tiled=True)]
    pallas_call x1 -> x2, Pallas kernels: 4.22 us -> 2.75 us  [the longest x1 2.75 us: restricted(): pl.pallas_call(body, out_shape=(inner, upper), in_specs=[HBM] * 4, out_sp...]
  transfers between devices with their start and end apart: 8 -> 7, of which waited for: 4 -> 4; matrix products, arithmetic and copies ran while one was open for 1% -> 0% of each run, Pallas kernels for 5% -> 4%
where the time goes in v5:
time: 148 us; the launch traced here: 147 us
  blocking collectives  83.7 us (57%)
  waiting for transfers between devices  30.6 us (21%)
  starting transfers between devices  20.6 us (14%)
  Pallas kernels  11.5 us (8%)
    all_to_all x7, blocking collectives, exchanged(): return lax.all_to_all(pieces, axis, split_axis=0, concat_axis=0, tiled=True)  83.7 us
    ppermute x7, waiting for transfers between devices, shifted(): return lax.ppermute(shard, axis, pairs)  30.6 us
    ppermute x7, starting transfers between devices, shifted(): return lax.ppermute(shard, axis, pairs)  20.6 us
    pallas_call x8, Pallas kernels, call(): pl.pallas_call(body, out_shape=shapes, in_specs=[VMEM] * len(operands), o...  6.19 us
  transfers between devices with their start and end apart: 7, of which 4 were waited for; matrix products, arithmetic and copies ran while one was open for 0% of the time, Pallas kernels for 4%

profile of v5, /device:TPU:1, one launch (start us, length us, event | category | flops | bytes accessed | tf_op | source)
XLA Modules:
  0.0 146.9 jit_solution(12386761314630336848)
XLA Ops:
  0.0 4.4 %collective-permute-start.4 = (f32[36,9216]{1,0:T(8,128)}, f32[36,9216]{1,0:T(8,128)S(1)}, u32[]{:S(2)}, u32[]{:S(2)}) collective-permute-start(f32[36,9216]{1,0:T(8,128)} %top.3), channel_id=1, source_target_pairs={{0,32},{32,64},{64,96},{96,128},{128,160},{160,192},{192,224},{1,3... | collective-permute-start | bytes 3981320 | tf_op jit(solution)/shard_map/ppermute | solution.py:25
  4.5 0.0 copy-start.1
  4.5 0.0 copy-start.2
  4.5 0.0 copy-start.3
  4.5 0.0 copy-start.4
  4.5 0.0 copy-start.5
  4.5 0.0 copy-start.6
  4.5 0.0 copy-start.7
  4.5 0.0 copy-start.8
  4.5 0.0 copy-start.9
  4.5 0.0 copy-start.10
  4.6 2.7 %restrict_twice.1 = (f32[7,8,32]{2,1,0:T(8,128)S(1)}, f32[16,128]{1,0:T(8,128)S(1)}) custom-call(s32[1,216]{1,0:T(1,128)} %bitcast.31, f32[4,24,24,24]{3,2,1,0:T(8,128)} %refs_1_.1, f32[4,24,24,24]{3,2,1,0:T(8,128)} %refs_2_.1, f32[24,24,24]{2,1,0:T(8,128)} %refs_3_.1), custom_call_target="tpu_custom_call" | custom-call | tf_op jit(solution)/shard_map/restrict_twice/pallas_call | solution.py:203
  7.3 0.0 copy-start
  7.3 3.6 %collective-permute-start = (f32[16,128]{1,0:T(8,128)S(1)}, f32[16,128]{1,0:T(8,128)S(1)}, u32[]{:S(2)}, u32[]{:S(2)}) collective-permute-start(f32[16,128]{1,0:T(8,128)S(1)} %get-tuple-element.28), channel_id=1, source_target_pairs={{0,32},{32,64},{64,96},{96,128},{128,160},{160,192},{192,224},{1,3... | collective-permute-start | bytes 24584 | tf_op jit(solution)/shard_map/ppermute | solution.py:25
  10.9 0.0 copy-done.1
  10.9 0.0 copy-done.2
  10.9 0.0 copy-done.3
  10.9 0.0 copy-done.4
  11.0 0.0 copy-done.5
  11.0 0.0 copy-done.6
  11.0 0.0 copy-done.7
  11.0 0.0 copy-done.8
  11.0 0.0 copy-done.9
  11.0 0.0 copy-done.10
  11.0 1.1 prepare.1
  12.2 23.5 %collective-permute-done.from_x = f32[16,128]{1,0:T(8,128)S(1)} collective-permute-done((f32[16,128]{1,0:T(8,128)S(1)}, f32[16,128]{1,0:T(8,128)S(1)}, u32[]{:S(2)}, u32[]{:S(2)}) %collective-permute-start) | collective-permute-done | bytes 8224 | tf_op jit(solution)/shard_map/ppermute | solution.py:25
  35.7 3.2 %collective-permute-start.1 = (f32[40,960]{1,0:T(8,128)S(1)}, f32[40,960]{1,0:T(8,128)S(1)}, u32[]{:S(2)}, u32[]{:S(2)}) collective-permute-start(f32[40,960]{1,0:T(8,128)S(1)} %y_message.1.second), channel_id=1, source_target_pairs={{0,8},{8,16},{16,24},{1,9},{9,17},{17,25},{2,10},{10,18},{18,26},{... | collective-permute-start | bytes 460808 | tf_op jit(solution)/shard_map/ppermute | solution.py:25
  38.9 3.7 %collective-permute-start.3 = (f32[56,256]{1,0:T(8,128)S(1)}, f32[56,256]{1,0:T(8,128)S(1)}, u32[]{:S(2)}, u32[]{:S(2)}) collective-permute-start(f32[56,256]{1,0:T(8,128)S(1)} %get-tuple-element.32), channel_id=1, source_target_pairs={{1,0},{2,1},{3,2},{4,3},{5,4},{6,5},{7,6},{9,8},{10,9},{11,10},{12... | collective-permute-start | bytes 172040 | tf_op jit(solution)/shard_map/ppermute | solution.py:25
  42.7 3.0 %collective-permute-start.2 = (f32[32,256]{1,0:T(8,128)S(1)}, f32[32,256]{1,0:T(8,128)S(1)}, u32[]{:S(2)}, u32[]{:S(2)}) collective-permute-start(f32[32,256]{1,0:T(8,128)S(1)} %get-tuple-element.31.first), channel_id=1, source_target_pairs={{0,1},{1,2},{2,3},{3,4},{4,5},{5,6},{6,7},{8,9},{9,10},{10,11},{11... | collective-permute-start | bytes 98312 | tf_op jit(solution)/shard_map/ppermute | solution.py:25
  45.7 1.0 collective-permute-done.2.below
  46.7 0.0 collective-permute-done.3.above
  46.7 0.0 collective-permute-done.1.from_y.below
  46.7 0.9 shard_map.136
  47.6 10.2 %all_to_all.35.received = f32[8,16,128]{2,1,0:T(8,128)S(1)} all-to-all(f32[8,16,128]{2,1,0:T(8,128)S(1)} %get-tuple-element.33), channel_id=1, replica_groups=mesh['gx'=8,'gy'=4,'gz'=8] {'gz'}, dimensions={0} | all-to-all | bytes 131072 | tf_op jit(solution)/shard_map/all_to_all | solution.py:29
  57.8 1.0 shard_map.137
  58.8 13.1 %all_to_all.36.received = f32[32,8,128]{2,1,0:T(8,128)S(1)} all-to-all(f32[32,8,128]{2,1,0:T(8,128)S(1)} %get-tuple-element.35), channel_id=1, replica_groups=mesh['gx'=8,'gy'=4,'gz'=8] {'gy','gz'}, dimensions={0} | all-to-all | bytes 262144 | tf_op jit(solution)/shard_map/all_to_all | solution.py:29
  71.9 0.0 collective-permute-done.4.below
  71.9 0.0 copy-done
  71.9 1.0 shard_map.138
  72.9 11.9 %all_to_all.37.received = f32[32,4,384]{2,1,0:T(4,128)S(1)} all-to-all(f32[32,4,384]{2,1,0:T(4,128)S(1)} %get-tuple-element.38), channel_id=1, replica_groups=mesh['gx'=8,'gy'=4,'gz'=8] {'gy','gz'}, dimensions={0} | all-to-all | bytes 393216 | tf_op jit(solution)/shard_map/all_to_all | solution.py:29
  84.8 16.8 %all_to_all.38.received = f32[8,4,384]{2,1,0:T(4,128)S(1)} all-to-all(f32[8,4,384]{2,1,0:T(4,128)S(1)} %shard_map.139), channel_id=1, replica_groups=mesh['gx'=8,'gy'=4,'gz'=8] {'gx'}, dimensions={0} | all-to-all | bytes 98304 | tf_op jit(solution)/shard_map/all_to_all | solution.py:29
  101.6 13.3 %all_to_all.39.whole = f32[32,4,384]{2,1,0:T(4,128)S(1)} all-to-all(f32[32,4,384]{2,1,0:T(4,128)S(1)} %shard_map.140), channel_id=1, replica_groups=mesh['gx'=8,'gy'=4,'gz'=8] {'gy','gz'}, dimensions={0} | all-to-all | bytes 393216 | tf_op jit(solution)/shard_map/all_to_all | solution.py:29
  114.9 1.5 %shard_map.141 = (f32[4,36]{1,0:T(4,128)S(1)}, f32[4,30]{1,0:T(4,128)S(1)}, f32[4,25]{1,0:T(4,128)S(1)}, f32[4,125]{1,0:T(4,128)S(1)}) custom-call(f32[32,4,384]{2,1,0:T(4,128)S(1)} %all_to_all.39.whole, f32[36,9216]{1,0:T(8,128)S(1)} %copy-done, f32[36,9216]{1,0:T(8,128)S(1)} %collective-permute-done.4.below, f32[4,30]{1,0:T(4,128)S(1)} %get-tuple-element.39.second_own, ...), custom_call_target="tpu_custom_call" | custom-call | tf_op jit(solution)/shard_map/pallas_call | solution.py:688
  116.4 10.9 %all_to_all.40 = f32[32,4,30]{2,1,0:T(4,128)S(1)} all-to-all(f32[32,4,30]{2,1,0:T(4,128)S(1)} %broadcast_in_dim.6), channel_id=1, replica_groups=mesh['gx'=8,'gy'=4,'gz'=8] {'gy','gz'}, dimensions={0} | all-to-all | bytes 30720 | tf_op jit(solution)/shard_map/all_to_all | solution.py:29
  127.4 0.1 reshape.15.whole
  127.5 0.7 shard_map.142
  128.2 7.5 %all_to_all.41.received = f32[8,8,128]{2,1,0:T(8,128)S(1)} all-to-all(f32[8,8,128]{2,1,0:T(8,128)S(1)} %broadcast_in_dim.7), channel_id=1, replica_groups=mesh['gx'=8,'gy'=4,'gz'=8] {'gz'}, dimensions={0} | all-to-all | bytes 65536 | tf_op jit(solution)/shard_map/all_to_all | solution.py:29
  135.7 1.0 shard_map.143.inner
  136.7 1.3 collective-permute-start.5
  138.1 3.0 %collective-permute-done.5.after_x = f32[8,32]{1,0:T(8,128)S(1)} collective-permute-done((f32[8,32]{1,0:T(8,128)S(1)}, f32[8,32]{1,0:T(8,128)S(1)}, u32[]{:S(2)}, u32[]{:S(2)}) %collective-permute-start.5) | collective-permute-done | bytes 1056 | tf_op jit(solution)/shard_map/ppermute | solution.py:25
  141.1 1.3 collective-permute-start.6
  142.4 3.1 %collective-permute-done.6.after_y = f32[7,32]{1,0:T(8,128)S(1)} collective-permute-done((f32[7,32]{1,0:T(8,128)S(1)}, f32[7,32]{1,0:T(8,128)S(1)}, u32[]{:S(2)}, u32[]{:S(2)}) %collective-permute-start.6) | collective-permute-done | bytes 928 | tf_op jit(solution)/shard_map/ppermute | solution.py:25
  145.5 1.4 prolong_twice.1
  (11 shorter events, 0.1 us)
Async XLA Ops:
  0.0 71.9 %collective-permute-start.4 = (f32[36,9216]{1,0:T(8,128)}, f32[36,9216]{1,0:T(8,128)S(1)}, u32[]{:S(2)}, u32[]{:S(2)}) collective-permute-start(f32[36,9216]{1,0:T(8,128)} %top.3), channel_id=1, source_target_pairs={{0,32},{32,64},{64,96},{96,128},{128,160},{160,192},{192,224},{1,3... | collective-permute-start | bytes 3981320 | tf_op jit(solution)/shard_map/ppermute | solution.py:25
  4.5 6.5 %copy-start.1 = (f32[1,30,960]{2,0,1:T(1,128)S(1)}, f32[1,30,960]{2,0,1:T(1,128)}, u32[]{:S(2)}) copy-start(f32[1,30,960]{2,0,1:T(1,128)} %param.25) | copy-start | bytes 345604
  4.5 6.5 %copy-start.2 = (f32[1,1,1,125,125]{4,2,3,1,0:T(1,128)S(1)}, f32[1,1,1,125,125]{4,2,3,1,0:T(1,128)}, u32[]{:S(2)}) copy-start(f32[1,1,1,125,125]{4,2,3,1,0:T(1,128)} %param.18) | copy-start | bytes 187504
  4.5 6.5 %copy-start.3 = (f32[1,1,1,125,72]{3,4,2,1,0:T(8,128)S(1)}, f32[1,1,1,125,72]{3,4,2,1,0:T(8,128)}, u32[]{:S(2)}) copy-start(f32[1,1,1,125,72]{3,4,2,1,0:T(8,128)} %param.21) | copy-start | bytes 108004
  4.5 6.5 %copy-start.4 = (f32[1,1,1,125,60]{3,2,4,1,0:T(1,128)S(1)}, f32[1,1,1,125,60]{3,2,4,1,0:T(1,128)}, u32[]{:S(2)}) copy-start(f32[1,1,1,125,60]{3,2,4,1,0:T(1,128)} %param.20) | copy-start | bytes 90004
  4.5 6.5 %copy-start.5 = (f32[1,1,1,125,50]{3,2,4,1,0:T(1,128)S(1)}, f32[1,1,1,125,50]{3,2,4,1,0:T(1,128)}, u32[]{:S(2)}) copy-start(f32[1,1,1,125,50]{3,2,4,1,0:T(1,128)} %param.19) | copy-start | bytes 75004
  4.5 6.5 %copy-start.6 = (f32[1,1,25,200]{3,1,2,0:T(1,128)S(1)}, f32[1,1,25,200]{3,1,2,0:T(1,128)}, u32[]{:S(2)}) copy-start(f32[1,1,25,200]{3,1,2,0:T(1,128)} %param.22) | copy-start | bytes 60004
  4.5 6.5 %copy-start.7 = (f32[1,1,1,30,72]{4,2,3,1,0:T(1,128)S(1)}, f32[1,1,1,30,72]{4,2,3,1,0:T(1,128)}, u32[]{:S(2)}) copy-start(f32[1,1,1,30,72]{4,2,3,1,0:T(1,128)} %param.26) | copy-start | bytes 25924
  4.5 6.5 %copy-start.8 = (f32[1,1,1,25,60]{4,2,3,1,0:T(1,128)S(1)}, f32[1,1,1,25,60]{4,2,3,1,0:T(1,128)}, u32[]{:S(2)}) copy-start(f32[1,1,1,25,60]{4,2,3,1,0:T(1,128)} %param.23) | copy-start | bytes 18004
  4.5 6.5 %copy-start.9 = (f32[1,1,1,25,72]{4,2,3,1,0:T(1,128)S(1)}, f32[1,1,1,25,72]{4,2,3,1,0:T(1,128)}, u32[]{:S(2)}) copy-start(f32[1,1,1,25,72]{4,2,3,1,0:T(1,128)} %param.24) | copy-start | bytes 21604
  4.5 6.5 %copy-start.10 = (s32[1,1,1,216]{3,2,1,0:T(1,128)S(1)}, s32[1,1,1,216]{3,2,1,0:T(1,128)}, u32[]{:S(2)}) copy-start(s32[1,1,1,216]{3,2,1,0:T(1,128)} %param.17) | copy-start | bytes 2596
  7.3 64.6 %copy-start = (f32[36,9216]{1,0:T(8,128)S(1)}, f32[36,9216]{1,0:T(8,128)}, u32[]{:S(2)}) copy-start(f32[36,9216]{1,0:T(8,128)} %top.3) | copy-start | bytes 3981316
  7.3 28.4 %collective-permute-start = (f32[16,128]{1,0:T(8,128)S(1)}, f32[16,128]{1,0:T(8,128)S(1)}, u32[]{:S(2)}, u32[]{:S(2)}) collective-permute-start(f32[16,128]{1,0:T(8,128)S(1)} %get-tuple-element.28), channel_id=1, source_target_pairs={{0,32},{32,64},{64,96},{96,128},{128,160},{160,192},{192,224},{1,3... | collective-permute-start | bytes 24584 | tf_op jit(solution)/shard_map/ppermute | solution.py:25
  35.7 11.0 %collective-permute-start.1 = (f32[40,960]{1,0:T(8,128)S(1)}, f32[40,960]{1,0:T(8,128)S(1)}, u32[]{:S(2)}, u32[]{:S(2)}) collective-permute-start(f32[40,960]{1,0:T(8,128)S(1)} %y_message.1.second), channel_id=1, source_target_pairs={{0,8},{8,16},{16,24},{1,9},{9,17},{17,25},{2,10},{10,18},{18,26},{... | collective-permute-start | bytes 460808 | tf_op jit(solution)/shard_map/ppermute | solution.py:25
  38.9 7.8 %collective-permute-start.3 = (f32[56,256]{1,0:T(8,128)S(1)}, f32[56,256]{1,0:T(8,128)S(1)}, u32[]{:S(2)}, u32[]{:S(2)}) collective-permute-start(f32[56,256]{1,0:T(8,128)S(1)} %get-tuple-element.32), channel_id=1, source_target_pairs={{1,0},{2,1},{3,2},{4,3},{5,4},{6,5},{7,6},{9,8},{10,9},{11,10},{12... | collective-permute-start | bytes 172040 | tf_op jit(solution)/shard_map/ppermute | solution.py:25
  42.7 4.0 %collective-permute-start.2 = (f32[32,256]{1,0:T(8,128)S(1)}, f32[32,256]{1,0:T(8,128)S(1)}, u32[]{:S(2)}, u32[]{:S(2)}) collective-permute-start(f32[32,256]{1,0:T(8,128)S(1)} %get-tuple-element.31.first), channel_id=1, source_target_pairs={{0,1},{1,2},{2,3},{3,4},{4,5},{5,6},{6,7},{8,9},{9,10},{10,11},{11... | collective-permute-start | bytes 98312 | tf_op jit(solution)/shard_map/ppermute | solution.py:25
  136.7 4.4 %collective-permute-start.5 = (f32[8,32]{1,0:T(8,128)S(1)}, f32[8,32]{1,0:T(8,128)S(1)}, u32[]{:S(2)}, u32[]{:S(2)}) collective-permute-start(f32[8,32]{1,0:T(8,128)S(1)} %slice_bitcast_fusion), channel_id=1, source_target_pairs={{32,0},{64,32},{96,64},{128,96},{160,128},{192,160},{224,192},{33,... | collective-permute-start | bytes 3080 | tf_op jit(solution)/shard_map/ppermute | solution.py:25
  141.1 4.4 %collective-permute-start.6 = (f32[7,32]{1,0:T(8,128)S(1)}, f32[7,32]{1,0:T(8,128)S(1)}, u32[]{:S(2)}, u32[]{:S(2)}) collective-permute-start(f32[7,32]{1,0:T(8,128)S(1)} %pad_maximum_fusion), channel_id=1, source_target_pairs={{8,0},{16,8},{24,16},{9,1},{17,9},{25,17},{10,2},{18,10},{26,18},{... | collective-permute-start | bytes 2696 | tf_op jit(solution)/shard_map/ppermute | solution.py:25

commit v6 on v5

--- a/solution.py
+++ b/solution.py
@@ -250,13 +250,30 @@
     )
 
 
-def picked(cells, count, side, number, order, layers=None):
-    total = None
-    for z in range(side) if layers is None else layers:
-        layer = cells[(z + 1) * count : (z + 2) * count]
-        term = times_weights(layer, one_hot(number + float(z), order))
-        total = term if total is None else total + term
+def layers_in(order, side):
+    return order - side * jnp.floor((order + 0.5) * (1.0 / side))
+
+
+def on_own_layer(rows, order, count, side):
+    row = lax.broadcasted_iota(jnp.int32, (rows, order.shape[1]), 0)
+    return (row // count).astype(jnp.float32) == layers_in(order, side)
+
+
+def picked(cells, count, side, number, order):
+    layers = cells[count : (side + 1) * count]
+    lanes = one_hot(number, order - layers_in(order, side))
+    values = times_weights(layers, lanes)
+    values = jnp.where(on_own_layer(side * count, order, count, side), values, 0.0)
+    total = values[0:count]
+    for z in range(1, side):
+        total = total + values[z * count : (z + 1) * count]
     return total
+
+
+def placed(values, count, side, number, order):
+    values = jnp.concatenate([values] * side, axis=0)
+    values = jnp.where(on_own_layer(side * count, order, count, side), values, 0.0)
+    return times_weights_back(values, one_hot(number, order - layers_in(order, side)))
 
 
 LEAF, TO_FIRST, TO_SECOND, TO_TOP = 0, 128, 184, 248
@@ -279,21 +296,12 @@
 
 
 def prepare_body(sizes, side, *refs):
-    sources, (up, down, beside, pack) = refs[:10], refs[10:14]
-    held, arrived = refs[14:24], refs[24]
-    copies = [
-        pltpu.make_async_copy(source, room, arrived.at[n])
-        for n, (source, room) in enumerate(zip(sources, held))
-    ]
-    for copy in copies:
-        copy.start()
+    order, leaf, to_first, first, second = refs[:5]
+    to_second, to_top, first_second, first_top, second_top = refs[5:10]
+    up, down, beside, pack = refs[10:]
     up[...] = jnp.zeros_like(up)
     down[...] = jnp.zeros_like(down)
     beside[sizes[2] :, :] = jnp.zeros_like(beside[sizes[2] :, :])
-    for copy in copies:
-        copy.wait()
-    order, leaf, to_first, first, second = held[:5]
-    to_second, to_top, first_second, first_top, second_top = held[5:]
     order = order[...].astype(jnp.float32)
     leaf_size, first_size, second_size = sizes[:3]
     leaf_rows, first_columns = leaf[:, 0, :], to_first[:, 0, :]
@@ -333,10 +341,8 @@
     return pl.pallas_call(
         functools.partial(prepare_body, sizes, side),
         out_shape=tuple(jax.ShapeDtypeStruct(o, jnp.float32) for o in shapes),
-        in_specs=[HBM] * len(sources),
+        in_specs=[VMEM] * len(sources),
         out_specs=(VMEM,) * len(shapes),
-        scratch_shapes=[pltpu.VMEM(x.shape, x.dtype) for x in sources]
-        + [pltpu.SemaphoreType.DMA((len(sources),))],
         compiler_params=LIMIT,
         name="prepare",
     )(*sources)
@@ -385,7 +391,7 @@
     cells_out[...] = cells
     number = numbers(side, "in")
     leaf_rhs = picked(cells, count, side, number, leaf_order)
-    first_rhs = picked(cells, count, side, number, first_order, [side - 1])
+    first_rhs = picked(cells, count, side, number, first_order)
     after = cells[(side + 1) * count : (side + 2) * count]
     before = cells[0:count]
     leaf = pack[LEAF : LEAF + leaf_size, 0:leaf_size]
@@ -467,6 +473,42 @@
     toward_out[:, top_size:] = toward[:, top_size:] - before_x
 
 
+def fold_body(top, out):
+    rows, columns = top.shape
+    full = rows // 8
+    for g in range(full):
+        out[:, g * columns : (g + 1) * columns] = top[8 * g : 8 * g + 8, :]
+    half = columns // 2
+    start = full * columns
+    out[0:4, start : start + half] = top[8 * full : rows, 0:half]
+    out[4:8, start : start + half] = top[8 * full : rows, half:columns]
+
+
+def folded(top):
+    rows, columns = top.shape
+    assert rows % 8 == 4
+    return pl.pallas_call(
+        fold_body,
+        out_shape=jax.ShapeDtypeStruct((8, columns * rows // 8), jnp.float32),
+        in_specs=[VMEM],
+        out_specs=VMEM,
+        compiler_params=LIMIT,
+        name="fold",
+    )(top)
+
+
+def unfolded(folds, rows, columns, start, width):
+    full = rows // 8
+    parts = []
+    for g in range(full):
+        at = g * columns + start
+        parts.append(folds[:, at : at + width])
+    half = start // (columns // 2)
+    at = full * columns + start - half * (columns // 2)
+    parts.append(folds[4 * half : 4 * half + 4, at : at + width])
+    return jnp.concatenate(parts, axis=0)
+
+
 def top_body(used, received, toward, rhs, pack, top, below, pieces, second_out):
     count = toward.shape[0]
     second_size = second_out.shape[1]
@@ -489,8 +531,9 @@
     for p in range(used):
         at = slice(p * width, (p + 1) * width)
         total = None
-        for (both, high), rows in zip(vectors, (top, below)):
-            first, second = parts_of(rows[:, at])
+        lower = unfolded(below, *top.shape, p * width, width)
+        for (both, high), rows in zip(vectors, (top[:, at], lower)):
+            first, second = parts_of(rows)
             term = dot(both, first)
             term = term[:count] + (term[count:] + dot(high, second))
             total = term if total is None else total + term
@@ -515,28 +558,17 @@
     width = whole.shape[2]
     top_size = top.shape[0]
 
-    def step(p, sums):
-        piece = whole[p]
-        start = pl.multiple_of(p * width, 128)
-        out = list(sums)
-        for t in range(width // 128):
-            at = pl.ds(start + t * 128, 128)
-            rows, lower = top[:, at], below[:, at]
-            for r in range(count):
-                line = piece[r : r + 1, t * 128 : (t + 1) * 128]
-                out[r] = out[r] + rows * line
-                out[count + r] = out[count + r] + lower * line
-        return tuple(out)
-
-    zero = jnp.zeros((top_size, 128), jnp.float32)
-    sums = lax.fori_loop(0, used, step, (zero,) * (2 * count))
-    line = lax.broadcasted_iota(jnp.int32, (count, 128), 0)
     halves = []
-    for half in range(2):
+    for fold in (False, True):
         total = None
-        for r in range(count):
-            ones = jnp.where(line == r, 1.0, 0.0).astype(jnp.bfloat16)
-            term = weights_times_back(ones, sums[half * count + r])
+        for p in range(used):
+            at = slice(p * width, (p + 1) * width)
+            high, low = parts_of(whole[p])
+            both = jnp.concatenate([high.astype(jnp.float32), low.astype(jnp.float32)], axis=0)
+            rows = unfolded(below, *top.shape, p * width, width) if fold else top[:, at]
+            first, second = parts_of(rows)
+            term = dot_back(both.astype(jnp.bfloat16), first)
+            term = term[:count] + (term[count:] + dot_back(high, second))
             total = term if total is None else total + term
         halves.append(total)
     own, lower = halves
@@ -613,19 +645,11 @@
     face = face - times_weights(moved, shift.astype(jnp.bfloat16))
     orders = packed_order(pack, sizes)
     number = numbers(side, "out")
-    layers = []
-    for z in range(side):
-        layer = times_weights_back(leaf_back, one_hot(number + float(z), orders[0]))
-        layer = layer + times_weights_back(
-            second_back[...], one_hot(number + float(z), orders[2])
-        )
-        layer = layer + times_weights_back(top_back[...], one_hot(number + float(z), orders[3]))
-        if z == side - 1:
-            layer = layer + times_weights_back(own, one_hot(number + float(z), orders[1]))
-        layers.append(layer)
-    layers.append(face)
-    layers.append(jnp.zeros_like(face))
-    cells = jnp.concatenate(layers, axis=0)
+    layers = placed(leaf_back, count, side, number, orders[0])
+    layers = layers + placed(own, count, side, number, orders[1])
+    layers = layers + placed(second_back[...], count, side, number, orders[2])
+    layers = layers + placed(top_back[...], count, side, number, orders[3])
+    cells = jnp.concatenate([layers, face, jnp.zeros_like(face)], axis=0)
     turned = weights_times_back(eye(reach), cells)
     window[...] = turned.reshape(window.shape)
 
@@ -759,7 +783,8 @@
     )
     first_below = shifted(up, "gz", 1)
     first_above = shifted(down, "gz", -1)
-    top_below = shifted(top_inverse, "gx", 1)
+    folds = folded(top_inverse)
+    top_below = shifted(folds, "gx", 1)
     beside = with_layer(inner, from_x, beside)
     second_below = shifted(beside, "gy", 1)
 

time: 148 us -> 146 us (0.986)
  waiting for transfers between devices: 30.6 us -> 27.9 us
    ppermute x7, waiting for transfers between devices: 30.6 us -> 27.9 us  [shifted(): return lax.ppermute(shard, axis, pairs)]
where the time goes in v6:
time: 146 us; the launch traced here: 145 us
  blocking collectives  83.7 us (57%)
  waiting for transfers between devices  27.9 us (19%)
  starting transfers between devices  20.6 us (14%)
  Pallas kernels  10.8 us (7%)
  local copies, waits for them, and re-layouts  1.6 us (1%)
    all_to_all x7, blocking collectives, exchanged(): return lax.all_to_all(pieces, axis, split_axis=0, concat_axis=0, tiled=True)  83.7 us
    ppermute x7, waiting for transfers between devices, shifted(): return lax.ppermute(shard, axis, pairs)  27.9 us
    ppermute x7, starting transfers between devices, shifted(): return lax.ppermute(shard, axis, pairs)  20.6 us
    pallas_call x8, Pallas kernels, call(): pl.pallas_call(body, out_shape=shapes, in_specs=[VMEM] * len(operands), o...  5.95 us
  transfers between devices with their start and end apart: 7, of which 4 were waited for; matrix products, arithmetic and copies ran while one was open for 0% of the time, Pallas kernels for 4%

profile of v6, /device:TPU:1, one launch (start us, length us, event | category | flops | bytes accessed | tf_op | source)
XLA Modules:
  0.0 144.8 jit_solution(4004181302402733205)
XLA Ops:
  0.0 0.0 copy-start
  0.0 1.4 copy-done
  1.4 0.1 fold.1
  1.5 4.4 %collective-permute-start.4 = (f32[8,41472]{1,0:T(8,128)S(1)}, f32[8,41472]{1,0:T(8,128)S(1)}, u32[]{:S(2)}, u32[]{:S(2)}) collective-permute-start(f32[8,41472]{1,0:T(8,128)S(1)} %fold.1), channel_id=1, source_target_pairs={{0,32},{32,64},{64,96},{96,128},{128,160},{160,192},{192,224},{1,3... | collective-permute-start | bytes 3981320 | tf_op jit(solution)/shard_map/ppermute | solution.py:25
  5.9 0.0 copy-start.2
  5.9 0.0 copy-start.3
  6.0 0.0 copy-start.4
  6.0 0.0 copy-start.5
  6.0 0.0 copy-start.6
  6.0 0.0 copy-start.7
  6.0 0.0 copy-start.8
  6.0 0.0 copy-start.9
  6.0 0.0 copy-start.10
  6.0 0.0 copy-start.11
  6.1 2.7 %restrict_twice.1 = (f32[7,8,32]{2,1,0:T(8,128)S(1)}, f32[16,128]{1,0:T(8,128)S(1)}) custom-call(s32[1,216]{1,0:T(1,128)} %bitcast.31, f32[4,24,24,24]{3,2,1,0:T(8,128)} %refs_1_.1, f32[4,24,24,24]{3,2,1,0:T(8,128)} %refs_2_.1, f32[24,24,24]{2,1,0:T(8,128)} %refs_3_.1), custom_call_target="tpu_custom_call" | custom-call | tf_op jit(solution)/shard_map/restrict_twice/pallas_call | solution.py:203
  8.8 0.0 copy-start.1
  8.8 3.6 %collective-permute-start = (f32[16,128]{1,0:T(8,128)S(1)}, f32[16,128]{1,0:T(8,128)S(1)}, u32[]{:S(2)}, u32[]{:S(2)}) collective-permute-start(f32[16,128]{1,0:T(8,128)S(1)} %get-tuple-element.28), channel_id=1, source_target_pairs={{0,32},{32,64},{64,96},{96,128},{128,160},{160,192},{192,224},{1,3... | collective-permute-start | bytes 24584 | tf_op jit(solution)/shard_map/ppermute | solution.py:25
  12.4 0.0 copy-done.2
  12.4 0.0 copy-done.3
  12.4 0.0 copy-done.4
  12.4 0.0 copy-done.5
  12.4 0.0 copy-done.6
  12.5 0.0 copy-done.7
  12.5 0.0 copy-done.8
  12.5 0.0 copy-done.9
  12.5 0.0 copy-done.10
  12.5 0.0 copy-done.11
  12.5 0.5 prepare.1
  13.1 20.8 %collective-permute-done.from_x = f32[16,128]{1,0:T(8,128)S(1)} collective-permute-done((f32[16,128]{1,0:T(8,128)S(1)}, f32[16,128]{1,0:T(8,128)S(1)}, u32[]{:S(2)}, u32[]{:S(2)}) %collective-permute-start) | collective-permute-done | bytes 8224 | tf_op jit(solution)/shard_map/ppermute | solution.py:25
  33.8 3.2 %collective-permute-start.1 = (f32[40,960]{1,0:T(8,128)S(1)}, f32[40,960]{1,0:T(8,128)S(1)}, u32[]{:S(2)}, u32[]{:S(2)}) collective-permute-start(f32[40,960]{1,0:T(8,128)S(1)} %y_message.1.second), channel_id=1, source_target_pairs={{0,8},{8,16},{16,24},{1,9},{9,17},{17,25},{2,10},{10,18},{18,26},{... | collective-permute-start | bytes 460808 | tf_op jit(solution)/shard_map/ppermute | solution.py:25
  37.0 3.7 %collective-permute-start.3 = (f32[56,256]{1,0:T(8,128)S(1)}, f32[56,256]{1,0:T(8,128)S(1)}, u32[]{:S(2)}, u32[]{:S(2)}) collective-permute-start(f32[56,256]{1,0:T(8,128)S(1)} %get-tuple-element.32), channel_id=1, source_target_pairs={{1,0},{2,1},{3,2},{4,3},{5,4},{6,5},{7,6},{9,8},{10,9},{11,10},{12... | collective-permute-start | bytes 172040 | tf_op jit(solution)/shard_map/ppermute | solution.py:25
  40.8 3.0 %collective-permute-start.2 = (f32[32,256]{1,0:T(8,128)S(1)}, f32[32,256]{1,0:T(8,128)S(1)}, u32[]{:S(2)}, u32[]{:S(2)}) collective-permute-start(f32[32,256]{1,0:T(8,128)S(1)} %get-tuple-element.31.first), channel_id=1, source_target_pairs={{0,1},{1,2},{2,3},{3,4},{4,5},{5,6},{6,7},{8,9},{9,10},{10,11},{11... | collective-permute-start | bytes 98312 | tf_op jit(solution)/shard_map/ppermute | solution.py:25
  43.8 1.0 collective-permute-done.2.below
  44.8 0.0 collective-permute-done.3.above
  44.8 0.0 collective-permute-done.1.from_y.below
  44.8 0.9 shard_map.136
  45.7 10.2 %all_to_all.35.received = f32[8,16,128]{2,1,0:T(8,128)S(1)} all-to-all(f32[8,16,128]{2,1,0:T(8,128)S(1)} %get-tuple-element.33), channel_id=1, replica_groups=mesh['gx'=8,'gy'=4,'gz'=8] {'gz'}, dimensions={0} | all-to-all | bytes 131072 | tf_op jit(solution)/shard_map/all_to_all | solution.py:29
  55.9 0.9 shard_map.137
  56.8 13.1 %all_to_all.36.received = f32[32,8,128]{2,1,0:T(8,128)S(1)} all-to-all(f32[32,8,128]{2,1,0:T(8,128)S(1)} %get-tuple-element.35), channel_id=1, replica_groups=mesh['gx'=8,'gy'=4,'gz'=8] {'gy','gz'}, dimensions={0} | all-to-all | bytes 262144 | tf_op jit(solution)/shard_map/all_to_all | solution.py:29
  69.9 0.0 collective-permute-done.4.below
  69.9 0.0 copy-done.1
  69.9 1.0 shard_map.138
  70.9 11.9 %all_to_all.37.received = f32[32,4,384]{2,1,0:T(4,128)S(1)} all-to-all(f32[32,4,384]{2,1,0:T(4,128)S(1)} %get-tuple-element.38), channel_id=1, replica_groups=mesh['gx'=8,'gy'=4,'gz'=8] {'gy','gz'}, dimensions={0} | all-to-all | bytes 393216 | tf_op jit(solution)/shard_map/all_to_all | solution.py:29
  82.8 16.8 %all_to_all.38.received = f32[8,4,384]{2,1,0:T(4,128)S(1)} all-to-all(f32[8,4,384]{2,1,0:T(4,128)S(1)} %shard_map.139), channel_id=1, replica_groups=mesh['gx'=8,'gy'=4,'gz'=8] {'gx'}, dimensions={0} | all-to-all | bytes 98304 | tf_op jit(solution)/shard_map/all_to_all | solution.py:29
  99.7 13.3 %all_to_all.39.whole = f32[32,4,384]{2,1,0:T(4,128)S(1)} all-to-all(f32[32,4,384]{2,1,0:T(4,128)S(1)} %shard_map.140), channel_id=1, replica_groups=mesh['gx'=8,'gy'=4,'gz'=8] {'gy','gz'}, dimensions={0} | all-to-all | bytes 393216 | tf_op jit(solution)/shard_map/all_to_all | solution.py:29
  112.9 1.5 %shard_map.141 = (f32[4,36]{1,0:T(4,128)S(1)}, f32[4,30]{1,0:T(4,128)S(1)}, f32[4,25]{1,0:T(4,128)S(1)}, f32[4,125]{1,0:T(4,128)S(1)}) custom-call(f32[32,4,384]{2,1,0:T(4,128)S(1)} %all_to_all.39.whole, f32[36,9216]{1,0:T(8,128)S(1)} %copy-done.1, f32[8,41472]{1,0:T(8,128)S(1)} %collective-permute-done.4.below, f32[4,30]{1,0:T(4,128)S(1)} %get-tuple-element.39.second_own, ...), custom_call_target="tpu_custom_call" | custom-call | tf_op jit(solution)/shard_map/pallas_call | solution.py:712
  114.5 10.9 %all_to_all.40 = f32[32,4,30]{2,1,0:T(4,128)S(1)} all-to-all(f32[32,4,30]{2,1,0:T(4,128)S(1)} %broadcast_in_dim.6), channel_id=1, replica_groups=mesh['gx'=8,'gy'=4,'gz'=8] {'gy','gz'}, dimensions={0} | all-to-all | bytes 30720 | tf_op jit(solution)/shard_map/all_to_all | solution.py:29
  125.4 0.1 reshape.15.whole
  125.5 0.7 shard_map.142
  126.3 7.5 %all_to_all.41.received = f32[8,8,128]{2,1,0:T(8,128)S(1)} all-to-all(f32[8,8,128]{2,1,0:T(8,128)S(1)} %broadcast_in_dim.7), channel_id=1, replica_groups=mesh['gx'=8,'gy'=4,'gz'=8] {'gz'}, dimensions={0} | all-to-all | bytes 65536 | tf_op jit(solution)/shard_map/all_to_all | solution.py:29
  133.7 0.9 shard_map.143.inner
  134.6 1.3 collective-permute-start.5
  136.0 3.0 %collective-permute-done.5.after_x = f32[8,32]{1,0:T(8,128)S(1)} collective-permute-done((f32[8,32]{1,0:T(8,128)S(1)}, f32[8,32]{1,0:T(8,128)S(1)}, u32[]{:S(2)}, u32[]{:S(2)}) %collective-permute-start.5) | collective-permute-done | bytes 1056 | tf_op jit(solution)/shard_map/ppermute | solution.py:25
  139.0 1.3 collective-permute-start.6
  140.3 3.1 %collective-permute-done.6.after_y = f32[7,32]{1,0:T(8,128)S(1)} collective-permute-done((f32[7,32]{1,0:T(8,128)S(1)}, f32[7,32]{1,0:T(8,128)S(1)}, u32[]{:S(2)}, u32[]{:S(2)}) %collective-permute-start.6) | collective-permute-done | bytes 928 | tf_op jit(solution)/shard_map/ppermute | solution.py:25
  143.4 1.4 prolong_twice.1
  (11 shorter events, 0.1 us)
Async XLA Ops:
  0.0 1.4 copy-start
  1.5 68.4 %collective-permute-start.4 = (f32[8,41472]{1,0:T(8,128)S(1)}, f32[8,41472]{1,0:T(8,128)S(1)}, u32[]{:S(2)}, u32[]{:S(2)}) collective-permute-start(f32[8,41472]{1,0:T(8,128)S(1)} %fold.1), channel_id=1, source_target_pairs={{0,32},{32,64},{64,96},{96,128},{128,160},{160,192},{192,224},{1,3... | collective-permute-start | bytes 3981320 | tf_op jit(solution)/shard_map/ppermute | solution.py:25
  5.9 6.5 %copy-start.2 = (f32[1,30,960]{2,0,1:T(1,128)S(1)}, f32[1,30,960]{2,0,1:T(1,128)}, u32[]{:S(2)}) copy-start(f32[1,30,960]{2,0,1:T(1,128)} %param.25) | copy-start | bytes 345604
  5.9 6.5 %copy-start.3 = (f32[1,1,1,125,125]{4,2,3,1,0:T(1,128)S(1)}, f32[1,1,1,125,125]{4,2,3,1,0:T(1,128)}, u32[]{:S(2)}) copy-start(f32[1,1,1,125,125]{4,2,3,1,0:T(1,128)} %param.18) | copy-start | bytes 187504
  6.0 6.5 %copy-start.4 = (f32[1,1,1,125,72]{3,4,2,1,0:T(8,128)S(1)}, f32[1,1,1,125,72]{3,4,2,1,0:T(8,128)}, u32[]{:S(2)}) copy-start(f32[1,1,1,125,72]{3,4,2,1,0:T(8,128)} %param.21) | copy-start | bytes 108004
  6.0 6.5 %copy-start.5 = (f32[1,1,1,125,60]{3,2,4,1,0:T(1,128)S(1)}, f32[1,1,1,125,60]{3,2,4,1,0:T(1,128)}, u32[]{:S(2)}) copy-start(f32[1,1,1,125,60]{3,2,4,1,0:T(1,128)} %param.20) | copy-start | bytes 90004
  6.0 6.5 %copy-start.6 = (f32[1,1,1,125,50]{3,2,4,1,0:T(1,128)S(1)}, f32[1,1,1,125,50]{3,2,4,1,0:T(1,128)}, u32[]{:S(2)}) copy-start(f32[1,1,1,125,50]{3,2,4,1,0:T(1,128)} %param.19) | copy-start | bytes 75004
  6.0 6.5 %copy-start.7 = (f32[1,1,25,200]{3,1,2,0:T(1,128)S(1)}, f32[1,1,25,200]{3,1,2,0:T(1,128)}, u32[]{:S(2)}) copy-start(f32[1,1,25,200]{3,1,2,0:T(1,128)} %param.22) | copy-start | bytes 60004
  6.0 6.5 %copy-start.8 = (f32[1,1,1,30,72]{4,2,3,1,0:T(1,128)S(1)}, f32[1,1,1,30,72]{4,2,3,1,0:T(1,128)}, u32[]{:S(2)}) copy-start(f32[1,1,1,30,72]{4,2,3,1,0:T(1,128)} %param.26) | copy-start | bytes 25924
  6.0 6.5 %copy-start.9 = (f32[1,1,1,25,60]{4,2,3,1,0:T(1,128)S(1)}, f32[1,1,1,25,60]{4,2,3,1,0:T(1,128)}, u32[]{:S(2)}) copy-start(f32[1,1,1,25,60]{4,2,3,1,0:T(1,128)} %param.23) | copy-start | bytes 18004
  6.0 6.5 %copy-start.10 = (f32[1,1,1,25,72]{4,2,3,1,0:T(1,128)S(1)}, f32[1,1,1,25,72]{4,2,3,1,0:T(1,128)}, u32[]{:S(2)}) copy-start(f32[1,1,1,25,72]{4,2,3,1,0:T(1,128)} %param.24) | copy-start | bytes 21604
  6.0 6.5 %copy-start.11 = (s32[1,1,1,216]{3,2,1,0:T(1,128)S(1)}, s32[1,1,1,216]{3,2,1,0:T(1,128)}, u32[]{:S(2)}) copy-start(s32[1,1,1,216]{3,2,1,0:T(1,128)} %param.17) | copy-start | bytes 2596
  8.8 61.1 %copy-start.1 = (f32[36,9216]{1,0:T(8,128)S(1)}, f32[36,9216]{1,0:T(8,128)}, u32[]{:S(2)}) copy-start(f32[36,9216]{1,0:T(8,128)} %top.5) | copy-start | bytes 3981316
  8.8 25.0 %collective-permute-start = (f32[16,128]{1,0:T(8,128)S(1)}, f32[16,128]{1,0:T(8,128)S(1)}, u32[]{:S(2)}, u32[]{:S(2)}) collective-permute-start(f32[16,128]{1,0:T(8,128)S(1)} %get-tuple-element.28), channel_id=1, source_target_pairs={{0,32},{32,64},{64,96},{96,128},{128,160},{160,192},{192,224},{1,3... | collective-permute-start | bytes 24584 | tf_op jit(solution)/shard_map/ppermute | solution.py:25
  33.8 11.0 %collective-permute-start.1 = (f32[40,960]{1,0:T(8,128)S(1)}, f32[40,960]{1,0:T(8,128)S(1)}, u32[]{:S(2)}, u32[]{:S(2)}) collective-permute-start(f32[40,960]{1,0:T(8,128)S(1)} %y_message.1.second), channel_id=1, source_target_pairs={{0,8},{8,16},{16,24},{1,9},{9,17},{17,25},{2,10},{10,18},{18,26},{... | collective-permute-start | bytes 460808 | tf_op jit(solution)/shard_map/ppermute | solution.py:25
  37.0 7.8 %collective-permute-start.3 = (f32[56,256]{1,0:T(8,128)S(1)}, f32[56,256]{1,0:T(8,128)S(1)}, u32[]{:S(2)}, u32[]{:S(2)}) collective-permute-start(f32[56,256]{1,0:T(8,128)S(1)} %get-tuple-element.32), channel_id=1, source_target_pairs={{1,0},{2,1},{3,2},{4,3},{5,4},{6,5},{7,6},{9,8},{10,9},{11,10},{12... | collective-permute-start | bytes 172040 | tf_op jit(solution)/shard_map/ppermute | solution.py:25
  40.8 4.0 %collective-permute-start.2 = (f32[32,256]{1,0:T(8,128)S(1)}, f32[32,256]{1,0:T(8,128)S(1)}, u32[]{:S(2)}, u32[]{:S(2)}) collective-permute-start(f32[32,256]{1,0:T(8,128)S(1)} %get-tuple-element.31.first), channel_id=1, source_target_pairs={{0,1},{1,2},{2,3},{3,4},{4,5},{5,6},{6,7},{8,9},{9,10},{10,11},{11... | collective-permute-start | bytes 98312 | tf_op jit(solution)/shard_map/ppermute | solution.py:25
  134.6 4.4 %collective-permute-start.5 = (f32[8,32]{1,0:T(8,128)S(1)}, f32[8,32]{1,0:T(8,128)S(1)}, u32[]{:S(2)}, u32[]{:S(2)}) collective-permute-start(f32[8,32]{1,0:T(8,128)S(1)} %slice_bitcast_fusion), channel_id=1, source_target_pairs={{32,0},{64,32},{96,64},{128,96},{160,128},{192,160},{224,192},{33,... | collective-permute-start | bytes 3080 | tf_op jit(solution)/shard_map/ppermute | solution.py:25
  139.0 4.4 %collective-permute-start.6 = (f32[7,32]{1,0:T(8,128)S(1)}, f32[7,32]{1,0:T(8,128)S(1)}, u32[]{:S(2)}, u32[]{:S(2)}) collective-permute-start(f32[7,32]{1,0:T(8,128)S(1)} %pad_maximum_fusion), channel_id=1, source_target_pairs={{8,0},{16,8},{24,16},{9,1},{17,9},{25,17},{10,2},{18,10},{26,18},{... | collective-permute-start | bytes 2696 | tf_op jit(solution)/shard_map/ppermute | solution.py:25

commit v7 on v6

--- a/solution.py
+++ b/solution.py
@@ -1,6 +1,5 @@
 import functools
 
-import numpy as np
 import jax
 import jax.numpy as jnp
 from jax import lax
@@ -82,20 +81,6 @@
     return dot_back(weights, first) + dot_back(weights, second)
 
 
-def two_restrictions(distance):
-    return np.maximum(0.0, 4.0 - np.abs(distance)) / 16.0
-
-
-def restriction_weights(fine):
-    cell = 4.0 * (np.arange(fine // 4 + 2) - 1)[:, None]
-    at = np.arange(fine)[None, :]
-    own = two_restrictions(cell - at)
-    through_before = two_restrictions(cell - (at - 1))
-    beside = through_before + two_restrictions(cell - (at + 1))
-    before = np.where(at == 0, through_before, 0.0)
-    return own, beside, before
-
-
 def weight_rows(coarse, fine, kind, missing):
     rows = lax.broadcasted_iota(jnp.int32, (coarse * coarse, coarse * fine), 0)
     columns = lax.broadcasted_iota(jnp.int32, (coarse * coarse, coarse * fine), 1)
@@ -121,12 +106,25 @@
     return weight(cell - at - 1) + (1.0 - before) * weight(cell - at + 1)
 
 
+def restricted_layers(layers):
+    out = {}
+    for x, layer in layers.items():
+        if x % 2 == 0:
+            shares = [(x // 2, 0.5)]
+        else:
+            shares = [((x - 1) // 2, 0.25), ((x + 1) // 2, 0.25)]
+        for cell, weight in shares:
+            term = weight * layer
+            out[cell] = out[cell] + term if cell in out else term
+    return out
+
+
 def restrict_body(
-    own, beside, before, order_in, rhs_in, iterate_in, coefficient_in, inner, upper,
+    order_in, rhs_in, iterate_in, coefficient_in, inner, upper,
     rhs, iterate, coefficient, order, arrived,
 ):
     count, fine = rhs.shape[:2]
-    coarse = own.shape[0]
+    coarse = inner.shape[1]
     half = fine // 2
     copies = [pltpu.make_async_copy(coefficient_in, coefficient, arrived.at[0])]
     for r in range(count):
@@ -158,23 +156,17 @@
             copy.wait()
         planes = [iterate[r, x] for x in range(fine)]
         gaps = [rhs[r, x] - (6.0 + coefficient[x]) * planes[x] for x in range(fine)]
-        values, cells = [], []
-        for i in range(coarse):
-            value = cell = None
-            for x in range(fine):
-                if own[i, x]:
-                    term = float(own[i, x]) * gaps[x]
-                    value = term if value is None else value + term
-                    term = float(own[i, x]) * planes[x]
-                    cell = term if cell is None else cell + term
-                if beside[i, x]:
-                    weight = float(beside[i, x])
-                    if before[i, x]:
-                        weight = weight - at_x * float(before[i, x])
-                    term = weight * planes[x]
-                    value = term if value is None else value + term
-            values.append(value)
-            cells.append(jnp.zeros_like(planes[0]) if cell is None else cell)
+        sums = {-1: (1.0 - at_x) * planes[0], fine: planes[-1]}
+        for x in range(fine):
+            total = gaps[x]
+            for beside in (x - 1, x + 1):
+                if 0 <= beside < fine:
+                    total = total + planes[beside]
+            sums[x] = total
+        values = restricted_layers(restricted_layers(sums))
+        cells = restricted_layers(restricted_layers(dict(enumerate(planes))))
+        values = [values[i] for i in range(-1, coarse - 1)]
+        cells = [jnp.zeros_like(planes[0])] + [cells[i] for i in range(coarse - 1)]
         value = jnp.concatenate(values, axis=0)
         cell = jnp.concatenate(cells, axis=0)
         term = times_weights(value, z_cells[r]) + times_weights(cell, z_pairs[r])
@@ -192,16 +184,12 @@
 
 def restricted(order, right_side, iterate, coefficient):
     count, fine = right_side.shape[:2]
-    own, beside, before = restriction_weights(fine)
-    coarse = own.shape[0]
-
-    def body(*refs):
-        restrict_body(own, beside, before, *refs)
+    coarse = fine // 4 + 2
 
     inner = jax.ShapeDtypeStruct((coarse - 1, coarse, coarse * count), jnp.float32)
     upper = jax.ShapeDtypeStruct((2 * coarse, 128), jnp.float32)
     return pl.pallas_call(
-        body,
+        restrict_body,
         out_shape=(inner, upper),
         in_specs=[HBM] * 4,
         out_specs=(VMEM,) * 2,
@@ -348,6 +336,8 @@
     )(*sources)
 
 
+AFTER, BEFORE, RIDING = 32, 128, 64
+
 LAYER = 32
 
 
@@ -371,17 +361,13 @@
     )(inner, from_x, beside)
 
 
-def first_body(
-    sizes, side, total, inner, from_x, from_y, pack, first, below, above, cells_out, pieces
-):
-    count = pieces.shape[1] // 4
-    peers = pieces.shape[0]
-    first_size = sizes[1]
-    leaf_size = sizes[0]
+def own_body(sizes, side, total, inner, from_x, from_y, pack, first, cells_out, terms, other):
+    leaf_size, first_size = sizes[:2]
     leaf_order, first_order = packed_order(pack, sizes)[:2]
     values = inner[...]
     across, along, lanes = values.shape
     reach = across * along
+    count = terms.shape[0]
     row = lax.broadcasted_iota(jnp.int32, values.shape, 0)
     values = values + jnp.where(row == 1, from_x[0:along, 0:lanes][None], 0.0)
     row = lax.broadcasted_iota(jnp.int32, values.shape, 1)
@@ -392,45 +378,49 @@
     number = numbers(side, "in")
     leaf_rhs = picked(cells, count, side, number, leaf_order)
     first_rhs = picked(cells, count, side, number, first_order)
-    after = cells[(side + 1) * count : (side + 2) * count]
-    before = cells[0:count]
     leaf = pack[LEAF : LEAF + leaf_size, 0:leaf_size]
     to_first = pack[TO_FIRST : TO_FIRST + 2 * first_size, 0:leaf_size]
     toward = product_back(product(leaf_rhs, leaf), to_first)
-    whole = total
-    own_rows = first[0:first_size, 0:whole]
-    below_rows = below[0:first_size, 0:whole]
+    terms[...] = product(first_rhs - toward[:, :first_size], first[0:first_size, 0:total])
+    other[...] = toward[:, first_size:]
+
+
+def first_body(sizes, side, total, cells, own_terms, other, first, below, above, pieces):
+    peers, count = pieces.shape[:2]
+    first_size = sizes[1]
+    reach = cells.shape[1]
+    after = cells[(side + 1) * count : (side + 2) * count, :]
+    before = cells[0:count, :]
     below_order = below[first_size : first_size + 1, 0 : sum(sizes)]
     below_order = split_order(below_order, sizes)[1]
-    from_before = times_weights(before, one_hot(number + float(side - 1), below_order))
-    through = product(after, above[:, whole : whole + 2 * first_size])
-    above_rows = above[0:first_size, 0:whole]
-    terms = product(first_rhs - toward[:, :first_size] - through[:, first_size:], own_rows)
-    terms = terms + product(from_before - toward[:, first_size:], below_rows)
-    terms = terms - product(through[:, :first_size], above_rows)
+    number = numbers(side, "in") + float(side - 1)
+    from_before = times_weights(before, one_hot(number, below_order))
+    through = product(after, above[:, total : total + 2 * first_size])
+    terms = own_terms[...] - product(through[:, first_size:], first[0:first_size, 0:total])
+    terms = terms + product(from_before - other[...], below[0:first_size, 0:total])
+    terms = terms - product(through[:, :first_size], above[0:first_size, 0:total])
     pieces[...] = jnp.zeros_like(pieces)
     place = lax.axis_index("gz")
     for p in range(peers):
-        pieces[p, 0:count, 0:first_size] = terms[:, p * first_size : (p + 1) * first_size]
-        pieces[p, count : 2 * count, 0:reach] = jnp.where(place + 1 == p, after, 0.0)
-        pieces[p, 2 * count : 3 * count, 0:reach] = jnp.where(place - 1 == p, before, 0.0)
+        pieces[p, :, 0:first_size] = terms[:, p * first_size : (p + 1) * first_size]
+        pieces[p, :, AFTER : AFTER + reach] = jnp.where(place + 1 == p, after, 0.0)
+        pieces[p, :, BEFORE : BEFORE + reach] = jnp.where(place - 1 == p, before, 0.0)
 
 
 def second_body(
     sizes, side, gz, received, cells, from_x, pack, second, below, pieces, leaf_out, first_out,
     toward_out, top_out,
 ):
-    peers, rows = pieces.shape[:2]
-    count = rows // 2
+    peers, count = pieces.shape[:2]
     leaf_size, first_size, second_size, top_size = sizes
     reach = cells.shape[1]
     total = received[0]
     for p in range(1, received.shape[0]):
         total = total + received[p]
-    first_own = total[0:count, 0:first_size]
+    first_own = total[:, 0:first_size]
     cells = cells[...]
-    after = total[count : 2 * count, 0:reach]
-    before = total[2 * count : 3 * count, 0:reach]
+    after = total[:, AFTER : AFTER + reach]
+    before = total[:, BEFORE : BEFORE + reach]
     cells = jnp.concatenate(
         [
             cells[0:count],
@@ -462,8 +452,9 @@
     pieces[...] = jnp.zeros_like(pieces)
     place = (lax.axis_index("gy") - 1) * gz + lax.axis_index("gz")
     for p in range(peers):
-        pieces[p, 0:count, 0:second_size] = terms[:, p * second_size : (p + 1) * second_size]
-        pieces[p, count : 2 * count, 0:top_size] = jnp.where(place == p, top_before, 0.0)
+        pieces[p, :, 0:second_size] = terms[:, p * second_size : (p + 1) * second_size]
+        riding = jnp.where(place == p, top_before, 0.0)
+        pieces[p, :, RIDING : RIDING + top_size] = riding
     leaf_out[...] = leaf_solved
     first_out[...] = first_own
     toward = product_back(leaf_solved, to_top) + product(first_own, first_top)
@@ -516,11 +507,11 @@
     total = received[0]
     for p in range(1, received.shape[0]):
         total = total + received[p]
-    second_own = total[0:count, 0:second_size]
+    second_own = total[:, 0:second_size]
     second_out[...] = second_own
     second_top = pack[SECOND_TOP : SECOND_TOP + second_size, 0 : 2 * top_size]
     toward = toward[...] + product(second_own, second_top)
-    own = rhs[...] + total[count : 2 * count, 0:top_size] - toward[:, :top_size]
+    own = rhs[...] + total[:, RIDING : RIDING + top_size] - toward[:, :top_size]
     other = toward[:, top_size:]
     width = pieces.shape[2]
     vectors = []
@@ -594,7 +585,6 @@
     sizes, side, whole, second, below, first_gap, leaf_gap, top_back, pack, sent, base_out,
     second_out,
 ):
-    count = whole.shape[0]
     leaf_size, first_size, second_size, _ = sizes
     reach = side * 8
     own = product_back(whole[...], second[0:second_size, :])
@@ -613,8 +603,8 @@
     face = face + times_weights_back(own, one_hot(number, second_order))
     face = face + times_weights_back(top_back[...], one_hot(number, top_order))
     sent[...] = jnp.zeros_like(sent)
-    sent[0:count, 0:first_size] = gap
-    sent[count : 2 * count, 0:reach] = face
+    sent[:, 0:first_size] = gap
+    sent[:, RIDING : RIDING + reach] = face
 
 
 def leaf_back_body(
@@ -624,7 +614,7 @@
     peers = received.shape[0]
     leaf_size, first_size, _, _ = sizes
     reach = side * 8
-    whole = jnp.concatenate([received[p, 0:count, 0:first_size] for p in range(peers)], axis=1)
+    whole = jnp.concatenate([received[p, :, 0:first_size] for p in range(peers)], axis=1)
     total = whole.shape[1]
     own = product_back(whole, first[0:first_size, 0:total])
     lower = product_back(whole, below[0:first_size, 0:total])
@@ -635,7 +625,8 @@
     face = jnp.zeros((count, reach), jnp.float32)
     place = lax.axis_index("gz") + 1
     for p in range(peers):
-        face = face + jnp.where(place == p, received[p, count : 2 * count, 0:reach], 0.0)
+        riding = received[p, :, RIDING : RIDING + reach]
+        face = face + jnp.where(place == p, riding, 0.0)
     through = above[:, total : total + 2 * first_size]
     moved = product_back(following, through[:, :first_size])
     moved = moved + product_back(own, through[:, first_size:])
@@ -662,6 +653,7 @@
 def prolong_body(inner, after_x, after_y, target, out, sent):
     count, fine = out.shape[:2]
     copies = []
+    half = inner.shape[0] // 2
     cells = inner.shape[0] + 1
     window = jnp.concatenate([inner[...], after_x[...][None]], axis=0)
     row = lax.broadcasted_iota(jnp.int32, window.shape, 1)
@@ -686,8 +678,14 @@
                 if q:
                     value = (1.0 - q / 4.0) * value + (q / 4.0) * planes[i + 1]
                 out[r, 4 * i + q] = value
-        copies.append(pltpu.make_async_copy(out.at[r], target.at[r], sent.at[r]))
-        copies[r].start()
+            if (i + 1) % half == 0:
+                part = pl.ds(4 * (i + 1 - half), 4 * half)
+                copies.append(
+                    pltpu.make_async_copy(
+                        out.at[r, part], target.at[r, part], sent.at[len(copies)]
+                    )
+                )
+                copies[-1].start()
     for copy in copies:
         copy.wait()
 
@@ -700,7 +698,7 @@
         out_specs=HBM,
         scratch_shapes=[
             pltpu.VMEM((count, fine, fine, fine), jnp.float32),
-            pltpu.SemaphoreType.DMA((count,)),
+            pltpu.SemaphoreType.DMA((2 * count,)),
         ],
         compiler_params=LIMIT,
         name="prolong_twice",
@@ -788,14 +786,23 @@
     beside = with_layer(inner, from_x, beside)
     second_below = shifted(beside, "gy", 1)
 
-    turned, pieces = call(
-        functools.partial(first_body, sizes, side, first.shape[2]),
-        [(lanes, lanes_of(side)), (gz, 4 * count, 128)],
+    total = first.shape[2]
+    turned, own_terms, other = call(
+        functools.partial(own_body, sizes, side, total),
+        [(lanes, lanes_of(side)), (count, total), (count, first_size)],
         inner,
         from_x,
         second_below,
         pack,
         up,
+    )
+    (pieces,) = call(
+        functools.partial(first_body, sizes, side, total),
+        [(gz, count, 256)],
+        turned,
+        own_terms,
+        other,
+        up,
         first_below,
         first_above,
     )
@@ -803,7 +810,7 @@
     pieces, leaf_solved, first_own, toward, top_rhs = call(
         functools.partial(second_body, sizes, side, gz),
         [
-            (plane_peers, 2 * count, 128),
+            (plane_peers, count, 128),
             (count, leaf_size),
             (count, first_size),
             (count, 2 * top_size),
@@ -848,7 +855,7 @@
     second_whole = jnp.moveaxis(sent_to_all(second_gap, PLANE), 0, 1).reshape(count, -1)
     sent, base, second_back = call(
         functools.partial(second_back_body, sizes, side),
-        [(2 * count, 128), (count, leaf_size), (count, second_size)],
+        [(count, 128), (count, leaf_size), (count, second_size)],
         second_whole,
         beside,
         second_below,

time: 146 us -> 145 us (level)
    pallas_call x8 -> x9, Pallas kernels: 5.95 us -> 6.46 us  [call(): pl.pallas_call(body, out_shape=shapes, in_specs=[VMEM] * len(operands), o...]
where the time goes in v7:
time: 145 us; the launch traced here: 144 us
  blocking collectives  83.1 us (57%)
  waiting for transfers between devices  27.2 us (19%)
  starting transfers between devices  20.6 us (14%)
  Pallas kernels  11.2 us (8%)
  local copies, waits for them, and re-layouts  1.6 us (1%)
    all_to_all x7, blocking collectives, exchanged(): return lax.all_to_all(pieces, axis, split_axis=0, concat_axis=0, tiled=True)  83.1 us
    ppermute x7, waiting for transfers between devices, shifted(): return lax.ppermute(shard, axis, pairs)  27.2 us
    ppermute x7, starting transfers between devices, shifted(): return lax.ppermute(shard, axis, pairs)  20.6 us
    pallas_call x9, Pallas kernels, call(): pl.pallas_call(body, out_shape=shapes, in_specs=[VMEM] * len(operands), o...  6.46 us
  transfers between devices with their start and end apart: 7, of which 4 were waited for; matrix products, arithmetic and copies ran while one was open for 0% of the time, Pallas kernels for 4%

profile of v7, /device:TPU:1, one launch (start us, length us, event | category | flops | bytes accessed | tf_op | source)
XLA Modules:
  0.0 143.9 jit_solution(6877636735886146771)
XLA Ops:
  0.0 0.0 copy-start
  0.0 1.4 copy-done
  1.4 0.1 fold.1
  1.5 4.4 %collective-permute-start.4 = (f32[8,41472]{1,0:T(8,128)S(1)}, f32[8,41472]{1,0:T(8,128)S(1)}, u32[]{:S(2)}, u32[]{:S(2)}) collective-permute-start(f32[8,41472]{1,0:T(8,128)S(1)} %fold.1), channel_id=1, source_target_pairs={{0,32},{32,64},{64,96},{96,128},{128,160},{160,192},{192,224},{1,3... | collective-permute-start | bytes 3981320 | tf_op jit(solution)/shard_map/ppermute | solution.py:24
  5.9 0.0 copy-start.2
  5.9 0.0 copy-start.3
  6.0 0.0 copy-start.4
  6.0 0.0 copy-start.5
  6.0 0.0 copy-start.6
  6.0 0.0 copy-start.7
  6.0 0.0 copy-start.8
  6.0 0.0 copy-start.9
  6.0 0.0 copy-start.10
  6.0 0.0 copy-start.11
  6.1 2.7 %restrict_twice.1 = (f32[7,8,32]{2,1,0:T(8,128)S(1)}, f32[16,128]{1,0:T(8,128)S(1)}) custom-call(s32[1,216]{1,0:T(1,128)} %bitcast.31, f32[4,24,24,24]{3,2,1,0:T(8,128)} %rhs_in.1, f32[4,24,24,24]{3,2,1,0:T(8,128)} %iterate_in.1, f32[24,24,24]{2,1,0:T(8,128)} %coefficient_in.1), custom_call_target="tpu_custom_call" | custom-call | tf_op jit(solution)/shard_map/restrict_twice/pallas_call | solution.py:191
  8.7 0.0 copy-start.1
  8.8 3.6 %collective-permute-start = (f32[16,128]{1,0:T(8,128)S(1)}, f32[16,128]{1,0:T(8,128)S(1)}, u32[]{:S(2)}, u32[]{:S(2)}) collective-permute-start(f32[16,128]{1,0:T(8,128)S(1)} %get-tuple-element.29), channel_id=1, source_target_pairs={{0,32},{32,64},{64,96},{96,128},{128,160},{160,192},{192,224},{1,3... | collective-permute-start | bytes 24584 | tf_op jit(solution)/shard_map/ppermute | solution.py:24
  12.4 0.0 copy-done.2
  12.4 0.0 copy-done.3
  12.4 0.0 copy-done.4
  12.4 0.0 copy-done.5
  12.4 0.0 copy-done.6
  12.4 0.0 copy-done.7
  12.4 0.0 copy-done.8
  12.4 0.0 copy-done.9
  12.4 0.0 copy-done.10
  12.4 0.0 copy-done.11
  12.5 0.5 prepare.1
  13.0 20.8 %collective-permute-done.from_x = f32[16,128]{1,0:T(8,128)S(1)} collective-permute-done((f32[16,128]{1,0:T(8,128)S(1)}, f32[16,128]{1,0:T(8,128)S(1)}, u32[]{:S(2)}, u32[]{:S(2)}) %collective-permute-start) | collective-permute-done | bytes 8224 | tf_op jit(solution)/shard_map/ppermute | solution.py:24
  33.8 3.2 %collective-permute-start.1 = (f32[40,960]{1,0:T(8,128)S(1)}, f32[40,960]{1,0:T(8,128)S(1)}, u32[]{:S(2)}, u32[]{:S(2)}) collective-permute-start(f32[40,960]{1,0:T(8,128)S(1)} %y_message.1.second), channel_id=1, source_target_pairs={{0,8},{8,16},{16,24},{1,9},{9,17},{17,25},{2,10},{10,18},{18,26},{... | collective-permute-start | bytes 460808 | tf_op jit(solution)/shard_map/ppermute | solution.py:24
  37.0 3.7 %collective-permute-start.3 = (f32[56,256]{1,0:T(8,128)S(1)}, f32[56,256]{1,0:T(8,128)S(1)}, u32[]{:S(2)}, u32[]{:S(2)}) collective-permute-start(f32[56,256]{1,0:T(8,128)S(1)} %get-tuple-element.36), channel_id=1, source_target_pairs={{1,0},{2,1},{3,2},{4,3},{5,4},{6,5},{7,6},{9,8},{10,9},{11,10},{12... | collective-permute-start | bytes 172040 | tf_op jit(solution)/shard_map/ppermute | solution.py:24
  40.8 3.0 %collective-permute-start.2 = (f32[32,256]{1,0:T(8,128)S(1)}, f32[32,256]{1,0:T(8,128)S(1)}, u32[]{:S(2)}, u32[]{:S(2)}) collective-permute-start(f32[32,256]{1,0:T(8,128)S(1)} %get-tuple-element.32.first), channel_id=1, source_target_pairs={{0,1},{1,2},{2,3},{3,4},{4,5},{5,6},{6,7},{8,9},{9,10},{10,11},{11... | collective-permute-start | bytes 98312 | tf_op jit(solution)/shard_map/ppermute | solution.py:24
  43.8 0.0 collective-permute-done.1.from_y.below
  43.8 0.7 shard_map.136
  44.5 0.3 collective-permute-done.2.below
  44.8 0.0 collective-permute-done.3.above
  44.8 0.5 shard_map.137
  45.3 10.0 %all_to_all.35.received = f32[8,4,256]{2,1,0:T(4,128)S(1)} all-to-all(f32[8,4,256]{2,1,0:T(4,128)S(1)} %shard_map.137), channel_id=1, replica_groups=mesh['gx'=8,'gy'=4,'gz'=8] {'gz'}, dimensions={0} | all-to-all | bytes 65536 | tf_op jit(solution)/shard_map/all_to_all | solution.py:28
  55.3 1.0 shard_map.138
  56.3 12.8 %all_to_all.36.received = f32[32,4,128]{2,1,0:T(4,128)S(1)} all-to-all(f32[32,4,128]{2,1,0:T(4,128)S(1)} %get-tuple-element.37), channel_id=1, replica_groups=mesh['gx'=8,'gy'=4,'gz'=8] {'gy','gz'}, dimensions={0} | all-to-all | bytes 131072 | tf_op jit(solution)/shard_map/all_to_all | solution.py:28
  69.1 0.0 collective-permute-done.4.below
  69.1 0.0 copy-done.1
  69.1 1.0 shard_map.139
  70.1 11.8 %all_to_all.37.received = f32[32,4,384]{2,1,0:T(4,128)S(1)} all-to-all(f32[32,4,384]{2,1,0:T(4,128)S(1)} %get-tuple-element.40), channel_id=1, replica_groups=mesh['gx'=8,'gy'=4,'gz'=8] {'gy','gz'}, dimensions={0} | all-to-all | bytes 393216 | tf_op jit(solution)/shard_map/all_to_all | solution.py:28
  81.9 16.8 %all_to_all.38.received = f32[8,4,384]{2,1,0:T(4,128)S(1)} all-to-all(f32[8,4,384]{2,1,0:T(4,128)S(1)} %shard_map.140), channel_id=1, replica_groups=mesh['gx'=8,'gy'=4,'gz'=8] {'gx'}, dimensions={0} | all-to-all | bytes 98304 | tf_op jit(solution)/shard_map/all_to_all | solution.py:28
  98.7 13.3 %all_to_all.39.whole = f32[32,4,384]{2,1,0:T(4,128)S(1)} all-to-all(f32[32,4,384]{2,1,0:T(4,128)S(1)} %shard_map.141), channel_id=1, replica_groups=mesh['gx'=8,'gy'=4,'gz'=8] {'gy','gz'}, dimensions={0} | all-to-all | bytes 393216 | tf_op jit(solution)/shard_map/all_to_all | solution.py:28
  112.0 1.5 %shard_map.142 = (f32[4,36]{1,0:T(4,128)S(1)}, f32[4,30]{1,0:T(4,128)S(1)}, f32[4,25]{1,0:T(4,128)S(1)}, f32[4,125]{1,0:T(4,128)S(1)}) custom-call(f32[32,4,384]{2,1,0:T(4,128)S(1)} %all_to_all.39.whole, f32[36,9216]{1,0:T(8,128)S(1)} %copy-done.1, f32[8,41472]{1,0:T(8,128)S(1)} %collective-permute-done.4.below, f32[4,30]{1,0:T(4,128)S(1)} %get-tuple-element.41.second_own, ...), custom_call_target="tpu_custom_call" | custom-call | tf_op jit(solution)/shard_map/pallas_call | solution.py:710
  113.6 10.9 %all_to_all.40 = f32[32,4,30]{2,1,0:T(4,128)S(1)} all-to-all(f32[32,4,30]{2,1,0:T(4,128)S(1)} %broadcast_in_dim.6), channel_id=1, replica_groups=mesh['gx'=8,'gy'=4,'gz'=8] {'gy','gz'}, dimensions={0} | all-to-all | bytes 30720 | tf_op jit(solution)/shard_map/all_to_all | solution.py:28
  124.5 0.1 reshape.15.whole
  124.6 0.8 shard_map.143
  125.4 7.4 %all_to_all.41.received = f32[8,4,128]{2,1,0:T(4,128)S(1)} all-to-all(f32[8,4,128]{2,1,0:T(4,128)S(1)} %broadcast_in_dim.7), channel_id=1, replica_groups=mesh['gx'=8,'gy'=4,'gz'=8] {'gz'}, dimensions={0} | all-to-all | bytes 32768 | tf_op jit(solution)/shard_map/all_to_all | solution.py:28
  132.8 0.9 shard_map.144.inner
  133.8 1.3 collective-permute-start.5
  135.1 3.0 %collective-permute-done.5.after_x = f32[8,32]{1,0:T(8,128)S(1)} collective-permute-done((f32[8,32]{1,0:T(8,128)S(1)}, f32[8,32]{1,0:T(8,128)S(1)}, u32[]{:S(2)}, u32[]{:S(2)}) %collective-permute-start.5) | collective-permute-done | bytes 1056 | tf_op jit(solution)/shard_map/ppermute | solution.py:24
  138.2 1.3 collective-permute-start.6
  139.5 3.1 %collective-permute-done.6.after_y = f32[7,32]{1,0:T(8,128)S(1)} collective-permute-done((f32[7,32]{1,0:T(8,128)S(1)}, f32[7,32]{1,0:T(8,128)S(1)}, u32[]{:S(2)}, u32[]{:S(2)}) %collective-permute-start.6) | collective-permute-done | bytes 928 | tf_op jit(solution)/shard_map/ppermute | solution.py:24
  142.5 1.4 prolong_twice.1
  (11 shorter events, 0.1 us)
Async XLA Ops:
  0.0 1.4 copy-start
  1.5 67.6 %collective-permute-start.4 = (f32[8,41472]{1,0:T(8,128)S(1)}, f32[8,41472]{1,0:T(8,128)S(1)}, u32[]{:S(2)}, u32[]{:S(2)}) collective-permute-start(f32[8,41472]{1,0:T(8,128)S(1)} %fold.1), channel_id=1, source_target_pairs={{0,32},{32,64},{64,96},{96,128},{128,160},{160,192},{192,224},{1,3... | collective-permute-start | bytes 3981320 | tf_op jit(solution)/shard_map/ppermute | solution.py:24
  5.9 6.4 %copy-start.2 = (f32[1,30,960]{2,0,1:T(1,128)S(1)}, f32[1,30,960]{2,0,1:T(1,128)}, u32[]{:S(2)}) copy-start(f32[1,30,960]{2,0,1:T(1,128)} %param.25) | copy-start | bytes 345604
  5.9 6.4 %copy-start.3 = (f32[1,1,1,125,125]{4,2,3,1,0:T(1,128)S(1)}, f32[1,1,1,125,125]{4,2,3,1,0:T(1,128)}, u32[]{:S(2)}) copy-start(f32[1,1,1,125,125]{4,2,3,1,0:T(1,128)} %param.18) | copy-start | bytes 187504
  6.0 6.4 %copy-start.4 = (f32[1,1,1,125,72]{3,4,2,1,0:T(8,128)S(1)}, f32[1,1,1,125,72]{3,4,2,1,0:T(8,128)}, u32[]{:S(2)}) copy-start(f32[1,1,1,125,72]{3,4,2,1,0:T(8,128)} %param.21) | copy-start | bytes 108004
  6.0 6.4 %copy-start.5 = (f32[1,1,1,125,60]{3,2,4,1,0:T(1,128)S(1)}, f32[1,1,1,125,60]{3,2,4,1,0:T(1,128)}, u32[]{:S(2)}) copy-start(f32[1,1,1,125,60]{3,2,4,1,0:T(1,128)} %param.20) | copy-start | bytes 90004
  6.0 6.4 %copy-start.6 = (f32[1,1,1,125,50]{3,2,4,1,0:T(1,128)S(1)}, f32[1,1,1,125,50]{3,2,4,1,0:T(1,128)}, u32[]{:S(2)}) copy-start(f32[1,1,1,125,50]{3,2,4,1,0:T(1,128)} %param.19) | copy-start | bytes 75004
  6.0 6.4 %copy-start.7 = (f32[1,1,25,200]{3,1,2,0:T(1,128)S(1)}, f32[1,1,25,200]{3,1,2,0:T(1,128)}, u32[]{:S(2)}) copy-start(f32[1,1,25,200]{3,1,2,0:T(1,128)} %param.22) | copy-start | bytes 60004
  6.0 6.4 %copy-start.8 = (f32[1,1,1,30,72]{4,2,3,1,0:T(1,128)S(1)}, f32[1,1,1,30,72]{4,2,3,1,0:T(1,128)}, u32[]{:S(2)}) copy-start(f32[1,1,1,30,72]{4,2,3,1,0:T(1,128)} %param.26) | copy-start | bytes 25924
  6.0 6.4 %copy-start.9 = (f32[1,1,1,25,60]{4,2,3,1,0:T(1,128)S(1)}, f32[1,1,1,25,60]{4,2,3,1,0:T(1,128)}, u32[]{:S(2)}) copy-start(f32[1,1,1,25,60]{4,2,3,1,0:T(1,128)} %param.23) | copy-start | bytes 18004
  6.0 6.4 %copy-start.10 = (f32[1,1,1,25,72]{4,2,3,1,0:T(1,128)S(1)}, f32[1,1,1,25,72]{4,2,3,1,0:T(1,128)}, u32[]{:S(2)}) copy-start(f32[1,1,1,25,72]{4,2,3,1,0:T(1,128)} %param.24) | copy-start | bytes 21604
  6.0 6.4 %copy-start.11 = (s32[1,1,1,216]{3,2,1,0:T(1,128)S(1)}, s32[1,1,1,216]{3,2,1,0:T(1,128)}, u32[]{:S(2)}) copy-start(s32[1,1,1,216]{3,2,1,0:T(1,128)} %param.17) | copy-start | bytes 2596
  8.7 60.3 %copy-start.1 = (f32[36,9216]{1,0:T(8,128)S(1)}, f32[36,9216]{1,0:T(8,128)}, u32[]{:S(2)}) copy-start(f32[36,9216]{1,0:T(8,128)} %top.5) | copy-start | bytes 3981316
  8.8 25.1 %collective-permute-start = (f32[16,128]{1,0:T(8,128)S(1)}, f32[16,128]{1,0:T(8,128)S(1)}, u32[]{:S(2)}, u32[]{:S(2)}) collective-permute-start(f32[16,128]{1,0:T(8,128)S(1)} %get-tuple-element.29), channel_id=1, source_target_pairs={{0,32},{32,64},{64,96},{96,128},{128,160},{160,192},{192,224},{1,3... | collective-permute-start | bytes 24584 | tf_op jit(solution)/shard_map/ppermute | solution.py:24
  33.8 10.0 %collective-permute-start.1 = (f32[40,960]{1,0:T(8,128)S(1)}, f32[40,960]{1,0:T(8,128)S(1)}, u32[]{:S(2)}, u32[]{:S(2)}) collective-permute-start(f32[40,960]{1,0:T(8,128)S(1)} %y_message.1.second), channel_id=1, source_target_pairs={{0,8},{8,16},{16,24},{1,9},{9,17},{17,25},{2,10},{10,18},{18,26},{... | collective-permute-start | bytes 460808 | tf_op jit(solution)/shard_map/ppermute | solution.py:24
  37.0 7.8 %collective-permute-start.3 = (f32[56,256]{1,0:T(8,128)S(1)}, f32[56,256]{1,0:T(8,128)S(1)}, u32[]{:S(2)}, u32[]{:S(2)}) collective-permute-start(f32[56,256]{1,0:T(8,128)S(1)} %get-tuple-element.36), channel_id=1, source_target_pairs={{1,0},{2,1},{3,2},{4,3},{5,4},{6,5},{7,6},{9,8},{10,9},{11,10},{12... | collective-permute-start | bytes 172040 | tf_op jit(solution)/shard_map/ppermute | solution.py:24
  40.8 4.0 %collective-permute-start.2 = (f32[32,256]{1,0:T(8,128)S(1)}, f32[32,256]{1,0:T(8,128)S(1)}, u32[]{:S(2)}, u32[]{:S(2)}) collective-permute-start(f32[32,256]{1,0:T(8,128)S(1)} %get-tuple-element.32.first), channel_id=1, source_target_pairs={{0,1},{1,2},{2,3},{3,4},{4,5},{5,6},{6,7},{8,9},{9,10},{10,11},{11... | collective-permute-start | bytes 98312 | tf_op jit(solution)/shard_map/ppermute | solution.py:24
  133.8 4.4 %collective-permute-start.5 = (f32[8,32]{1,0:T(8,128)S(1)}, f32[8,32]{1,0:T(8,128)S(1)}, u32[]{:S(2)}, u32[]{:S(2)}) collective-permute-start(f32[8,32]{1,0:T(8,128)S(1)} %slice_bitcast_fusion), channel_id=1, source_target_pairs={{32,0},{64,32},{96,64},{128,96},{160,128},{192,160},{224,192},{33,... | collective-permute-start | bytes 3080 | tf_op jit(solution)/shard_map/ppermute | solution.py:24
  138.2 4.4 %collective-permute-start.6 = (f32[7,32]{1,0:T(8,128)S(1)}, f32[7,32]{1,0:T(8,128)S(1)}, u32[]{:S(2)}, u32[]{:S(2)}) collective-permute-start(f32[7,32]{1,0:T(8,128)S(1)} %pad_maximum_fusion), channel_id=1, source_target_pairs={{8,0},{16,8},{24,16},{9,1},{17,9},{25,17},{10,2},{18,10},{26,18},{... | collective-permute-start | bytes 2696 | tf_op jit(solution)/shard_map/ppermute | solution.py:24

commit v8 on v7

--- a/solution.py
+++ b/solution.py
@@ -120,8 +120,8 @@
 
 
 def restrict_body(
-    order_in, rhs_in, iterate_in, coefficient_in, inner, upper,
-    rhs, iterate, coefficient, order, arrived,
+    order_in, rhs_in, iterate_in, coefficient_in, top_in, inner, upper, folds,
+    rhs, iterate, coefficient, order, top, arrived,
 ):
     count, fine = rhs.shape[:2]
     coarse = inner.shape[1]
@@ -137,6 +137,7 @@
                     )
                 )
     copies.append(pltpu.make_async_copy(order_in, order, arrived.at[len(copies)]))
+    copies.append(pltpu.make_async_copy(top_in, top, arrived.at[len(copies)]))
     for copy in copies:
         copy.start()
     at_x, at_y, at_z = [jnp.where(lax.axis_index(a) == 0, 1.0, 0.0) for a in AXES]
@@ -177,32 +178,36 @@
     result = result.reshape(coarse, coarse, coarse * count)
     inner[...] = result[:-1]
     upper[0:layer, 0:lanes] = result[coarse - 1]
+    copies[-2].wait()
     copies[-1].wait()
+    fold_body(top, folds)
     orders = order[...].astype(jnp.float32)
     upper[layer : layer + 1, 0:top_size] = orders[:, orders.shape[1] - top_size :]
 
 
-def restricted(order, right_side, iterate, coefficient):
+def restricted(order, right_side, iterate, coefficient, top):
     count, fine = right_side.shape[:2]
     coarse = fine // 4 + 2
 
     inner = jax.ShapeDtypeStruct((coarse - 1, coarse, coarse * count), jnp.float32)
     upper = jax.ShapeDtypeStruct((2 * coarse, 128), jnp.float32)
+    folds = jax.ShapeDtypeStruct((8, top.size // 8), jnp.float32)
     return pl.pallas_call(
         restrict_body,
-        out_shape=(inner, upper),
-        in_specs=[HBM] * 4,
-        out_specs=(VMEM,) * 2,
+        out_shape=(inner, upper, folds),
+        in_specs=[HBM] * 5,
+        out_specs=(VMEM,) * 3,
         scratch_shapes=[
             pltpu.VMEM(right_side.shape, jnp.float32),
             pltpu.VMEM(iterate.shape, jnp.float32),
             pltpu.VMEM(coefficient.shape, jnp.float32),
             pltpu.VMEM(order.shape, order.dtype),
-            pltpu.SemaphoreType.DMA((4 * count + 2,)),
+            pltpu.VMEM(top.shape, jnp.float32),
+            pltpu.SemaphoreType.DMA((4 * count + 3,)),
         ],
         compiler_params=LIMIT,
         name="restrict_twice",
-    )(*map(in_hbm, (order, right_side, iterate, coefficient)))
+    )(*map(in_hbm, (order, right_side, iterate, coefficient, top)))
 
 
 def numbers(side, kind):
@@ -475,19 +480,6 @@
     out[4:8, start : start + half] = top[8 * full : rows, half:columns]
 
 
-def folded(top):
-    rows, columns = top.shape
-    assert rows % 8 == 4
-    return pl.pallas_call(
-        fold_body,
-        out_shape=jax.ShapeDtypeStruct((8, columns * rows // 8), jnp.float32),
-        in_specs=[VMEM],
-        out_specs=VMEM,
-        compiler_params=LIMIT,
-        name="fold",
-    )(top)
-
-
 def unfolded(folds, rows, columns, start, width):
     full = rows // 8
     parts = []
@@ -500,7 +492,7 @@
     return jnp.concatenate(parts, axis=0)
 
 
-def top_body(used, received, toward, rhs, pack, top, below, pieces, second_out):
+def top_body(used, shape, received, toward, rhs, pack, top, below, pieces, second_out):
     count = toward.shape[0]
     second_size = second_out.shape[1]
     top_size = rhs.shape[1]
@@ -520,11 +512,9 @@
         both = jnp.concatenate([high.astype(jnp.float32), low.astype(jnp.float32)], axis=0)
         vectors.append((both.astype(jnp.bfloat16), high))
     for p in range(used):
-        at = slice(p * width, (p + 1) * width)
         total = None
-        lower = unfolded(below, *top.shape, p * width, width)
-        for (both, high), rows in zip(vectors, (top[:, at], lower)):
-            first, second = parts_of(rows)
+        for (both, high), folds in zip(vectors, (top, below)):
+            first, second = parts_of(unfolded(folds, *shape, p * width, width))
             term = dot(both, first)
             term = term[:count] + (term[count:] + dot(high, second))
             total = term if total is None else total + term
@@ -542,22 +532,20 @@
 
 
 def top_back_body(
-    used, whole, top, below, second_own, first_own, leaf_solved, pack, pair_out, second_gap,
+    used, shape, whole, top, below, second_own, first_own, leaf_solved, pack, pair_out, second_gap,
     first_gap, leaf_gap,
 ):
     count = whole.shape[1]
     width = whole.shape[2]
-    top_size = top.shape[0]
+    top_size = shape[0]
 
     halves = []
-    for fold in (False, True):
+    for folds in (top, below):
         total = None
         for p in range(used):
-            at = slice(p * width, (p + 1) * width)
             high, low = parts_of(whole[p])
             both = jnp.concatenate([high.astype(jnp.float32), low.astype(jnp.float32)], axis=0)
-            rows = unfolded(below, *top.shape, p * width, width) if fold else top[:, at]
-            first, second = parts_of(rows)
+            first, second = parts_of(unfolded(folds, *shape, p * width, width))
             term = dot_back(both.astype(jnp.bfloat16), first)
             term = term[:count] + (term[count:] + dot_back(high, second))
             total = term if total is None else total + term
@@ -761,7 +749,7 @@
     second = jnp.transpose(second_inverse, (1, 0, 2))
     order = ordering.reshape(1, cells)
 
-    inner, upper = restricted(order, right_side, iterate, coefficient)
+    inner, upper, folds = restricted(order, right_side, iterate, coefficient, top_inverse)
     from_x = shifted(upper, "gx", 1)
     whole_first = -(-max(first.shape[2] + 2 * first_size, cells) // 128) * 128
     up, down, beside, pack = prepared(
@@ -781,7 +769,6 @@
     )
     first_below = shifted(up, "gz", 1)
     first_above = shifted(down, "gz", -1)
-    folds = folded(top_inverse)
     top_below = shifted(folds, "gx", 1)
     beside = with_layer(inner, from_x, beside)
     second_below = shifted(beside, "gy", 1)
@@ -827,13 +814,13 @@
     width = 128 * -(-top_total // (128 * plane_peers))
     used = top_total // width
     pieces, second_own = call(
-        functools.partial(top_body, used),
+        functools.partial(top_body, used, top_inverse.shape),
         [(plane_peers, count, width), (count, second_size)],
         received,
         toward,
         top_rhs,
         pack,
-        top_inverse,
+        folds,
         top_below,
     )
     received = exchanged(pieces, PLANE)
@@ -842,10 +829,10 @@
     (pieces,) = call(spread_sum_body, [(plane_peers, count, width)], received)
     received = exchanged(pieces, PLANE)
     top_back, second_gap, first_gap, leaf_gap = call(
-        functools.partial(top_back_body, used),
+        functools.partial(top_back_body, used, top_inverse.shape),
         [(count, top_size), (count, second_size), (count, first_size), (count, leaf_size)],
         received,
-        top_inverse,
+        folds,
         top_below,
         second_own,
         first_own,

time: 145 us -> 147 us (1.014)
  waiting for transfers between devices: 27.2 us -> 30.1 us
    ppermute x7, waiting for transfers between devices: 27.2 us -> 30.1 us  [shifted(): return lax.ppermute(shard, axis, pairs)]
  transfers between devices with their start and end apart: 7 -> 7, of which waited for: 4 -> 4; matrix products, arithmetic and copies ran while one was open for 0% -> 0% of each run, Pallas kernels for 4% -> 2%
where the time goes in v8:
time: 147 us; the launch traced here: 145 us
  blocking collectives  83.1 us (57%)
  waiting for transfers between devices  30.1 us (20%)
  starting transfers between devices  20.4 us (14%)
  Pallas kernels  11.2 us (8%)
    all_to_all x7, blocking collectives, exchanged(): return lax.all_to_all(pieces, axis, split_axis=0, concat_axis=0, tiled=True)  83.1 us
    ppermute x7, waiting for transfers between devices, shifted(): return lax.ppermute(shard, axis, pairs)  30.1 us
    ppermute x7, starting transfers between devices, shifted(): return lax.ppermute(shard, axis, pairs)  20.4 us
    pallas_call x9, Pallas kernels, call(): pl.pallas_call(body, out_shape=shapes, in_specs=[VMEM] * len(operands), o...  6.45 us
  transfers between devices with their start and end apart: 7, of which 4 were waited for; matrix products, arithmetic and copies ran while one was open for 0% of the time, Pallas kernels for 2%

profile of v8, /device:TPU:1, one launch (start us, length us, event | category | flops | bytes accessed | tf_op | source)
XLA Modules:
  0.0 145.4 jit_solution(9678517386969397100)
XLA Ops:
  0.0 0.0 copy-start
  0.0 0.0 copy-start.1
  0.0 0.0 copy-start.2
  0.0 0.0 copy-start.3
  0.0 0.0 copy-start.4
  0.0 0.0 copy-start.5
  0.0 0.0 copy-start.6
  0.0 0.0 copy-start.7
  0.1 0.0 copy-start.8
  0.1 0.0 copy-start.9
  0.1 2.8 %restrict_twice.1 = (f32[7,8,32]{2,1,0:T(8,128)S(1)}, f32[16,128]{1,0:T(8,128)S(1)}, f32[8,41472]{1,0:T(8,128)S(1)}) custom-call(s32[1,216]{1,0:T(1,128)} %bitcast.31, f32[4,24,24,24]{3,2,1,0:T(8,128)} %rhs_in.1, f32[4,24,24,24]{3,2,1,0:T(8,128)} %iterate_in.1, f32[24,24,24]{2,1,0:T(8,128)} %coefficient_in.1, f32[36,9216]{1,0:T(8,128)} %top_in.1), custom_call_target="tpu_custom_call" | custom-call | tf_op jit(solution)/shard_map/restrict_twice/pallas_call | solution.py:195
  2.9 4.4 %collective-permute-start.4 = (f32[8,41472]{1,0:T(8,128)S(1)}, f32[8,41472]{1,0:T(8,128)S(1)}, u32[]{:S(2)}, u32[]{:S(2)}) collective-permute-start(f32[8,41472]{1,0:T(8,128)S(1)} %get-tuple-element.41.top), channel_id=1, source_target_pairs={{0,32},{32,64},{64,96},{96,128},{128,160},{160,192},{192,224},{1,3... | collective-permute-start | bytes 3981320 | tf_op jit(solution)/shard_map/ppermute | solution.py:24
  7.4 3.5 %collective-permute-start = (f32[16,128]{1,0:T(8,128)S(1)}, f32[16,128]{1,0:T(8,128)S(1)}, u32[]{:S(2)}, u32[]{:S(2)}) collective-permute-start(f32[16,128]{1,0:T(8,128)S(1)} %get-tuple-element.30), channel_id=1, source_target_pairs={{0,32},{32,64},{64,96},{96,128},{128,160},{160,192},{192,224},{1,3... | collective-permute-start | bytes 24584 | tf_op jit(solution)/shard_map/ppermute | solution.py:24
  10.8 0.0 copy-done
  10.8 0.0 copy-done.1
  10.8 0.0 copy-done.2
  10.9 0.0 copy-done.3
  10.9 0.0 copy-done.4
  10.9 0.0 copy-done.5
  10.9 0.0 copy-done.6
  10.9 0.0 copy-done.7
  10.9 0.0 copy-done.8
  10.9 0.0 copy-done.9
  10.9 0.5 prepare.1
  11.5 23.8 %collective-permute-done.from_x = f32[16,128]{1,0:T(8,128)S(1)} collective-permute-done((f32[16,128]{1,0:T(8,128)S(1)}, f32[16,128]{1,0:T(8,128)S(1)}, u32[]{:S(2)}, u32[]{:S(2)}) %collective-permute-start) | collective-permute-done | bytes 8224 | tf_op jit(solution)/shard_map/ppermute | solution.py:24
  35.2 3.2 %collective-permute-start.1 = (f32[40,960]{1,0:T(8,128)S(1)}, f32[40,960]{1,0:T(8,128)S(1)}, u32[]{:S(2)}, u32[]{:S(2)}) collective-permute-start(f32[40,960]{1,0:T(8,128)S(1)} %y_message.1.second), channel_id=1, source_target_pairs={{0,8},{8,16},{16,24},{1,9},{9,17},{17,25},{2,10},{10,18},{18,26},{... | collective-permute-start | bytes 460808 | tf_op jit(solution)/shard_map/ppermute | solution.py:24
  38.5 3.7 %collective-permute-start.3 = (f32[56,256]{1,0:T(8,128)S(1)}, f32[56,256]{1,0:T(8,128)S(1)}, u32[]{:S(2)}, u32[]{:S(2)}) collective-permute-start(f32[56,256]{1,0:T(8,128)S(1)} %get-tuple-element.37), channel_id=1, source_target_pairs={{1,0},{2,1},{3,2},{4,3},{5,4},{6,5},{7,6},{9,8},{10,9},{11,10},{12... | collective-permute-start | bytes 172040 | tf_op jit(solution)/shard_map/ppermute | solution.py:24
  42.2 3.0 %collective-permute-start.2 = (f32[32,256]{1,0:T(8,128)S(1)}, f32[32,256]{1,0:T(8,128)S(1)}, u32[]{:S(2)}, u32[]{:S(2)}) collective-permute-start(f32[32,256]{1,0:T(8,128)S(1)} %get-tuple-element.33.first), channel_id=1, source_target_pairs={{0,1},{1,2},{2,3},{3,4},{4,5},{5,6},{6,7},{8,9},{9,10},{10,11},{11... | collective-permute-start | bytes 98312 | tf_op jit(solution)/shard_map/ppermute | solution.py:24
  45.2 0.0 collective-permute-done.1.from_y.below
  45.2 0.7 shard_map.136
  45.9 0.3 collective-permute-done.2.below
  46.2 0.0 collective-permute-done.3.above
  46.2 0.5 shard_map.137
  46.7 10.0 %all_to_all.35.received = f32[8,4,256]{2,1,0:T(4,128)S(1)} all-to-all(f32[8,4,256]{2,1,0:T(4,128)S(1)} %shard_map.137), channel_id=1, replica_groups=mesh['gx'=8,'gy'=4,'gz'=8] {'gz'}, dimensions={0} | all-to-all | bytes 65536 | tf_op jit(solution)/shard_map/all_to_all | solution.py:28
  56.7 1.0 shard_map.138
  57.7 12.8 %all_to_all.36.received = f32[32,4,128]{2,1,0:T(4,128)S(1)} all-to-all(f32[32,4,128]{2,1,0:T(4,128)S(1)} %get-tuple-element.38), channel_id=1, replica_groups=mesh['gx'=8,'gy'=4,'gz'=8] {'gy','gz'}, dimensions={0} | all-to-all | bytes 131072 | tf_op jit(solution)/shard_map/all_to_all | solution.py:28
  70.5 0.0 collective-permute-done.4.below
  70.5 1.0 shard_map.139
  71.5 11.8 %all_to_all.37.received = f32[32,4,384]{2,1,0:T(4,128)S(1)} all-to-all(f32[32,4,384]{2,1,0:T(4,128)S(1)} %get-tuple-element.42), channel_id=1, replica_groups=mesh['gx'=8,'gy'=4,'gz'=8] {'gy','gz'}, dimensions={0} | all-to-all | bytes 393216 | tf_op jit(solution)/shard_map/all_to_all | solution.py:28
  83.3 16.9 %all_to_all.38.received = f32[8,4,384]{2,1,0:T(4,128)S(1)} all-to-all(f32[8,4,384]{2,1,0:T(4,128)S(1)} %shard_map.140), channel_id=1, replica_groups=mesh['gx'=8,'gy'=4,'gz'=8] {'gx'}, dimensions={0} | all-to-all | bytes 98304 | tf_op jit(solution)/shard_map/all_to_all | solution.py:28
  100.2 13.3 %all_to_all.39.whole = f32[32,4,384]{2,1,0:T(4,128)S(1)} all-to-all(f32[32,4,384]{2,1,0:T(4,128)S(1)} %shard_map.141), channel_id=1, replica_groups=mesh['gx'=8,'gy'=4,'gz'=8] {'gy','gz'}, dimensions={0} | all-to-all | bytes 393216 | tf_op jit(solution)/shard_map/all_to_all | solution.py:28
  113.5 1.5 %shard_map.142 = (f32[4,36]{1,0:T(4,128)S(1)}, f32[4,30]{1,0:T(4,128)S(1)}, f32[4,25]{1,0:T(4,128)S(1)}, f32[4,125]{1,0:T(4,128)S(1)}) custom-call(f32[32,4,384]{2,1,0:T(4,128)S(1)} %all_to_all.39.whole, f32[8,41472]{1,0:T(8,128)S(1)} %get-tuple-element.41.top, f32[8,41472]{1,0:T(8,128)S(1)} %collective-permute-done.4.below, ...), custom_call_target="tpu_custom_call" | custom-call | tf_op jit(solution)/shard_map/pallas_call | solution.py:698
  115.0 10.9 %all_to_all.40 = f32[32,4,30]{2,1,0:T(4,128)S(1)} all-to-all(f32[32,4,30]{2,1,0:T(4,128)S(1)} %broadcast_in_dim.6), channel_id=1, replica_groups=mesh['gx'=8,'gy'=4,'gz'=8] {'gy','gz'}, dimensions={0} | all-to-all | bytes 30720 | tf_op jit(solution)/shard_map/all_to_all | solution.py:28
  126.0 0.1 reshape.15.whole
  126.1 0.8 shard_map.143
  126.9 7.4 %all_to_all.41.received = f32[8,4,128]{2,1,0:T(4,128)S(1)} all-to-all(f32[8,4,128]{2,1,0:T(4,128)S(1)} %broadcast_in_dim.7), channel_id=1, replica_groups=mesh['gx'=8,'gy'=4,'gz'=8] {'gz'}, dimensions={0} | all-to-all | bytes 32768 | tf_op jit(solution)/shard_map/all_to_all | solution.py:28
  134.3 0.9 shard_map.144.inner
  135.3 1.3 collective-permute-start.5
  136.6 3.0 %collective-permute-done.5.after_x = f32[8,32]{1,0:T(8,128)S(1)} collective-permute-done((f32[8,32]{1,0:T(8,128)S(1)}, f32[8,32]{1,0:T(8,128)S(1)}, u32[]{:S(2)}, u32[]{:S(2)}) %collective-permute-start.5) | collective-permute-done | bytes 1056 | tf_op jit(solution)/shard_map/ppermute | solution.py:24
  139.6 1.3 collective-permute-start.6
  140.9 3.1 %collective-permute-done.6.after_y = f32[7,32]{1,0:T(8,128)S(1)} collective-permute-done((f32[7,32]{1,0:T(8,128)S(1)}, f32[7,32]{1,0:T(8,128)S(1)}, u32[]{:S(2)}, u32[]{:S(2)}) %collective-permute-start.6) | collective-permute-done | bytes 928 | tf_op jit(solution)/shard_map/ppermute | solution.py:24
  144.0 1.4 prolong_twice.1
  (11 shorter events, 0.1 us)
Async XLA Ops:
  0.0 10.8 %copy-start = (f32[1,30,960]{2,0,1:T(1,128)S(1)}, f32[1,30,960]{2,0,1:T(1,128)}, u32[]{:S(2)}) copy-start(f32[1,30,960]{2,0,1:T(1,128)} %param.25) | copy-start | bytes 345604
  0.0 10.8 %copy-start.1 = (f32[1,1,1,125,125]{4,2,3,1,0:T(1,128)S(1)}, f32[1,1,1,125,125]{4,2,3,1,0:T(1,128)}, u32[]{:S(2)}) copy-start(f32[1,1,1,125,125]{4,2,3,1,0:T(1,128)} %param.18) | copy-start | bytes 187504
  0.0 10.8 %copy-start.2 = (f32[1,1,1,125,72]{3,4,2,1,0:T(8,128)S(1)}, f32[1,1,1,125,72]{3,4,2,1,0:T(8,128)}, u32[]{:S(2)}) copy-start(f32[1,1,1,125,72]{3,4,2,1,0:T(8,128)} %param.21) | copy-start | bytes 108004
  0.0 10.8 %copy-start.3 = (f32[1,1,1,125,60]{3,2,4,1,0:T(1,128)S(1)}, f32[1,1,1,125,60]{3,2,4,1,0:T(1,128)}, u32[]{:S(2)}) copy-start(f32[1,1,1,125,60]{3,2,4,1,0:T(1,128)} %param.20) | copy-start | bytes 90004
  0.0 10.8 %copy-start.4 = (f32[1,1,1,125,50]{3,2,4,1,0:T(1,128)S(1)}, f32[1,1,1,125,50]{3,2,4,1,0:T(1,128)}, u32[]{:S(2)}) copy-start(f32[1,1,1,125,50]{3,2,4,1,0:T(1,128)} %param.19) | copy-start | bytes 75004
  0.0 10.8 %copy-start.5 = (f32[1,1,25,200]{3,1,2,0:T(1,128)S(1)}, f32[1,1,25,200]{3,1,2,0:T(1,128)}, u32[]{:S(2)}) copy-start(f32[1,1,25,200]{3,1,2,0:T(1,128)} %param.22) | copy-start | bytes 60004
  0.0 10.8 %copy-start.6 = (f32[1,1,1,30,72]{4,2,3,1,0:T(1,128)S(1)}, f32[1,1,1,30,72]{4,2,3,1,0:T(1,128)}, u32[]{:S(2)}) copy-start(f32[1,1,1,30,72]{4,2,3,1,0:T(1,128)} %param.26) | copy-start | bytes 25924
  0.0 10.8 %copy-start.7 = (f32[1,1,1,25,60]{4,2,3,1,0:T(1,128)S(1)}, f32[1,1,1,25,60]{4,2,3,1,0:T(1,128)}, u32[]{:S(2)}) copy-start(f32[1,1,1,25,60]{4,2,3,1,0:T(1,128)} %param.23) | copy-start | bytes 18004
  0.1 10.8 %copy-start.8 = (f32[1,1,1,25,72]{4,2,3,1,0:T(1,128)S(1)}, f32[1,1,1,25,72]{4,2,3,1,0:T(1,128)}, u32[]{:S(2)}) copy-start(f32[1,1,1,25,72]{4,2,3,1,0:T(1,128)} %param.24) | copy-start | bytes 21604
  0.1 10.8 %copy-start.9 = (s32[1,1,1,216]{3,2,1,0:T(1,128)S(1)}, s32[1,1,1,216]{3,2,1,0:T(1,128)}, u32[]{:S(2)}) copy-start(s32[1,1,1,216]{3,2,1,0:T(1,128)} %param.17) | copy-start | bytes 2596
  2.9 67.6 %collective-permute-start.4 = (f32[8,41472]{1,0:T(8,128)S(1)}, f32[8,41472]{1,0:T(8,128)S(1)}, u32[]{:S(2)}, u32[]{:S(2)}) collective-permute-start(f32[8,41472]{1,0:T(8,128)S(1)} %get-tuple-element.41.top), channel_id=1, source_target_pairs={{0,32},{32,64},{64,96},{96,128},{128,160},{160,192},{192,224},{1,3... | collective-permute-start | bytes 3981320 | tf_op jit(solution)/shard_map/ppermute | solution.py:24
  7.4 27.9 %collective-permute-start = (f32[16,128]{1,0:T(8,128)S(1)}, f32[16,128]{1,0:T(8,128)S(1)}, u32[]{:S(2)}, u32[]{:S(2)}) collective-permute-start(f32[16,128]{1,0:T(8,128)S(1)} %get-tuple-element.30), channel_id=1, source_target_pairs={{0,32},{32,64},{64,96},{96,128},{128,160},{160,192},{192,224},{1,3... | collective-permute-start | bytes 24584 | tf_op jit(solution)/shard_map/ppermute | solution.py:24
  35.2 10.0 %collective-permute-start.1 = (f32[40,960]{1,0:T(8,128)S(1)}, f32[40,960]{1,0:T(8,128)S(1)}, u32[]{:S(2)}, u32[]{:S(2)}) collective-permute-start(f32[40,960]{1,0:T(8,128)S(1)} %y_message.1.second), channel_id=1, source_target_pairs={{0,8},{8,16},{16,24},{1,9},{9,17},{17,25},{2,10},{10,18},{18,26},{... | collective-permute-start | bytes 460808 | tf_op jit(solution)/shard_map/ppermute | solution.py:24
  38.5 7.8 %collective-permute-start.3 = (f32[56,256]{1,0:T(8,128)S(1)}, f32[56,256]{1,0:T(8,128)S(1)}, u32[]{:S(2)}, u32[]{:S(2)}) collective-permute-start(f32[56,256]{1,0:T(8,128)S(1)} %get-tuple-element.37), channel_id=1, source_target_pairs={{1,0},{2,1},{3,2},{4,3},{5,4},{6,5},{7,6},{9,8},{10,9},{11,10},{12... | collective-permute-start | bytes 172040 | tf_op jit(solution)/shard_map/ppermute | solution.py:24
  42.2 4.0 %collective-permute-start.2 = (f32[32,256]{1,0:T(8,128)S(1)}, f32[32,256]{1,0:T(8,128)S(1)}, u32[]{:S(2)}, u32[]{:S(2)}) collective-permute-start(f32[32,256]{1,0:T(8,128)S(1)} %get-tuple-element.33.first), channel_id=1, source_target_pairs={{0,1},{1,2},{2,3},{3,4},{4,5},{5,6},{6,7},{8,9},{9,10},{10,11},{11... | collective-permute-start | bytes 98312 | tf_op jit(solution)/shard_map/ppermute | solution.py:24
  135.3 4.4 %collective-permute-start.5 = (f32[8,32]{1,0:T(8,128)S(1)}, f32[8,32]{1,0:T(8,128)S(1)}, u32[]{:S(2)}, u32[]{:S(2)}) collective-permute-start(f32[8,32]{1,0:T(8,128)S(1)} %slice_bitcast_fusion), channel_id=1, source_target_pairs={{32,0},{64,32},{96,64},{128,96},{160,128},{192,160},{224,192},{33,... | collective-permute-start | bytes 3080 | tf_op jit(solution)/shard_map/ppermute | solution.py:24
  139.6 4.4 %collective-permute-start.6 = (f32[7,32]{1,0:T(8,128)S(1)}, f32[7,32]{1,0:T(8,128)S(1)}, u32[]{:S(2)}, u32[]{:S(2)}) collective-permute-start(f32[7,32]{1,0:T(8,128)S(1)} %pad_maximum_fusion), channel_id=1, source_target_pairs={{8,0},{16,8},{24,16},{9,1},{17,9},{25,17},{10,2},{18,10},{26,18},{... | collective-permute-start | bytes 2696 | tf_op jit(solution)/shard_map/ppermute | solution.py:24

commit v9 on v8

--- a/solution.py
+++ b/solution.py
@@ -290,8 +290,7 @@
 
 def prepare_body(sizes, side, *refs):
     order, leaf, to_first, first, second = refs[:5]
-    to_second, to_top, first_second, first_top, second_top = refs[5:10]
-    up, down, beside, pack = refs[10:]
+    up, down, beside, pack = refs[5:]
     up[...] = jnp.zeros_like(up)
     down[...] = jnp.zeros_like(down)
     beside[sizes[2] :, :] = jnp.zeros_like(beside[sizes[2] :, :])
@@ -310,9 +309,12 @@
     beside[second_size : second_size + 1, 0 : order.shape[1]] = order
     pack[ORDER : ORDER + 1, 0:leaf_size] = order[:, :leaf_size]
     pack[ORDER + 1 : ORDER + 2, 0 : order.shape[1] - leaf_size] = order[:, leaf_size:]
+    for start, rows in ((LEAF, leaf_rows), (TO_FIRST, first_columns)):
+        pack[start : start + rows.shape[0], 0 : rows.shape[1]] = rows
+
+
+def pack_later(pack, to_second, to_top, first_second, first_top, second_top):
     for start, rows in (
-        (LEAF, leaf_rows),
-        (TO_FIRST, first_columns),
         (TO_SECOND, to_second[:, 0, :]),
         (TO_TOP, to_top[...]),
         (FIRST_SECOND, first_second[:, 0, :]),
@@ -366,7 +368,11 @@
     )(inner, from_x, beside)
 
 
-def own_body(sizes, side, total, inner, from_x, from_y, pack, first, cells_out, terms, other):
+def own_body(
+    sizes, side, total, inner, from_x, from_y, pack, first, *refs
+):
+    later, (cells_out, terms, other, pack_out) = refs[:5], refs[5:]
+    pack_later(pack_out, *later)
     leaf_size, first_size = sizes[:2]
     leaf_order, first_order = packed_order(pack, sizes)[:2]
     values = inner[...]
@@ -693,13 +699,14 @@
     )(inner, after_x, after_y)
 
 
-def call(body, outs, *operands):
+def call(body, outs, *operands, aliases={}):
     shapes = tuple(jax.ShapeDtypeStruct(o, jnp.float32) for o in outs)
     return pl.pallas_call(
         body,
         out_shape=shapes,
         in_specs=[VMEM] * len(operands),
         out_specs=(VMEM,) * len(shapes),
+        input_output_aliases=aliases,
         compiler_params=LIMIT,
     )(*operands)
 
@@ -761,27 +768,28 @@
         to_first,
         first,
         second,
+    )
+    first_below = shifted(up, "gz", 1)
+    first_above = shifted(down, "gz", -1)
+    top_below = shifted(folds, "gx", 1)
+    beside = with_layer(inner, from_x, beside)
+    second_below = shifted(beside, "gy", 1)
+
+    total = first.shape[2]
+    turned, own_terms, other, pack = call(
+        functools.partial(own_body, sizes, side, total),
+        [(lanes, lanes_of(side)), (count, total), (count, first_size), pack.shape],
+        inner,
+        from_x,
+        second_below,
+        pack,
+        up,
         to_second,
         to_top,
         first_to_second,
         first_to_top,
         second_to_top,
-    )
-    first_below = shifted(up, "gz", 1)
-    first_above = shifted(down, "gz", -1)
-    top_below = shifted(folds, "gx", 1)
-    beside = with_layer(inner, from_x, beside)
-    second_below = shifted(beside, "gy", 1)
-
-    total = first.shape[2]
-    turned, own_terms, other = call(
-        functools.partial(own_body, sizes, side, total),
-        [(lanes, lanes_of(side)), (count, total), (count, first_size)],
-        inner,
-        from_x,
-        second_below,
-        pack,
-        up,
+        aliases={3: 3},
     )
     (pieces,) = call(
         functools.partial(first_body, sizes, side, total),

time: 147 us -> 147 us (level)
  no operation moved by 1% of the time
where the time goes in v9:
time: 147 us; the launch traced here: 145 us
  blocking collectives  83.1 us (57%)
  waiting for transfers between devices  30.1 us (20%)
  starting transfers between devices  20.4 us (14%)
  Pallas kernels  11.2 us (8%)
    all_to_all x7, blocking collectives, exchanged(): return lax.all_to_all(pieces, axis, split_axis=0, concat_axis=0, tiled=True)  83.1 us
    ppermute x7, waiting for transfers between devices, shifted(): return lax.ppermute(shard, axis, pairs)  30.1 us
    ppermute x7, starting transfers between devices, shifted(): return lax.ppermute(shard, axis, pairs)  20.4 us
    pallas_call x9, Pallas kernels, call(): pl.pallas_call(body, out_shape=shapes, in_specs=[VMEM] * len(operands), o...  6.45 us
  transfers between devices with their start and end apart: 7, of which 4 were waited for; matrix products, arithmetic and copies ran while one was open for 0% of the time, Pallas kernels for 2%

profile of v9, /device:TPU:1, one launch (start us, length us, event | category | flops | bytes accessed | tf_op | source)
XLA Modules:
  0.0 145.4 jit_solution(11488786259701179926)
XLA Ops:
  0.0 0.0 copy-start
  0.0 0.0 copy-start.1
  0.0 0.0 copy-start.4
  0.0 0.0 copy-start.5
  0.0 0.0 copy-start.9
  0.0 0.0 copy-start.2
  0.0 0.0 copy-start.3
  0.0 0.0 copy-start.6
  0.1 0.0 copy-start.7
  0.1 0.0 copy-start.8
  0.1 2.8 %restrict_twice.1 = (f32[7,8,32]{2,1,0:T(8,128)S(1)}, f32[16,128]{1,0:T(8,128)S(1)}, f32[8,41472]{1,0:T(8,128)S(1)}) custom-call(s32[1,216]{1,0:T(1,128)} %bitcast.31, f32[4,24,24,24]{3,2,1,0:T(8,128)} %rhs_in.1, f32[4,24,24,24]{3,2,1,0:T(8,128)} %iterate_in.1, f32[24,24,24]{2,1,0:T(8,128)} %coefficient_in.1, f32[36,9216]{1,0:T(8,128)} %top_in.1), custom_call_target="tpu_custom_call" | custom-call | tf_op jit(solution)/shard_map/restrict_twice/pallas_call | solution.py:195
  2.9 4.4 %collective-permute-start.4 = (f32[8,41472]{1,0:T(8,128)S(1)}, f32[8,41472]{1,0:T(8,128)S(1)}, u32[]{:S(2)}, u32[]{:S(2)}) collective-permute-start(f32[8,41472]{1,0:T(8,128)S(1)} %get-tuple-element.43.top), channel_id=1, source_target_pairs={{0,32},{32,64},{64,96},{96,128},{128,160},{160,192},{192,224},{1,3... | collective-permute-start | bytes 3981320 | tf_op jit(solution)/shard_map/ppermute | solution.py:24
  7.4 3.5 %collective-permute-start = (f32[16,128]{1,0:T(8,128)S(1)}, f32[16,128]{1,0:T(8,128)S(1)}, u32[]{:S(2)}, u32[]{:S(2)}) collective-permute-start(f32[16,128]{1,0:T(8,128)S(1)} %get-tuple-element.31), channel_id=1, source_target_pairs={{0,32},{32,64},{64,96},{96,128},{128,160},{160,192},{192,224},{1,3... | collective-permute-start | bytes 24584 | tf_op jit(solution)/shard_map/ppermute | solution.py:24
  10.8 0.0 copy-done
  10.8 0.0 copy-done.1
  10.8 0.0 copy-done.4
  10.9 0.0 copy-done.5
  10.9 0.0 copy-done.9
  10.9 0.5 prepare.1
  11.4 23.8 %collective-permute-done.from_x = f32[16,128]{1,0:T(8,128)S(1)} collective-permute-done((f32[16,128]{1,0:T(8,128)S(1)}, f32[16,128]{1,0:T(8,128)S(1)}, u32[]{:S(2)}, u32[]{:S(2)}) %collective-permute-start) | collective-permute-done | bytes 8224 | tf_op jit(solution)/shard_map/ppermute | solution.py:24
  35.2 3.2 %collective-permute-start.1 = (f32[40,960]{1,0:T(8,128)S(1)}, f32[40,960]{1,0:T(8,128)S(1)}, u32[]{:S(2)}, u32[]{:S(2)}) collective-permute-start(f32[40,960]{1,0:T(8,128)S(1)} %y_message.1.second), channel_id=1, source_target_pairs={{0,8},{8,16},{16,24},{1,9},{9,17},{17,25},{2,10},{10,18},{18,26},{... | collective-permute-start | bytes 460808 | tf_op jit(solution)/shard_map/ppermute | solution.py:24
  38.5 3.7 %collective-permute-start.3 = (f32[56,256]{1,0:T(8,128)S(1)}, f32[56,256]{1,0:T(8,128)S(1)}, u32[]{:S(2)}, u32[]{:S(2)}) collective-permute-start(f32[56,256]{1,0:T(8,128)S(1)} %get-tuple-element.38), channel_id=1, source_target_pairs={{1,0},{2,1},{3,2},{4,3},{5,4},{6,5},{7,6},{9,8},{10,9},{11,10},{12... | collective-permute-start | bytes 172040 | tf_op jit(solution)/shard_map/ppermute | solution.py:24
  42.2 3.0 %collective-permute-start.2 = (f32[32,256]{1,0:T(8,128)S(1)}, f32[32,256]{1,0:T(8,128)S(1)}, u32[]{:S(2)}, u32[]{:S(2)}) collective-permute-start(f32[32,256]{1,0:T(8,128)S(1)} %get-tuple-element.34.first), channel_id=1, source_target_pairs={{0,1},{1,2},{2,3},{3,4},{4,5},{5,6},{6,7},{8,9},{9,10},{10,11},{11... | collective-permute-start | bytes 98312 | tf_op jit(solution)/shard_map/ppermute | solution.py:24
  45.2 0.0 collective-permute-done.1.from_y.below
  45.2 0.0 copy-done.2
  45.2 0.0 copy-done.3
  45.2 0.0 copy-done.6
  45.2 0.0 copy-done.7
  45.3 0.0 copy-done.8
  45.3 0.7 shard_map.136
  46.0 0.2 collective-permute-done.2.below
  46.2 0.0 collective-permute-done.3.above
  46.2 0.5 shard_map.137
  46.7 10.0 %all_to_all.35.received = f32[8,4,256]{2,1,0:T(4,128)S(1)} all-to-all(f32[8,4,256]{2,1,0:T(4,128)S(1)} %shard_map.137), channel_id=1, replica_groups=mesh['gx'=8,'gy'=4,'gz'=8] {'gz'}, dimensions={0} | all-to-all | bytes 65536 | tf_op jit(solution)/shard_map/all_to_all | solution.py:28
  56.7 1.0 shard_map.138
  57.7 12.8 %all_to_all.36.received = f32[32,4,128]{2,1,0:T(4,128)S(1)} all-to-all(f32[32,4,128]{2,1,0:T(4,128)S(1)} %get-tuple-element.40), channel_id=1, replica_groups=mesh['gx'=8,'gy'=4,'gz'=8] {'gy','gz'}, dimensions={0} | all-to-all | bytes 131072 | tf_op jit(solution)/shard_map/all_to_all | solution.py:28
  70.5 0.0 collective-permute-done.4.below
  70.5 1.0 shard_map.139
  71.5 11.8 %all_to_all.37.received = f32[32,4,384]{2,1,0:T(4,128)S(1)} all-to-all(f32[32,4,384]{2,1,0:T(4,128)S(1)} %get-tuple-element.44), channel_id=1, replica_groups=mesh['gx'=8,'gy'=4,'gz'=8] {'gy','gz'}, dimensions={0} | all-to-all | bytes 393216 | tf_op jit(solution)/shard_map/all_to_all | solution.py:28
  83.3 16.9 %all_to_all.38.received = f32[8,4,384]{2,1,0:T(4,128)S(1)} all-to-all(f32[8,4,384]{2,1,0:T(4,128)S(1)} %shard_map.140), channel_id=1, replica_groups=mesh['gx'=8,'gy'=4,'gz'=8] {'gx'}, dimensions={0} | all-to-all | bytes 98304 | tf_op jit(solution)/shard_map/all_to_all | solution.py:28
  100.2 13.3 %all_to_all.39.whole = f32[32,4,384]{2,1,0:T(4,128)S(1)} all-to-all(f32[32,4,384]{2,1,0:T(4,128)S(1)} %shard_map.141), channel_id=1, replica_groups=mesh['gx'=8,'gy'=4,'gz'=8] {'gy','gz'}, dimensions={0} | all-to-all | bytes 393216 | tf_op jit(solution)/shard_map/all_to_all | solution.py:28
  113.5 1.5 %shard_map.142 = (f32[4,36]{1,0:T(4,128)S(1)}, f32[4,30]{1,0:T(4,128)S(1)}, f32[4,25]{1,0:T(4,128)S(1)}, f32[4,125]{1,0:T(4,128)S(1)}) custom-call(f32[32,4,384]{2,1,0:T(4,128)S(1)} %all_to_all.39.whole, f32[8,41472]{1,0:T(8,128)S(1)} %get-tuple-element.43.top, f32[8,41472]{1,0:T(8,128)S(1)} %collective-permute-done.4.below, ...), custom_call_target="tpu_custom_call" | custom-call | tf_op jit(solution)/shard_map/pallas_call | solution.py:704
  115.0 10.9 %all_to_all.40 = f32[32,4,30]{2,1,0:T(4,128)S(1)} all-to-all(f32[32,4,30]{2,1,0:T(4,128)S(1)} %broadcast_in_dim.6), channel_id=1, replica_groups=mesh['gx'=8,'gy'=4,'gz'=8] {'gy','gz'}, dimensions={0} | all-to-all | bytes 30720 | tf_op jit(solution)/shard_map/all_to_all | solution.py:28
  126.0 0.1 reshape.15.whole
  126.1 0.8 shard_map.143
  126.9 7.4 %all_to_all.41.received = f32[8,4,128]{2,1,0:T(4,128)S(1)} all-to-all(f32[8,4,128]{2,1,0:T(4,128)S(1)} %broadcast_in_dim.7), channel_id=1, replica_groups=mesh['gx'=8,'gy'=4,'gz'=8] {'gz'}, dimensions={0} | all-to-all | bytes 32768 | tf_op jit(solution)/shard_map/all_to_all | solution.py:28
  134.3 0.9 shard_map.144.inner
  135.3 1.3 collective-permute-start.5
  136.6 3.0 %collective-permute-done.5.after_x = f32[8,32]{1,0:T(8,128)S(1)} collective-permute-done((f32[8,32]{1,0:T(8,128)S(1)}, f32[8,32]{1,0:T(8,128)S(1)}, u32[]{:S(2)}, u32[]{:S(2)}) %collective-permute-start.5) | collective-permute-done | bytes 1056 | tf_op jit(solution)/shard_map/ppermute | solution.py:24
  139.6 1.3 collective-permute-start.6
  140.9 3.1 %collective-permute-done.6.after_y = f32[7,32]{1,0:T(8,128)S(1)} collective-permute-done((f32[7,32]{1,0:T(8,128)S(1)}, f32[7,32]{1,0:T(8,128)S(1)}, u32[]{:S(2)}, u32[]{:S(2)}) %collective-permute-start.6) | collective-permute-done | bytes 928 | tf_op jit(solution)/shard_map/ppermute | solution.py:24
  144.0 1.4 prolong_twice.1
  (11 shorter events, 0.1 us)
Async XLA Ops:
  0.0 10.8 %copy-start = (f32[1,30,960]{2,0,1:T(1,128)S(1)}, f32[1,30,960]{2,0,1:T(1,128)}, u32[]{:S(2)}) copy-start(f32[1,30,960]{2,0,1:T(1,128)} %param.25) | copy-start | bytes 345604
  0.0 10.8 %copy-start.1 = (f32[1,1,1,125,125]{4,2,3,1,0:T(1,128)S(1)}, f32[1,1,1,125,125]{4,2,3,1,0:T(1,128)}, u32[]{:S(2)}) copy-start(f32[1,1,1,125,125]{4,2,3,1,0:T(1,128)} %param.18) | copy-start | bytes 187504
  0.0 10.8 %copy-start.4 = (f32[1,1,1,125,50]{3,2,4,1,0:T(1,128)S(1)}, f32[1,1,1,125,50]{3,2,4,1,0:T(1,128)}, u32[]{:S(2)}) copy-start(f32[1,1,1,125,50]{3,2,4,1,0:T(1,128)} %param.19) | copy-start | bytes 75004
  0.0 10.8 %copy-start.5 = (f32[1,1,25,200]{3,1,2,0:T(1,128)S(1)}, f32[1,1,25,200]{3,1,2,0:T(1,128)}, u32[]{:S(2)}) copy-start(f32[1,1,25,200]{3,1,2,0:T(1,128)} %param.22) | copy-start | bytes 60004
  0.0 10.8 %copy-start.9 = (s32[1,1,1,216]{3,2,1,0:T(1,128)S(1)}, s32[1,1,1,216]{3,2,1,0:T(1,128)}, u32[]{:S(2)}) copy-start(s32[1,1,1,216]{3,2,1,0:T(1,128)} %param.17) | copy-start | bytes 2596
  0.0 45.2 %copy-start.2 = (f32[1,1,1,125,72]{3,4,2,1,0:T(8,128)S(1)}, f32[1,1,1,125,72]{3,4,2,1,0:T(8,128)}, u32[]{:S(2)}) copy-start(f32[1,1,1,125,72]{3,4,2,1,0:T(8,128)} %param.21) | copy-start | bytes 108004
  0.0 45.2 %copy-start.3 = (f32[1,1,1,125,60]{3,2,4,1,0:T(1,128)S(1)}, f32[1,1,1,125,60]{3,2,4,1,0:T(1,128)}, u32[]{:S(2)}) copy-start(f32[1,1,1,125,60]{3,2,4,1,0:T(1,128)} %param.20) | copy-start | bytes 90004
  0.0 45.2 %copy-start.6 = (f32[1,1,1,30,72]{4,2,3,1,0:T(1,128)S(1)}, f32[1,1,1,30,72]{4,2,3,1,0:T(1,128)}, u32[]{:S(2)}) copy-start(f32[1,1,1,30,72]{4,2,3,1,0:T(1,128)} %param.26) | copy-start | bytes 25924
  0.1 45.2 %copy-start.7 = (f32[1,1,1,25,60]{4,2,3,1,0:T(1,128)S(1)}, f32[1,1,1,25,60]{4,2,3,1,0:T(1,128)}, u32[]{:S(2)}) copy-start(f32[1,1,1,25,60]{4,2,3,1,0:T(1,128)} %param.23) | copy-start | bytes 18004
  0.1 45.2 %copy-start.8 = (f32[1,1,1,25,72]{4,2,3,1,0:T(1,128)S(1)}, f32[1,1,1,25,72]{4,2,3,1,0:T(1,128)}, u32[]{:S(2)}) copy-start(f32[1,1,1,25,72]{4,2,3,1,0:T(1,128)} %param.24) | copy-start | bytes 21604
  2.9 67.6 %collective-permute-start.4 = (f32[8,41472]{1,0:T(8,128)S(1)}, f32[8,41472]{1,0:T(8,128)S(1)}, u32[]{:S(2)}, u32[]{:S(2)}) collective-permute-start(f32[8,41472]{1,0:T(8,128)S(1)} %get-tuple-element.43.top), channel_id=1, source_target_pairs={{0,32},{32,64},{64,96},{96,128},{128,160},{160,192},{192,224},{1,3... | collective-permute-start | bytes 3981320 | tf_op jit(solution)/shard_map/ppermute | solution.py:24
  7.4 27.9 %collective-permute-start = (f32[16,128]{1,0:T(8,128)S(1)}, f32[16,128]{1,0:T(8,128)S(1)}, u32[]{:S(2)}, u32[]{:S(2)}) collective-permute-start(f32[16,128]{1,0:T(8,128)S(1)} %get-tuple-element.31), channel_id=1, source_target_pairs={{0,32},{32,64},{64,96},{96,128},{128,160},{160,192},{192,224},{1,3... | collective-permute-start | bytes 24584 | tf_op jit(solution)/shard_map/ppermute | solution.py:24
  35.2 10.0 %collective-permute-start.1 = (f32[40,960]{1,0:T(8,128)S(1)}, f32[40,960]{1,0:T(8,128)S(1)}, u32[]{:S(2)}, u32[]{:S(2)}) collective-permute-start(f32[40,960]{1,0:T(8,128)S(1)} %y_message.1.second), channel_id=1, source_target_pairs={{0,8},{8,16},{16,24},{1,9},{9,17},{17,25},{2,10},{10,18},{18,26},{... | collective-permute-start | bytes 460808 | tf_op jit(solution)/shard_map/ppermute | solution.py:24
  38.5 7.8 %collective-permute-start.3 = (f32[56,256]{1,0:T(8,128)S(1)}, f32[56,256]{1,0:T(8,128)S(1)}, u32[]{:S(2)}, u32[]{:S(2)}) collective-permute-start(f32[56,256]{1,0:T(8,128)S(1)} %get-tuple-element.38), channel_id=1, source_target_pairs={{1,0},{2,1},{3,2},{4,3},{5,4},{6,5},{7,6},{9,8},{10,9},{11,10},{12... | collective-permute-start | bytes 172040 | tf_op jit(solution)/shard_map/ppermute | solution.py:24
  42.2 4.0 %collective-permute-start.2 = (f32[32,256]{1,0:T(8,128)S(1)}, f32[32,256]{1,0:T(8,128)S(1)}, u32[]{:S(2)}, u32[]{:S(2)}) collective-permute-start(f32[32,256]{1,0:T(8,128)S(1)} %get-tuple-element.34.first), channel_id=1, source_target_pairs={{0,1},{1,2},{2,3},{3,4},{4,5},{5,6},{6,7},{8,9},{9,10},{10,11},{11... | collective-permute-start | bytes 98312 | tf_op jit(solution)/shard_map/ppermute | solution.py:24
  135.3 4.4 %collective-permute-start.5 = (f32[8,32]{1,0:T(8,128)S(1)}, f32[8,32]{1,0:T(8,128)S(1)}, u32[]{:S(2)}, u32[]{:S(2)}) collective-permute-start(f32[8,32]{1,0:T(8,128)S(1)} %slice_bitcast_fusion), channel_id=1, source_target_pairs={{32,0},{64,32},{96,64},{128,96},{160,128},{192,160},{224,192},{33,... | collective-permute-start | bytes 3080 | tf_op jit(solution)/shard_map/ppermute | solution.py:24
  139.6 4.4 %collective-permute-start.6 = (f32[7,32]{1,0:T(8,128)S(1)}, f32[7,32]{1,0:T(8,128)S(1)}, u32[]{:S(2)}, u32[]{:S(2)}) collective-permute-start(f32[7,32]{1,0:T(8,128)S(1)} %pad_maximum_fusion), channel_id=1, source_target_pairs={{8,0},{16,8},{24,16},{9,1},{17,9},{25,17},{10,2},{18,10},{26,18},{... | collective-permute-start | bytes 2696 | tf_op jit(solution)/shard_map/ppermute | solution.py:24
